TPU v7x, 512 devices: a whole 4x8x8 slice. The times are simulated.
512 devices in a mesh: gx: 4 (over x), gy: 8 (over y), gz: 16 (over z, core).
Axes of the slice: x: 4, y: 8, z: 8, core: 2. Of those that a mesh axis runs over, the one named last changes fastest.
Arguments:
- opening_warmth_field: float32 [32, 128, 2048], P('gx', 'gy', 'gz'), may hold values from -42 to 42
- cellwise_warming_source: float32 [32, 128, 2048], P('gx', 'gy', 'gz'), may hold values from -6 to 6
- substance_category_per_voxel: int32 [32, 128, 2048], P('gx', 'gy', 'gz'), may hold values from 0 to 15
- thermal_coefficient_table: float32 [16], replicated, may hold values from 0.2 to 5
- boundary_cooling_flags: int32 [32, 128, 2048], P('gx', 'gy', 'gz'), may hold values 0 or 1
Outputs:
- closing_warmth_field: float32 [32, 128, 2048], P('gx', 'gy', 'gz')
- remaining_mismatch: float32 [32, 128, 2048], P('gx', 'gy', 'gz')
All inputs are finite; a program needn't handle non-finite values. No bound on the sum of `boundary_cooling_flags` on one device may be relied on, other than what follows from the above.
Results may differ from a plain program's by a relative error of at most 0.00055.
Values sent between devices are 32-bit elements; how exact they have to be, the bound alone decides.
No kernel may reach another device: no remote copies, remote signals or barrier semaphores. Data moves between devices by JAX's collectives and lax.ppermute only.
A program may use at most 64 MiB of HBM per device.

v0:
```python
import jax
import jax.numpy as jnp
from jax import lax
from jax.sharding import Mesh
from jax.sharding import PartitionSpec as P

ITERS = 4
GZ = ("gz_0", "gz_1")


interval_delta = 2.0
cooling = 3.0
kind_weights = (1.0, 0.5, 0.25)
kind_counts = (6.0, 12.0, 8.0)


def padded_2(cells, sides, width):
    for axis, dim in sides:
        count = lax.axis_size(axis)
        ends = count - 1
        head = lax.slice_in_dim(cells, 0, width, axis=dim)
        tail = lax.slice_in_dim(cells, cells.shape[dim] - width, cells.shape[dim], axis=dim)
        cells = jnp.concatenate(
            [
                lax.ppermute(tail, axis, [(i, (i + 1) % count) for i in range(ends)]),
                cells,
                lax.ppermute(head, axis, [((i + 1) % count, i) for i in range(ends)]),
            ],
            axis=dim,
        )
    return cells


def from_everyone(array, axis):
    copies = jnp.broadcast_to(array, (lax.axis_size(axis), *array.shape))
    return lax.all_to_all(copies, axis, split_axis=0, concat_axis=0, tiled=True)


def over_copies(array, axis):
    return from_everyone(array, axis).sum(axis=0)


def one_axis_at_a_time(array, axes):
    far, near = axes
    return over_copies(over_copies(array, near), far)


def together(arrays, axis):
    ends = [0]
    for a in arrays:
        ends.append(ends[-1] + a.size)
    so_far = one_axis_at_a_time(jnp.concatenate([a.ravel() for a in arrays]), axis)
    return tuple((so_far[b:e].reshape(a.shape) for a, b, e in zip(arrays, ends, ends[1:])))


def split_axis(values, axis):
    length = values.shape[axis] - 2
    center = lax.slice_in_dim(values, 1, length + 1, axis=axis)
    beside = lax.slice_in_dim(values, 0, length, axis=axis) + lax.slice_in_dim(
        values, 2, length + 2, axis=axis
    )
    return (center, beside)


def neighbor_sums(padded):
    leading_extent = padded.ndim - 3
    pieces = [(padded, 0)]
    for shift_vector in range(3):
        next_pieces = []
        for values, neighbors in pieces:
            center, beside = split_axis(values, leading_extent + shift_vector)
            next_pieces.append((center, neighbors))
            next_pieces.append((beside, neighbors + 1))
        pieces = next_pieces
    totals = [None, None, None]
    for values, neighbors in pieces:
        if neighbors > 0:
            if totals[neighbors - 1] is None:
                totals[neighbors - 1] = values
            else:
                totals[neighbors - 1] = totals[neighbors - 1] + values
    return totals


def coupling(padded, padded_flux, cond):
    field_sums = neighbor_sums(padded)
    accumulated_flux = neighbor_sums(padded_flux)
    computed_output = kind_weights[0] * (cond * field_sums[0] + accumulated_flux[0])
    computed_output = computed_output + kind_weights[1] * (
        cond * field_sums[1] + accumulated_flux[1]
    )
    computed_output = computed_output + kind_weights[2] * (
        cond * field_sums[2] + accumulated_flux[2]
    )
    return computed_output


def body(
    opening_warmth_field,
    cellwise_warming_source,
    substance_category_per_voxel,
    thermal_coefficient_table,
    boundary_cooling_flags,
):
    classes = thermal_coefficient_table.shape[0]
    picks = (
        substance_category_per_voxel[None]
        == jnp.arange(classes, dtype=jnp.int32)[:, None, None, None]
    )
    cond = jnp.sum(jnp.where(picks, thermal_coefficient_table[:, None, None, None], 0.0), axis=0)
    padded_cond = padded_2(cond, (("gx", 0), ("gy", 1), (GZ, 2)), 1)
    cond_sums = neighbor_sums(padded_cond)
    spread = kind_weights[0] * (kind_counts[0] * cond + cond_sums[0])
    spread = spread + kind_weights[1] * (kind_counts[1] * cond + cond_sums[1])
    spread = spread + kind_weights[2] * (kind_counts[2] * cond + cond_sums[2])
    diagonal = (
        1.0
        + interval_delta * cooling * boundary_cooling_flags.astype(jnp.float32)
        + 0.5 * interval_delta * spread
    )

    def apply_stencil_matrix(field):
        padded = padded_2(field, (("gx", 0), ("gy", 1), (GZ, 2)), 1)
        padded_flux = padded_cond * padded
        return diagonal * field - 0.5 * interval_delta * coupling(padded, padded_flux, cond)

    def two_products(remaining_mismatch, image):
        return together(
            (jnp.sum(remaining_mismatch * remaining_mismatch), jnp.sum(remaining_mismatch * image)),
            (("gx", "gy"), ("gz_0", "gz_1")),
        )

    closing_warmth_field = opening_warmth_field
    remaining_mismatch = opening_warmth_field
    forcing_term = closing_warmth_field + interval_delta * cellwise_warming_source
    remaining_mismatch = forcing_term - apply_stencil_matrix(closing_warmth_field)
    image = apply_stencil_matrix(remaining_mismatch)
    norm_now, product = two_products(remaining_mismatch, image)
    descent_alpha = norm_now / product
    search_heading = remaining_mismatch
    along = image
    for step in range(ITERS):
        closing_warmth_field = closing_warmth_field + descent_alpha * search_heading
        remaining_mismatch = remaining_mismatch - descent_alpha * along
        if step + 1 < ITERS:
            image = apply_stencil_matrix(remaining_mismatch)
            following_norm, product = two_products(remaining_mismatch, image)
            ratio = following_norm / norm_now
            descent_alpha = following_norm / (product - ratio * following_norm / descent_alpha)
            search_heading = remaining_mismatch + ratio * search_heading
            along = image + ratio * along
            norm_now = following_norm
    return (closing_warmth_field, remaining_mismatch)


def solution(mesh):
    split = Mesh(
        mesh.devices.reshape(mesh.shape["gx"], mesh.shape["gy"], 8, 2), ("gx", "gy", "gz_0", "gz_1")
    )
    in_specs = (P("gx", "gy", GZ), P("gx", "gy", GZ), P("gx", "gy", GZ), P(), P("gx", "gy", GZ))
    out_specs = (P("gx", "gy", GZ), P("gx", "gy", GZ))
    return jax.shard_map(body, mesh=split, in_specs=in_specs, out_specs=out_specs, check_vma=False)
```

profile of v0, /device:TPU:1, one launch (start us, length us, event | category | flops | bytes accessed | tf_op | source)
XLA Modules:
  0.0 288.3 jit_solution(13231290129625093462)
XLA Ops:
  0.6 1.1 select_reduce_fusion
  1.7 3.9 %collective-permute-start = (f32[1,16,128]{2,1,0:T(8,128)S(1)}, f32[1,16,128]{2,1,0:T(8,128)S(1)}, u32[]{:S(2)}, u32[]{:S(2)}) collective-permute-start(f32[1,16,128]{2,1,0:T(8,128)S(1)} %get-tuple-element.63), channel_id=1, source_target_pairs={{0,128},{128,256},{256,384},{1,129},{129,257},{257,385},{2,130},{1... | collective-permute-start | bytes 24584 | tf_op jit(solution)/shard_map/ppermute | solution.py:25
  5.7 1.3 collective-permute-start.1
  7.0 1.3 collective-permute-start.7
  8.3 4.6 %collective-permute-start.6 = (f32[1,16,128]{2,1,0:T(8,128)S(1)}, f32[1,16,128]{2,1,0:T(8,128)S(1)}, u32[]{:S(2)}, u32[]{:S(2)}) collective-permute-start(f32[1,16,128]{2,1,0:T(8,128)S(1)} %get-tuple-element.66), channel_id=1, source_target_pairs={{0,128},{128,256},{256,384},{1,129},{129,257},{257,385},{2,130},{1... | collective-permute-start | bytes 24584 | tf_op jit(solution)/shard_map/ppermute | solution.py:25
  12.9 3.2 %collective-permute-start.2 = (f32[10,1,128]{2,1,0:T(1,128)S(1)}, f32[10,1,128]{2,1,0:T(1,128)S(1)}, u32[]{:S(2)}, u32[]{:S(2)}) collective-permute-start(f32[10,1,128]{2,1,0:T(1,128)S(1)} %get-tuple-element.49), channel_id=1, source_target_pairs={{0,16},{16,32},{32,48},{48,64},{64,80},{80,96},{96,112},{1,17},{17... | collective-permute-start | bytes 15368 | tf_op jit(solution)/shard_map/ppermute | solution.py:25
  16.1 1.3 collective-permute-start.3
  17.5 4.0 %collective-permute-start.8 = (f32[10,1,128]{2,1,0:T(1,128)S(1)}, f32[10,1,128]{2,1,0:T(1,128)S(1)}, u32[]{:S(2)}, u32[]{:S(2)}) collective-permute-start(f32[10,1,128]{2,1,0:T(1,128)S(1)} %get-tuple-element.51), channel_id=1, source_target_pairs={{0,16},{16,32},{32,48},{48,64},{64,80},{80,96},{96,112},{1,17},{17... | collective-permute-start | bytes 15368 | tf_op jit(solution)/shard_map/ppermute | solution.py:25
  21.5 1.3 collective-permute-start.9
  23.0 2.9 %collective-permute-done.9 = f32[10,1,128]{2,1,0:T(1,128)S(1)} collective-permute-done((f32[10,1,128]{2,1,0:T(1,128)S(1)}, f32[10,1,128]{2,1,0:T(1,128)S(1)}, u32[]{:S(2)}, u32[]{:S(2)}) %collective-permute-start.9) | collective-permute-done | bytes 5152 | tf_op jit(solution)/shard_map/ppermute | solution.py:27
  26.0 7.4 %collective-permute-start.10 = (f32[10,18,1]{2,1,0:T(8,128)S(1)}, f32[10,18,1]{2,1,0:T(8,128)S(1)}, u32[]{:S(2)}, u32[]{:S(2)}) collective-permute-start(f32[10,18,1]{2,1,0:T(8,128)S(1)} %get-tuple-element.39), channel_id=1, source_target_pairs={{0,1},{1,2},{2,3},{3,4},{4,5},{5,6},{6,7},{7,8},{8,9},{9,10},{10,1... | collective-permute-start | bytes 2168 | tf_op jit(solution)/shard_map/ppermute | solution.py:25
  33.4 1.9 collective-permute-start.11
  35.3 3.6 %collective-permute-start.4 = (f32[10,18,1]{2,1,0:T(8,128)S(1)}, f32[10,18,1]{2,1,0:T(8,128)S(1)}, u32[]{:S(2)}, u32[]{:S(2)}) collective-permute-start(f32[10,18,1]{2,1,0:T(8,128)S(1)} %get-tuple-element.37), channel_id=1, source_target_pairs={{0,1},{1,2},{2,3},{3,4},{4,5},{5,6},{6,7},{7,8},{8,9},{9,10},{10,1... | collective-permute-start | bytes 2168 | tf_op jit(solution)/shard_map/ppermute | solution.py:25
  39.0 1.9 collective-permute-start.5
  40.9 4.2 %collective-permute-done.5 = f32[10,18,1]{2,1,0:T(8,128)S(1)} collective-permute-done((f32[10,18,1]{2,1,0:T(8,128)S(1)}, f32[10,18,1]{2,1,0:T(8,128)S(1)}, u32[]{:S(2)}, u32[]{:S(2)}) %collective-permute-start.5) | collective-permute-done | bytes 752 | tf_op jit(solution)/shard_map/ppermute | solution.py:27
  47.1 3.6 %collective-permute-start.12 = (f32[1,16,128]{2,1,0:T(8,128)S(1)}, f32[1,16,128]{2,1,0:T(8,128)S(1)}, u32[]{:S(2)}, u32[]{:S(2)}) collective-permute-start(f32[1,16,128]{2,1,0:T(8,128)S(1)} %get-tuple-element.61), channel_id=1, source_target_pairs={{0,128},{128,256},{256,384},{1,129},{129,257},{257,385},{2,130},{1... | collective-permute-start | bytes 24584 | tf_op jit(solution)/shard_map/ppermute | solution.py:25
  50.8 1.3 collective-permute-start.13
  52.1 3.1 %collective-permute-done.13 = f32[1,16,128]{2,1,0:T(8,128)S(1)} collective-permute-done((f32[1,16,128]{2,1,0:T(8,128)S(1)}, f32[1,16,128]{2,1,0:T(8,128)S(1)}, u32[]{:S(2)}, u32[]{:S(2)}) %collective-permute-start.13) | collective-permute-done | bytes 8224 | tf_op jit(solution)/shard_map/ppermute | solution.py:27
  55.2 3.5 %collective-permute-start.14 = (f32[10,1,128]{2,1,0:T(1,128)S(1)}, f32[10,1,128]{2,1,0:T(1,128)S(1)}, u32[]{:S(2)}, u32[]{:S(2)}) collective-permute-start(f32[10,1,128]{2,1,0:T(1,128)S(1)} %get-tuple-element.47), channel_id=1, source_target_pairs={{0,16},{16,32},{32,48},{48,64},{64,80},{80,96},{96,112},{1,17},{17... | collective-permute-start | bytes 15368 | tf_op jit(solution)/shard_map/ppermute | solution.py:25
  58.8 1.3 collective-permute-start.15
  60.1 4.5 %collective-permute-done.15 = f32[10,1,128]{2,1,0:T(1,128)S(1)} collective-permute-done((f32[10,1,128]{2,1,0:T(1,128)S(1)}, f32[10,1,128]{2,1,0:T(1,128)S(1)}, u32[]{:S(2)}, u32[]{:S(2)}) %collective-permute-start.15) | collective-permute-done | bytes 5152 | tf_op jit(solution)/shard_map/ppermute | solution.py:27
  64.7 4.4 %collective-permute-start.16 = (f32[10,18,1]{2,1,0:T(8,128)S(1)}, f32[10,18,1]{2,1,0:T(8,128)S(1)}, u32[]{:S(2)}, u32[]{:S(2)}) collective-permute-start(f32[10,18,1]{2,1,0:T(8,128)S(1)} %get-tuple-element.35), channel_id=1, source_target_pairs={{0,1},{1,2},{2,3},{3,4},{4,5},{5,6},{6,7},{7,8},{8,9},{9,10},{10,1... | collective-permute-start | bytes 2168 | tf_op jit(solution)/shard_map/ppermute | solution.py:25
  69.1 1.9 collective-permute-start.17
  71.0 4.3 %collective-permute-done.17 = f32[10,18,1]{2,1,0:T(8,128)S(1)} collective-permute-done((f32[10,18,1]{2,1,0:T(8,128)S(1)}, f32[10,18,1]{2,1,0:T(8,128)S(1)}, u32[]{:S(2)}, u32[]{:S(2)}) %collective-permute-start.17) | collective-permute-done | bytes 752 | tf_op jit(solution)/shard_map/ppermute | solution.py:27
  76.7 1.4 pad_maximum_fusion.83
  78.0 19.1 %all_to_all.48 = f32[16,1,2]{2,1,0:T(1,128)S(1)} all-to-all(f32[16,1,2]{2,1,0:T(1,128)S(1)} %broadcast_in_dim.41), channel_id=1, replica_groups=mesh['gx'=4,'gy'=8,'gz_0'=8,'gz_1'=2] {'gz_0','gz_1'}, dimensions={0} | all-to-all | bytes 256 | tf_op jit(solution)/shard_map/all_to_all | solution.py:36
  97.1 16.2 %all_to_all.49 = f32[32,1,2]{2,1,0:T(1,128)S(1)} all-to-all(f32[32,1,2]{2,1,0:T(1,128)S(1)} %broadcast_in_dim.42), channel_id=1, replica_groups=mesh['gx'=4,'gy'=8,'gz_0'=8,'gz_1'=2] {'gx','gy'}, dimensions={0} | all-to-all | bytes 512 | tf_op jit(solution)/shard_map/all_to_all | solution.py:36
  115.3 2.2 collective-permute-start.18
  117.6 1.3 collective-permute-start.19
  118.9 3.1 %collective-permute-done.19 = f32[1,16,128]{2,1,0:T(8,128)S(1)} collective-permute-done((f32[1,16,128]{2,1,0:T(8,128)S(1)}, f32[1,16,128]{2,1,0:T(8,128)S(1)}, u32[]{:S(2)}, u32[]{:S(2)}) %collective-permute-start.19) | collective-permute-done | bytes 8224 | tf_op jit(solution)/shard_map/ppermute | solution.py:27
  122.0 2.2 collective-permute-start.20
  124.2 1.3 collective-permute-start.21
  125.5 3.1 %collective-permute-done.21 = f32[10,1,128]{2,1,0:T(1,128)S(1)} collective-permute-done((f32[10,1,128]{2,1,0:T(1,128)S(1)}, f32[10,1,128]{2,1,0:T(1,128)S(1)}, u32[]{:S(2)}, u32[]{:S(2)}) %collective-permute-start.21) | collective-permute-done | bytes 5152 | tf_op jit(solution)/shard_map/ppermute | solution.py:27
  128.7 7.0 %collective-permute-start.22 = (f32[10,18,1]{2,1,0:T(8,128)S(1)}, f32[10,18,1]{2,1,0:T(8,128)S(1)}, u32[]{:S(2)}, u32[]{:S(2)}) collective-permute-start(f32[10,18,1]{2,1,0:T(8,128)S(1)} %get-tuple-element.33), channel_id=1, source_target_pairs={{0,1},{1,2},{2,3},{3,4},{4,5},{5,6},{6,7},{7,8},{8,9},{9,10},{10,1... | collective-permute-start | bytes 2168 | tf_op jit(solution)/shard_map/ppermute | solution.py:25
  135.7 1.9 collective-permute-start.23
  137.7 4.3 %collective-permute-done.23 = f32[10,18,1]{2,1,0:T(8,128)S(1)} collective-permute-done((f32[10,18,1]{2,1,0:T(8,128)S(1)}, f32[10,18,1]{2,1,0:T(8,128)S(1)}, u32[]{:S(2)}, u32[]{:S(2)}) %collective-permute-start.23) | collective-permute-done | bytes 752 | tf_op jit(solution)/shard_map/ppermute | solution.py:27
  143.3 1.3 pad_maximum_fusion.84
  144.6 10.1 %all_to_all.50 = f32[16,1,2]{2,1,0:T(1,128)S(1)} all-to-all(f32[16,1,2]{2,1,0:T(1,128)S(1)} %broadcast_in_dim.43), channel_id=1, replica_groups=mesh['gx'=4,'gy'=8,'gz_0'=8,'gz_1'=2] {'gz_0','gz_1'}, dimensions={0} | all-to-all | bytes 256 | tf_op jit(solution)/shard_map/all_to_all | solution.py:36
  154.8 13.1 %all_to_all.51 = f32[32,1,2]{2,1,0:T(1,128)S(1)} all-to-all(f32[32,1,2]{2,1,0:T(1,128)S(1)} %broadcast_in_dim.44), channel_id=1, replica_groups=mesh['gx'=4,'gy'=8,'gz_0'=8,'gz_1'=2] {'gx','gy'}, dimensions={0} | all-to-all | bytes 512 | tf_op jit(solution)/shard_map/all_to_all | solution.py:36
  173.1 2.2 collective-permute-start.24
  175.3 1.3 collective-permute-start.25
  176.6 3.1 %collective-permute-done.25 = f32[1,16,128]{2,1,0:T(8,128)S(1)} collective-permute-done((f32[1,16,128]{2,1,0:T(8,128)S(1)}, f32[1,16,128]{2,1,0:T(8,128)S(1)}, u32[]{:S(2)}, u32[]{:S(2)}) %collective-permute-start.25) | collective-permute-done | bytes 8224 | tf_op jit(solution)/shard_map/ppermute | solution.py:27
  179.7 2.2 collective-permute-start.26
  182.0 1.3 collective-permute-start.27
  183.3 3.1 %collective-permute-done.27 = f32[10,1,128]{2,1,0:T(1,128)S(1)} collective-permute-done((f32[10,1,128]{2,1,0:T(1,128)S(1)}, f32[10,1,128]{2,1,0:T(1,128)S(1)}, u32[]{:S(2)}, u32[]{:S(2)}) %collective-permute-start.27) | collective-permute-done | bytes 5152 | tf_op jit(solution)/shard_map/ppermute | solution.py:27
  186.5 7.0 %collective-permute-start.28 = (f32[10,18,1]{2,1,0:T(8,128)S(1)}, f32[10,18,1]{2,1,0:T(8,128)S(1)}, u32[]{:S(2)}, u32[]{:S(2)}) collective-permute-start(f32[10,18,1]{2,1,0:T(8,128)S(1)} %get-tuple-element.31), channel_id=1, source_target_pairs={{0,1},{1,2},{2,3},{3,4},{4,5},{5,6},{6,7},{7,8},{8,9},{9,10},{10,1... | collective-permute-start | bytes 2168 | tf_op jit(solution)/shard_map/ppermute | solution.py:25
  193.5 1.9 collective-permute-start.29
  195.4 4.3 %collective-permute-done.29 = f32[10,18,1]{2,1,0:T(8,128)S(1)} collective-permute-done((f32[10,18,1]{2,1,0:T(8,128)S(1)}, f32[10,18,1]{2,1,0:T(8,128)S(1)}, u32[]{:S(2)}, u32[]{:S(2)}) %collective-permute-start.29) | collective-permute-done | bytes 752 | tf_op jit(solution)/shard_map/ppermute | solution.py:27
  201.0 1.4 pad_maximum_fusion.85
  202.4 10.1 %all_to_all.52 = f32[16,1,2]{2,1,0:T(1,128)S(1)} all-to-all(f32[16,1,2]{2,1,0:T(1,128)S(1)} %broadcast_in_dim.45), channel_id=1, replica_groups=mesh['gx'=4,'gy'=8,'gz_0'=8,'gz_1'=2] {'gz_0','gz_1'}, dimensions={0} | all-to-all | bytes 256 | tf_op jit(solution)/shard_map/all_to_all | solution.py:36
  212.5 13.1 %all_to_all.53 = f32[32,1,2]{2,1,0:T(1,128)S(1)} all-to-all(f32[32,1,2]{2,1,0:T(1,128)S(1)} %broadcast_in_dim.46), channel_id=1, replica_groups=mesh['gx'=4,'gy'=8,'gz_0'=8,'gz_1'=2] {'gx','gy'}, dimensions={0} | all-to-all | bytes 512 | tf_op jit(solution)/shard_map/all_to_all | solution.py:36
  230.1 2.2 collective-permute-start.30
  232.4 1.3 collective-permute-start.31
  233.7 3.1 %collective-permute-done.31 = f32[1,16,128]{2,1,0:T(8,128)S(1)} collective-permute-done((f32[1,16,128]{2,1,0:T(8,128)S(1)}, f32[1,16,128]{2,1,0:T(8,128)S(1)}, u32[]{:S(2)}, u32[]{:S(2)}) %collective-permute-start.31) | collective-permute-done | bytes 8224 | tf_op jit(solution)/shard_map/ppermute | solution.py:27
  236.8 2.2 collective-permute-start.32
  239.0 1.3 collective-permute-start.33
  240.4 3.1 %collective-permute-done.33 = f32[10,1,128]{2,1,0:T(1,128)S(1)} collective-permute-done((f32[10,1,128]{2,1,0:T(1,128)S(1)}, f32[10,1,128]{2,1,0:T(1,128)S(1)}, u32[]{:S(2)}, u32[]{:S(2)}) %collective-permute-start.33) | collective-permute-done | bytes 5152 | tf_op jit(solution)/shard_map/ppermute | solution.py:27
  243.5 7.0 %collective-permute-start.34 = (f32[10,18,1]{2,1,0:T(8,128)S(1)}, f32[10,18,1]{2,1,0:T(8,128)S(1)}, u32[]{:S(2)}, u32[]{:S(2)}) collective-permute-start(f32[10,18,1]{2,1,0:T(8,128)S(1)} %get-tuple-element.29), channel_id=1, source_target_pairs={{0,1},{1,2},{2,3},{3,4},{4,5},{5,6},{6,7},{7,8},{8,9},{9,10},{10,1... | collective-permute-start | bytes 2168 | tf_op jit(solution)/shard_map/ppermute | solution.py:25
  250.5 1.9 collective-permute-start.35
  252.5 4.3 %collective-permute-done.35 = f32[10,18,1]{2,1,0:T(8,128)S(1)} collective-permute-done((f32[10,18,1]{2,1,0:T(8,128)S(1)}, f32[10,18,1]{2,1,0:T(8,128)S(1)}, u32[]{:S(2)}, u32[]{:S(2)}) %collective-permute-start.35) | collective-permute-done | bytes 752 | tf_op jit(solution)/shard_map/ppermute | solution.py:27
  257.1 1.1 multiply_reduce_fusion.1
  258.2 1.4 pad_maximum_fusion.86
  259.6 10.1 %all_to_all.54 = f32[16,1,2]{2,1,0:T(1,128)S(1)} all-to-all(f32[16,1,2]{2,1,0:T(1,128)S(1)} %broadcast_in_dim.47), channel_id=1, replica_groups=mesh['gx'=4,'gy'=8,'gz_0'=8,'gz_1'=2] {'gz_0','gz_1'}, dimensions={0} | all-to-all | bytes 256 | tf_op jit(solution)/shard_map/all_to_all | solution.py:36
  269.7 13.1 %all_to_all.55 = f32[32,1,2]{2,1,0:T(1,128)S(1)} all-to-all(f32[32,1,2]{2,1,0:T(1,128)S(1)} %broadcast_in_dim.48), channel_id=1, replica_groups=mesh['gx'=4,'gy'=8,'gz_0'=8,'gz_1'=2] {'gx','gy'}, dimensions={0} | all-to-all | bytes 512 | tf_op jit(solution)/shard_map/all_to_all | solution.py:36
  (118 shorter events, 10.5 us)
Async XLA Ops:
  0.6 6.3 %copy-start = (f32[8,16,128]{2,1,0:T(8,128)S(1)}, f32[8,16,128]{2,1,0:T(8,128)}, u32[]{:S(2)}) copy-start(f32[8,16,128]{2,1,0:T(8,128)} %param.5) | copy-start | bytes 196612
  1.7 11.2 %collective-permute-start = (f32[1,16,128]{2,1,0:T(8,128)S(1)}, f32[1,16,128]{2,1,0:T(8,128)S(1)}, u32[]{:S(2)}, u32[]{:S(2)}) collective-permute-start(f32[1,16,128]{2,1,0:T(8,128)S(1)} %get-tuple-element.63), channel_id=1, source_target_pairs={{0,128},{128,256},{256,384},{1,129},{129,257},{257,385},{2,130},{1... | collective-permute-start | bytes 24584 | tf_op jit(solution)/shard_map/ppermute | solution.py:25
  5.7 7.3 %collective-permute-start.1 = (f32[1,16,128]{2,1,0:T(8,128)S(1)}, f32[1,16,128]{2,1,0:T(8,128)S(1)}, u32[]{:S(2)}, u32[]{:S(2)}) collective-permute-start(f32[1,16,128]{2,1,0:T(8,128)S(1)} %get-tuple-element.64), channel_id=1, source_target_pairs={{128,0},{256,128},{384,256},{129,1},{257,129},{385,257},{130,2},{2... | collective-permute-start | bytes 24584 | tf_op jit(solution)/shard_map/ppermute | solution.py:27
  7.0 10.5 %collective-permute-start.7 = (f32[1,16,128]{2,1,0:T(8,128)S(1)}, f32[1,16,128]{2,1,0:T(8,128)S(1)}, u32[]{:S(2)}, u32[]{:S(2)}) collective-permute-start(f32[1,16,128]{2,1,0:T(8,128)S(1)} %get-tuple-element.65), channel_id=1, source_target_pairs={{128,0},{256,128},{384,256},{129,1},{257,129},{385,257},{130,2},{2... | collective-permute-start | bytes 24584 | tf_op jit(solution)/shard_map/ppermute | solution.py:27
  8.3 9.2 %collective-permute-start.6 = (f32[1,16,128]{2,1,0:T(8,128)S(1)}, f32[1,16,128]{2,1,0:T(8,128)S(1)}, u32[]{:S(2)}, u32[]{:S(2)}) collective-permute-start(f32[1,16,128]{2,1,0:T(8,128)S(1)} %get-tuple-element.66), channel_id=1, source_target_pairs={{0,128},{128,256},{256,384},{1,129},{129,257},{257,385},{2,130},{1... | collective-permute-start | bytes 24584 | tf_op jit(solution)/shard_map/ppermute | solution.py:25
  12.9 9.9 %collective-permute-start.2 = (f32[10,1,128]{2,1,0:T(1,128)S(1)}, f32[10,1,128]{2,1,0:T(1,128)S(1)}, u32[]{:S(2)}, u32[]{:S(2)}) collective-permute-start(f32[10,1,128]{2,1,0:T(1,128)S(1)} %get-tuple-element.49), channel_id=1, source_target_pairs={{0,16},{16,32},{32,48},{48,64},{64,80},{80,96},{96,112},{1,17},{17... | collective-permute-start | bytes 15368 | tf_op jit(solution)/shard_map/ppermute | solution.py:25
  16.1 6.7 %collective-permute-start.3 = (f32[10,1,128]{2,1,0:T(1,128)S(1)}, f32[10,1,128]{2,1,0:T(1,128)S(1)}, u32[]{:S(2)}, u32[]{:S(2)}) collective-permute-start(f32[10,1,128]{2,1,0:T(1,128)S(1)} %get-tuple-element.50), channel_id=1, source_target_pairs={{16,0},{32,16},{48,32},{64,48},{80,64},{96,80},{112,96},{17,1},{33... | collective-permute-start | bytes 15368 | tf_op jit(solution)/shard_map/ppermute | solution.py:27
  17.5 5.4 %collective-permute-start.8 = (f32[10,1,128]{2,1,0:T(1,128)S(1)}, f32[10,1,128]{2,1,0:T(1,128)S(1)}, u32[]{:S(2)}, u32[]{:S(2)}) collective-permute-start(f32[10,1,128]{2,1,0:T(1,128)S(1)} %get-tuple-element.51), channel_id=1, source_target_pairs={{0,16},{16,32},{32,48},{48,64},{64,80},{80,96},{96,112},{1,17},{17... | collective-permute-start | bytes 15368 | tf_op jit(solution)/shard_map/ppermute | solution.py:25
  21.5 4.4 %collective-permute-start.9 = (f32[10,1,128]{2,1,0:T(1,128)S(1)}, f32[10,1,128]{2,1,0:T(1,128)S(1)}, u32[]{:S(2)}, u32[]{:S(2)}) collective-permute-start(f32[10,1,128]{2,1,0:T(1,128)S(1)} %get-tuple-element.52), channel_id=1, source_target_pairs={{16,0},{32,16},{48,32},{64,48},{80,64},{96,80},{112,96},{17,1},{33... | collective-permute-start | bytes 15368 | tf_op jit(solution)/shard_map/ppermute | solution.py:27
  26.0 14.9 %collective-permute-start.10 = (f32[10,18,1]{2,1,0:T(8,128)S(1)}, f32[10,18,1]{2,1,0:T(8,128)S(1)}, u32[]{:S(2)}, u32[]{:S(2)}) collective-permute-start(f32[10,18,1]{2,1,0:T(8,128)S(1)} %get-tuple-element.39), channel_id=1, source_target_pairs={{0,1},{1,2},{2,3},{3,4},{4,5},{5,6},{6,7},{7,8},{8,9},{9,10},{10,1... | collective-permute-start | bytes 2168 | tf_op jit(solution)/shard_map/ppermute | solution.py:25
  33.4 7.5 %collective-permute-start.11 = (f32[10,18,1]{2,1,0:T(8,128)S(1)}, f32[10,18,1]{2,1,0:T(8,128)S(1)}, u32[]{:S(2)}, u32[]{:S(2)}) collective-permute-start(f32[10,18,1]{2,1,0:T(8,128)S(1)} %get-tuple-element.40), channel_id=1, source_target_pairs={{1,0},{2,1},{3,2},{4,3},{5,4},{6,5},{7,6},{8,7},{9,8},{10,9},{11,1... | collective-permute-start | bytes 2168 | tf_op jit(solution)/shard_map/ppermute | solution.py:27
  35.3 5.6 %collective-permute-start.4 = (f32[10,18,1]{2,1,0:T(8,128)S(1)}, f32[10,18,1]{2,1,0:T(8,128)S(1)}, u32[]{:S(2)}, u32[]{:S(2)}) collective-permute-start(f32[10,18,1]{2,1,0:T(8,128)S(1)} %get-tuple-element.37), channel_id=1, source_target_pairs={{0,1},{1,2},{2,3},{3,4},{4,5},{5,6},{6,7},{7,8},{8,9},{9,10},{10,1... | collective-permute-start | bytes 2168 | tf_op jit(solution)/shard_map/ppermute | solution.py:25
  39.0 6.2 %collective-permute-start.5 = (f32[10,18,1]{2,1,0:T(8,128)S(1)}, f32[10,18,1]{2,1,0:T(8,128)S(1)}, u32[]{:S(2)}, u32[]{:S(2)}) collective-permute-start(f32[10,18,1]{2,1,0:T(8,128)S(1)} %get-tuple-element.38), channel_id=1, source_target_pairs={{1,0},{2,1},{3,2},{4,3},{5,4},{6,5},{7,6},{8,7},{9,8},{10,9},{11,1... | collective-permute-start | bytes 2168 | tf_op jit(solution)/shard_map/ppermute | solution.py:27
  45.7 0.8 copy-start.1
  45.7 0.9 copy-start.2
  47.1 5.0 %collective-permute-start.12 = (f32[1,16,128]{2,1,0:T(8,128)S(1)}, f32[1,16,128]{2,1,0:T(8,128)S(1)}, u32[]{:S(2)}, u32[]{:S(2)}) collective-permute-start(f32[1,16,128]{2,1,0:T(8,128)S(1)} %get-tuple-element.61), channel_id=1, source_target_pairs={{0,128},{128,256},{256,384},{1,129},{129,257},{257,385},{2,130},{1... | collective-permute-start | bytes 24584 | tf_op jit(solution)/shard_map/ppermute | solution.py:25
  50.8 4.4 %collective-permute-start.13 = (f32[1,16,128]{2,1,0:T(8,128)S(1)}, f32[1,16,128]{2,1,0:T(8,128)S(1)}, u32[]{:S(2)}, u32[]{:S(2)}) collective-permute-start(f32[1,16,128]{2,1,0:T(8,128)S(1)} %get-tuple-element.62), channel_id=1, source_target_pairs={{128,0},{256,128},{384,256},{129,1},{257,129},{385,257},{130,2},{2... | collective-permute-start | bytes 24584 | tf_op jit(solution)/shard_map/ppermute | solution.py:27
  55.2 4.9 %collective-permute-start.14 = (f32[10,1,128]{2,1,0:T(1,128)S(1)}, f32[10,1,128]{2,1,0:T(1,128)S(1)}, u32[]{:S(2)}, u32[]{:S(2)}) collective-permute-start(f32[10,1,128]{2,1,0:T(1,128)S(1)} %get-tuple-element.47), channel_id=1, source_target_pairs={{0,16},{16,32},{32,48},{48,64},{64,80},{80,96},{96,112},{1,17},{17... | collective-permute-start | bytes 15368 | tf_op jit(solution)/shard_map/ppermute | solution.py:25
  58.8 5.9 %collective-permute-start.15 = (f32[10,1,128]{2,1,0:T(1,128)S(1)}, f32[10,1,128]{2,1,0:T(1,128)S(1)}, u32[]{:S(2)}, u32[]{:S(2)}) collective-permute-start(f32[10,1,128]{2,1,0:T(1,128)S(1)} %get-tuple-element.48), channel_id=1, source_target_pairs={{16,0},{32,16},{48,32},{64,48},{80,64},{96,80},{112,96},{17,1},{33... | collective-permute-start | bytes 15368 | tf_op jit(solution)/shard_map/ppermute | solution.py:27
  64.7 6.3 %collective-permute-start.16 = (f32[10,18,1]{2,1,0:T(8,128)S(1)}, f32[10,18,1]{2,1,0:T(8,128)S(1)}, u32[]{:S(2)}, u32[]{:S(2)}) collective-permute-start(f32[10,18,1]{2,1,0:T(8,128)S(1)} %get-tuple-element.35), channel_id=1, source_target_pairs={{0,1},{1,2},{2,3},{3,4},{4,5},{5,6},{6,7},{7,8},{8,9},{9,10},{10,1... | collective-permute-start | bytes 2168 | tf_op jit(solution)/shard_map/ppermute | solution.py:25
  69.1 6.2 %collective-permute-start.17 = (f32[10,18,1]{2,1,0:T(8,128)S(1)}, f32[10,18,1]{2,1,0:T(8,128)S(1)}, u32[]{:S(2)}, u32[]{:S(2)}) collective-permute-start(f32[10,18,1]{2,1,0:T(8,128)S(1)} %get-tuple-element.36), channel_id=1, source_target_pairs={{1,0},{2,1},{3,2},{4,3},{5,4},{6,5},{7,6},{8,7},{9,8},{10,9},{11,1... | collective-permute-start | bytes 2168 | tf_op jit(solution)/shard_map/ppermute | solution.py:27
  115.3 3.6 %collective-permute-start.18 = (f32[1,16,128]{2,1,0:T(8,128)S(1)}, f32[1,16,128]{2,1,0:T(8,128)S(1)}, u32[]{:S(2)}, u32[]{:S(2)}) collective-permute-start(f32[1,16,128]{2,1,0:T(8,128)S(1)} %get-tuple-element.59), channel_id=1, source_target_pairs={{0,128},{128,256},{256,384},{1,129},{129,257},{257,385},{2,130},{1... | collective-permute-start | bytes 24584 | tf_op jit(solution)/shard_map/ppermute | solution.py:25
  117.6 4.4 %collective-permute-start.19 = (f32[1,16,128]{2,1,0:T(8,128)S(1)}, f32[1,16,128]{2,1,0:T(8,128)S(1)}, u32[]{:S(2)}, u32[]{:S(2)}) collective-permute-start(f32[1,16,128]{2,1,0:T(8,128)S(1)} %get-tuple-element.60), channel_id=1, source_target_pairs={{128,0},{256,128},{384,256},{129,1},{257,129},{385,257},{130,2},{2... | collective-permute-start | bytes 24584 | tf_op jit(solution)/shard_map/ppermute | solution.py:27
  122.0 3.6 %collective-permute-start.20 = (f32[10,1,128]{2,1,0:T(1,128)S(1)}, f32[10,1,128]{2,1,0:T(1,128)S(1)}, u32[]{:S(2)}, u32[]{:S(2)}) collective-permute-start(f32[10,1,128]{2,1,0:T(1,128)S(1)} %get-tuple-element.45), channel_id=1, source_target_pairs={{0,16},{16,32},{32,48},{48,64},{64,80},{80,96},{96,112},{1,17},{17... | collective-permute-start | bytes 15368 | tf_op jit(solution)/shard_map/ppermute | solution.py:25
  124.2 4.4 %collective-permute-start.21 = (f32[10,1,128]{2,1,0:T(1,128)S(1)}, f32[10,1,128]{2,1,0:T(1,128)S(1)}, u32[]{:S(2)}, u32[]{:S(2)}) collective-permute-start(f32[10,1,128]{2,1,0:T(1,128)S(1)} %get-tuple-element.46), channel_id=1, source_target_pairs={{16,0},{32,16},{48,32},{64,48},{80,64},{96,80},{112,96},{17,1},{33... | collective-permute-start | bytes 15368 | tf_op jit(solution)/shard_map/ppermute | solution.py:27
  128.7 8.9 %collective-permute-start.22 = (f32[10,18,1]{2,1,0:T(8,128)S(1)}, f32[10,18,1]{2,1,0:T(8,128)S(1)}, u32[]{:S(2)}, u32[]{:S(2)}) collective-permute-start(f32[10,18,1]{2,1,0:T(8,128)S(1)} %get-tuple-element.33), channel_id=1, source_target_pairs={{0,1},{1,2},{2,3},{3,4},{4,5},{5,6},{6,7},{7,8},{8,9},{9,10},{10,1... | collective-permute-start | bytes 2168 | tf_op jit(solution)/shard_map/ppermute | solution.py:25
  135.7 6.2 %collective-permute-start.23 = (f32[10,18,1]{2,1,0:T(8,128)S(1)}, f32[10,18,1]{2,1,0:T(8,128)S(1)}, u32[]{:S(2)}, u32[]{:S(2)}) collective-permute-start(f32[10,18,1]{2,1,0:T(8,128)S(1)} %get-tuple-element.34), channel_id=1, source_target_pairs={{1,0},{2,1},{3,2},{4,3},{5,4},{6,5},{7,6},{8,7},{9,8},{10,9},{11,1... | collective-permute-start | bytes 2168 | tf_op jit(solution)/shard_map/ppermute | solution.py:27
  173.1 3.6 %collective-permute-start.24 = (f32[1,16,128]{2,1,0:T(8,128)S(1)}, f32[1,16,128]{2,1,0:T(8,128)S(1)}, u32[]{:S(2)}, u32[]{:S(2)}) collective-permute-start(f32[1,16,128]{2,1,0:T(8,128)S(1)} %get-tuple-element.57), channel_id=1, source_target_pairs={{0,128},{128,256},{256,384},{1,129},{129,257},{257,385},{2,130},{1... | collective-permute-start | bytes 24584 | tf_op jit(solution)/shard_map/ppermute | solution.py:25
  175.3 4.4 %collective-permute-start.25 = (f32[1,16,128]{2,1,0:T(8,128)S(1)}, f32[1,16,128]{2,1,0:T(8,128)S(1)}, u32[]{:S(2)}, u32[]{:S(2)}) collective-permute-start(f32[1,16,128]{2,1,0:T(8,128)S(1)} %get-tuple-element.58), channel_id=1, source_target_pairs={{128,0},{256,128},{384,256},{129,1},{257,129},{385,257},{130,2},{2... | collective-permute-start | bytes 24584 | tf_op jit(solution)/shard_map/ppermute | solution.py:27
  179.7 3.6 %collective-permute-start.26 = (f32[10,1,128]{2,1,0:T(1,128)S(1)}, f32[10,1,128]{2,1,0:T(1,128)S(1)}, u32[]{:S(2)}, u32[]{:S(2)}) collective-permute-start(f32[10,1,128]{2,1,0:T(1,128)S(1)} %get-tuple-element.43), channel_id=1, source_target_pairs={{0,16},{16,32},{32,48},{48,64},{64,80},{80,96},{96,112},{1,17},{17... | collective-permute-start | bytes 15368 | tf_op jit(solution)/shard_map/ppermute | solution.py:25
  182.0 4.4 %collective-permute-start.27 = (f32[10,1,128]{2,1,0:T(1,128)S(1)}, f32[10,1,128]{2,1,0:T(1,128)S(1)}, u32[]{:S(2)}, u32[]{:S(2)}) collective-permute-start(f32[10,1,128]{2,1,0:T(1,128)S(1)} %get-tuple-element.44), channel_id=1, source_target_pairs={{16,0},{32,16},{48,32},{64,48},{80,64},{96,80},{112,96},{17,1},{33... | collective-permute-start | bytes 15368 | tf_op jit(solution)/shard_map/ppermute | solution.py:27
  186.5 8.9 %collective-permute-start.28 = (f32[10,18,1]{2,1,0:T(8,128)S(1)}, f32[10,18,1]{2,1,0:T(8,128)S(1)}, u32[]{:S(2)}, u32[]{:S(2)}) collective-permute-start(f32[10,18,1]{2,1,0:T(8,128)S(1)} %get-tuple-element.31), channel_id=1, source_target_pairs={{0,1},{1,2},{2,3},{3,4},{4,5},{5,6},{6,7},{7,8},{8,9},{9,10},{10,1... | collective-permute-start | bytes 2168 | tf_op jit(solution)/shard_map/ppermute | solution.py:25
  193.5 6.2 %collective-permute-start.29 = (f32[10,18,1]{2,1,0:T(8,128)S(1)}, f32[10,18,1]{2,1,0:T(8,128)S(1)}, u32[]{:S(2)}, u32[]{:S(2)}) collective-permute-start(f32[10,18,1]{2,1,0:T(8,128)S(1)} %get-tuple-element.32), channel_id=1, source_target_pairs={{1,0},{2,1},{3,2},{4,3},{5,4},{6,5},{7,6},{8,7},{9,8},{10,9},{11,1... | collective-permute-start | bytes 2168 | tf_op jit(solution)/shard_map/ppermute | solution.py:27
  230.1 3.6 %collective-permute-start.30 = (f32[1,16,128]{2,1,0:T(8,128)S(1)}, f32[1,16,128]{2,1,0:T(8,128)S(1)}, u32[]{:S(2)}, u32[]{:S(2)}) collective-permute-start(f32[1,16,128]{2,1,0:T(8,128)S(1)} %get-tuple-element.55), channel_id=1, source_target_pairs={{0,128},{128,256},{256,384},{1,129},{129,257},{257,385},{2,130},{1... | collective-permute-start | bytes 24584 | tf_op jit(solution)/shard_map/ppermute | solution.py:25
  232.4 4.4 %collective-permute-start.31 = (f32[1,16,128]{2,1,0:T(8,128)S(1)}, f32[1,16,128]{2,1,0:T(8,128)S(1)}, u32[]{:S(2)}, u32[]{:S(2)}) collective-permute-start(f32[1,16,128]{2,1,0:T(8,128)S(1)} %get-tuple-element.56), channel_id=1, source_target_pairs={{128,0},{256,128},{384,256},{129,1},{257,129},{385,257},{130,2},{2... | collective-permute-start | bytes 24584 | tf_op jit(solution)/shard_map/ppermute | solution.py:27
  236.8 3.6 %collective-permute-start.32 = (f32[10,1,128]{2,1,0:T(1,128)S(1)}, f32[10,1,128]{2,1,0:T(1,128)S(1)}, u32[]{:S(2)}, u32[]{:S(2)}) collective-permute-start(f32[10,1,128]{2,1,0:T(1,128)S(1)} %get-tuple-element.41), channel_id=1, source_target_pairs={{0,16},{16,32},{32,48},{48,64},{64,80},{80,96},{96,112},{1,17},{17... | collective-permute-start | bytes 15368 | tf_op jit(solution)/shard_map/ppermute | solution.py:25
  239.0 4.4 %collective-permute-start.33 = (f32[10,1,128]{2,1,0:T(1,128)S(1)}, f32[10,1,128]{2,1,0:T(1,128)S(1)}, u32[]{:S(2)}, u32[]{:S(2)}) collective-permute-start(f32[10,1,128]{2,1,0:T(1,128)S(1)} %get-tuple-element.42), channel_id=1, source_target_pairs={{16,0},{32,16},{48,32},{64,48},{80,64},{96,80},{112,96},{17,1},{33... | collective-permute-start | bytes 15368 | tf_op jit(solution)/shard_map/ppermute | solution.py:27
  243.5 8.9 %collective-permute-start.34 = (f32[10,18,1]{2,1,0:T(8,128)S(1)}, f32[10,18,1]{2,1,0:T(8,128)S(1)}, u32[]{:S(2)}, u32[]{:S(2)}) collective-permute-start(f32[10,18,1]{2,1,0:T(8,128)S(1)} %get-tuple-element.29), channel_id=1, source_target_pairs={{0,1},{1,2},{2,3},{3,4},{4,5},{5,6},{6,7},{7,8},{8,9},{9,10},{10,1... | collective-permute-start | bytes 2168 | tf_op jit(solution)/shard_map/ppermute | solution.py:25
  250.5 6.2 %collective-permute-start.35 = (f32[10,18,1]{2,1,0:T(8,128)S(1)}, f32[10,18,1]{2,1,0:T(8,128)S(1)}, u32[]{:S(2)}, u32[]{:S(2)}) collective-permute-start(f32[10,18,1]{2,1,0:T(8,128)S(1)} %get-tuple-element.30), channel_id=1, source_target_pairs={{1,0},{2,1},{3,2},{4,3},{5,4},{6,5},{7,6},{8,7},{9,8},{10,9},{11,1... | collective-permute-start | bytes 2168 | tf_op jit(solution)/shard_map/ppermute | solution.py:27
where the time goes:
time: 290 us; the launch traced here: 288 us
  blocking collectives  105 us (36%)
  starting transfers between devices  99.8 us (34%)
  waiting for transfers between devices  50.3 us (17%)
  between operations  15.3 us (5%)
  other arithmetic  14.1 us (5%)
  local copies, waits for them, and re-layouts  3.94 us (1%)
    all_to_all x8, blocking collectives, from_everyone(): return lax.all_to_all(copies, axis, split_axis=0, concat_axis=0, tiled=True)  105 us
    ppermute x18, starting transfers between devices, padded_2(): lax.ppermute(tail, axis, [(i, (i + 1) % count) for i in range(ends)])  72.8 us
    ppermute x18, waiting for transfers between devices, padded_2(): lax.ppermute(head, axis, [((i + 1) % count, i) for i in range(ends)])  50.2 us
    ppermute x18, starting transfers between devices, padded_2(): lax.ppermute(head, axis, [((i + 1) % count, i) for i in range(ends)])  27 us
  transfers between devices with their start and end apart: 36, of which 14 were waited for; matrix products, arithmetic and copies ran while one was open for 0% of the time, Pallas kernels for 0%

commit v1 on v0

v1 whole, which is shorter than its diff:
```python
import jax
import jax.numpy as jnp
from jax import lax
from jax.sharding import Mesh
from jax.sharding import PartitionSpec as P

ITERS = 4
GZ = ("gz_0", "gz_1")
HALO = ITERS + 1


def padded(cells, sides, width):
    for axis, dim in sides:
        count = lax.axis_size(axis)
        ends = count - 1
        head = lax.slice_in_dim(cells, 0, width, axis=dim)
        tail = lax.slice_in_dim(cells, cells.shape[dim] - width, cells.shape[dim], axis=dim)
        cells = jnp.concatenate(
            [
                lax.ppermute(tail, axis, [(i, i + 1) for i in range(ends)]),
                cells,
                lax.ppermute(head, axis, [(i + 1, i) for i in range(ends)]),
            ],
            axis=dim,
        )
    return cells


def over(array, axes):
    copies = jnp.broadcast_to(array, (lax.axis_size(axes), 1, array.shape[0]))
    return lax.all_to_all(copies, axes, split_axis=0, concat_axis=0, tiled=True).sum(axis=(0, 1))


def smooth(values):
    for dim in range(3):
        n = values.shape[dim]
        low = lax.slice_in_dim(values, 0, n - 2, axis=dim)
        mid = lax.slice_in_dim(values, 1, n - 1, axis=dim)
        high = lax.slice_in_dim(values, 2, n, axis=dim)
        values = mid + 0.5 * (low + high)
    return values


def inner(values, by):
    return values[by:-by, by:-by, by:-by] if by else values


def body(opening, source, category, table, flags):
    classes = table.shape[0]
    picks = category[None] == jnp.arange(classes, dtype=jnp.int32)[:, None, None, None]
    cond = jnp.sum(jnp.where(picks, table[:, None, None, None], 0.0), axis=0)
    flag = flags.astype(jnp.float32)
    rest = 2.0 * source - 6.0 * flag * opening
    fields = padded(
        jnp.stack([cond, opening, rest, flag]), (("gx", 1), ("gy", 2), (GZ, 3)), HALO
    )
    cond, start, rest, flag = fields

    least, most, mean = jnp.min(table), jnp.max(table), jnp.mean(table)
    top = 4.0 + 16.0 * most + 16.0 * mean
    low = 2.0 + 8.0 * least + 8.0 * mean
    half = 0.5 * (top - low)
    middle = 0.5 * (top + low)
    shifts = [middle + half * c for c in (0.9238795, -0.9238795, 0.3826834, -0.3826834)]

    near = 16.0 * inner(cond, 1) + 2.0 * smooth(cond)
    diagonal = near + 1.0 + 6.0 * inner(flag, 1)
    inside = (inner(cond, 1) > 0.0).astype(jnp.float32)
    c1 = inner(cond, 1)
    vector = inside * (
        inner(rest, 1) - near * inner(start, 1) + 2.0 * (c1 * smooth(start) + smooth(cond * start))
    )
    basis = [vector]
    for k in range(ITERS):
        at = inner(cond, k + 1)
        d, c, m = (inner(a, k + 1) for a in (diagonal, c1, inside))
        image = (d - shifts[k]) * inner(vector, 1) - 2.0 * (c * smooth(vector) + smooth(at * vector))
        vector = m * image / half
        basis.append(vector)
    own = [inner(v, ITERS - k) for k, v in enumerate(basis)]
    start = inner(start, HALO)

    pairs = [(i, j) for i in range(ITERS) for j in range(i, ITERS + 1)]
    dots = jnp.stack([jnp.sum(own[i] * own[j]) for i, j in pairs])
    dots = over(over(dots, ("gx", "gz_1")), ("gy", "gz_0"))
    gram = {}
    for n, (i, j) in enumerate(pairs):
        gram[i, j] = gram[j, i] = dots[n]

    def product(a, b):
        return sum(
            sum(gram[i, j] * a[i] * b[j] for j in range(len(b))) for i in range(len(a))
        )

    zero = jnp.zeros((), jnp.float32)
    r = [zero + 1.0]
    p = list(r)
    y = [zero] * ITERS
    rr = gram[0, 0]
    for k in range(ITERS):
        image = [shifts[i] * p[i] for i in range(k + 1)] + [zero]
        for i in range(k + 1):
            image[i + 1] = image[i + 1] + half * p[i]
        step = rr / product(p, image)
        y = [y[i] + step * p[i] if i <= k else y[i] for i in range(ITERS)]
        r = [(r[i] if i <= k else zero) - step * image[i] for i in range(k + 2)]
        if k + 1 < ITERS:
            new = product(r, r)
            p = [r[i] + (new / rr) * (p[i] if i <= k else zero) for i in range(k + 2)]
            rr = new
    closing = start + sum(y[i] * own[i] for i in range(ITERS))
    mismatch = sum(r[i] * own[i] for i in range(ITERS + 1))
    return closing, mismatch


def solution(mesh):
    split = Mesh(
        mesh.devices.reshape(mesh.shape["gx"], mesh.shape["gy"], 8, 2), ("gx", "gy", "gz_0", "gz_1")
    )
    spec = P("gx", "gy", GZ)
    return jax.shard_map(
        body, mesh=split, in_specs=(spec, spec, spec, P(), spec), out_specs=(spec, spec), check_vma=False
    )
```

time: 290 us -> 144 us (0.50)
  starting transfers between devices: 99.8 us -> 20 us
  blocking collectives: 105 us -> 36.5 us
  waiting for transfers between devices: 50.3 us -> 10.9 us
  between operations: 15.3 us -> 48.5 us
  local copies, waits for them, and re-layouts: 3.94 us -> 14.1 us
    ppermute x36 -> x6, starting transfers between devices: 99.8 us -> 20 us  [the longest x3 11.6 us: padded(): lax.ppermute(tail, axis, [(i, i + 1) for i in range(ends)])]
    all_to_all x8 -> x2, blocking collectives: 105 us -> 36.5 us  [over(): lax.all_to_all(copies, axes, split_axis=0, concat_axis=0, tiled=True)]
    ppermute x36 -> x6, waiting for transfers between devices: 50.3 us -> 10.9 us  [the longest x3 7.66 us: padded(): lax.ppermute(head, axis, [(i + 1, i) for i in range(ends)])]
    another operation x0 -> x2, local copies, waits for them, and re-layouts: none -> 9.03 us  [the longest x1 8.85 us: body(): dots = jnp.stack([jnp.sum(own[i] * own[j]) for i, j in pairs])]
    concatenate x10 -> x3, other arithmetic: 5.6 us -> 1.51 us  [padded(): jnp.concatenate([lax.ppermute(tail, axis, [(i, i + 1) for i in range(ends...]
    reduce_sum x13 -> x4, other arithmetic: 5.4 us -> 2.12 us  [the longest x1 1.03 us: body(): cond = jnp.sum(jnp.where(picks, table[:, None, None, None], 0.0), axis=0)]
  transfers between devices with their start and end apart: 36 -> 6, of which waited for: 14 -> 4; matrix products, arithmetic and copies ran while one was open for 0% -> 1% of each run, Pallas kernels for 0% -> 0%
where the time goes in v1:
time: 144 us; the launch traced here: 143 us
  between operations  48.5 us (34%)
  blocking collectives  36.5 us (25%)
  starting transfers between devices  20 us (14%)
  local copies, waits for them, and re-layouts  14.1 us (10%)
  other arithmetic  12.7 us (9%)
  waiting for transfers between devices  10.9 us (8%)
    all_to_all x2, blocking collectives, over(): lax.all_to_all(copies, axes, split_axis=0, concat_axis=0, tiled=True)  36.5 us
    ppermute x3, starting transfers between devices, padded(): lax.ppermute(tail, axis, [(i, i + 1) for i in range(ends)])  11.6 us
    another operation x1, local copies, waits for them, and re-layouts, body(): dots = jnp.stack([jnp.sum(own[i] * own[j]) for i, j in pairs])  8.85 us
    ppermute x3, starting transfers between devices, padded(): lax.ppermute(head, axis, [(i + 1, i) for i in range(ends)])  8.44 us
    ppermute x3, waiting for transfers between devices, padded(): lax.ppermute(head, axis, [(i + 1, i) for i in range(ends)])  7.66 us
    ppermute x3, waiting for transfers between devices, padded(): lax.ppermute(tail, axis, [(i, i + 1) for i in range(ends)])  3.27 us
    mul x4, other arithmetic, body(): at * vector  2.94 us
  transfers between devices with their start and end apart: 6, of which 4 were waited for; matrix products, arithmetic and copies ran while one was open for 1% of the time, Pallas kernels for 0%

profile of v1, /device:TPU:1, one launch (start us, length us, event | category | flops | bytes accessed | tf_op | source)
XLA Modules:
  0.0 142.7 jit_solution(1411724620107575550)
XLA Ops:
  0.6 0.0 copy-start
  0.6 0.9 convert_bitcast_fusion
  1.5 0.9 subtract_bitcast_fusion
  2.4 1.0 select_reduce_fusion
  3.5 0.9 pad_maximum_fusion.3
  4.4 3.9 %collective-permute-start = (f32[4,5,16,128]{3,2,1,0:T(8,128)S(1)}, f32[4,5,16,128]{3,2,1,0:T(8,128)S(1)}, u32[]{:S(2)}, u32[]{:S(2)}) collective-permute-start(f32[4,5,16,128]{3,2,1,0:T(8,128)S(1)} %get-tuple-element.45), channel_id=1, source_target_pairs={{0,128},{128,256},{256,384},{1,129},{129,257},{257,385},{2,130},{1... | collective-permute-start | bytes 491528 | tf_op jit(solution)/shard_map/ppermute | solution.py:20
  8.3 1.3 collective-permute-start.1
  9.6 0.9 collective-permute-done
  10.6 3.8 %collective-permute-done.1 = f32[4,5,16,128]{3,2,1,0:T(8,128)S(1)} collective-permute-done((f32[4,5,16,128]{3,2,1,0:T(8,128)S(1)}, f32[4,5,16,128]{3,2,1,0:T(8,128)S(1)}, u32[]{:S(2)}, u32[]{:S(2)}) %collective-permute-start.1) | collective-permute-done | bytes 163872 | tf_op jit(solution)/shard_map/ppermute | solution.py:22
  14.4 0.0 copy-done
  14.5 3.9 %collective-permute-start.2 = (f32[4,18,5,128]{3,2,1,0:T(8,128)S(1)}, f32[4,18,5,128]{3,2,1,0:T(8,128)S(1)}, u32[]{:S(2)}, u32[]{:S(2)}) collective-permute-start(f32[4,18,5,128]{3,2,1,0:T(8,128)S(1)} %get-tuple-element.42), channel_id=1, source_target_pairs={{0,16},{16,32},{32,48},{48,64},{64,80},{80,96},{96,112},{1,17},{17... | collective-permute-start | bytes 552968 | tf_op jit(solution)/shard_map/ppermute | solution.py:20
  18.4 1.3 collective-permute-start.3
  19.7 2.3 %collective-permute-done.2 = f32[4,18,5,128]{3,2,1,0:T(8,128)S(1)} collective-permute-done((f32[4,18,5,128]{3,2,1,0:T(8,128)S(1)}, f32[4,18,5,128]{3,2,1,0:T(8,128)S(1)}, u32[]{:S(2)}, u32[]{:S(2)}) %collective-permute-start.2) | collective-permute-done | bytes 184352 | tf_op jit(solution)/shard_map/ppermute | solution.py:20
  22.0 3.8 %collective-permute-done.3 = f32[4,18,5,128]{3,2,1,0:T(8,128)S(1)} collective-permute-done((f32[4,18,5,128]{3,2,1,0:T(8,128)S(1)}, f32[4,18,5,128]{3,2,1,0:T(8,128)S(1)}, u32[]{:S(2)}, u32[]{:S(2)}) %collective-permute-start.3) | collective-permute-done | bytes 184352 | tf_op jit(solution)/shard_map/ppermute | solution.py:22
  25.8 0.2 pad_maximum_fusion.1
  26.0 0.4 fusion.111
  26.4 0.0 copy-start.2
  26.4 1.2 copy.40
  27.7 0.0 copy-start.1
  27.7 0.5 copy.41
  28.2 5.9 %collective-permute-start.5 = (f32[4,18,26,5]{2,0,3,1:T(4,128)S(1)}, f32[4,18,26,5]{2,0,3,1:T(4,128)}, u32[]{:S(2)}, u32[]{:S(2)}) collective-permute-start(f32[4,18,26,5]{2,0,3,1:T(4,128)S(1)} %copy.41), channel_id=1, source_target_pairs={{1,0},{2,1},{3,2},{4,3},{5,4},{6,5},{7,6},{8,7},{9,8},{10,9},{11,1... | collective-permute-start | bytes 112328 | tf_op jit(solution)/shard_map/ppermute | solution.py:22
  34.1 0.0 copy-done.1
  34.1 3.8 %collective-permute-start.4 = (f32[4,18,26,5]{2,0,3,1:T(4,128)S(1)}, f32[4,18,26,5]{2,0,3,1:T(4,128)S(1)}, u32[]{:S(2)}, u32[]{:S(2)}) collective-permute-start(f32[4,18,26,5]{2,0,3,1:T(4,128)S(1)} %copy-done.1), channel_id=1, source_target_pairs={{0,1},{1,2},{2,3},{3,4},{4,5},{5,6},{6,7},{7,8},{8,9},{9,10},{10,1... | collective-permute-start | bytes 112328 | tf_op jit(solution)/shard_map/ppermute | solution.py:20
  37.9 0.0 copy-done.2
  37.9 0.7 fusion.103
  41.1 0.0 collective-permute-done.4
  41.1 0.6 copy.42
  41.7 0.0 collective-permute-done.5
  41.7 1.5 %copy.43 = f32[4,18,26,5]{3,2,1,0:T(8,128)S(1)} copy(f32[4,18,26,5]{2,0,3,1:T(4,128)} %collective-permute-done.5) | data formatting | bytes 74880 | tf_op jit(solution)/shard_map/ppermute | solution.py:22
  43.2 1.3 pad_maximum_fusion
  44.5 0.1 fusion.102
  44.6 0.1 fusion.7
  44.7 0.2 slice_bitcast_fusion.1
  44.9 0.1 fusion.1
  45.0 0.1 fusion.16
  45.1 0.2 fusion.108
  45.3 0.2 fusion.21
  45.4 0.5 fusion.8
  45.9 0.8 slice_multiply_fusion.4
  46.8 0.1 fusion.37
  47.0 0.1 fusion.44
  47.0 0.8 slice_multiply_fusion.3
  47.9 0.1 fusion.55
  48.0 0.1 fusion.62
  48.1 0.7 slice_multiply_fusion.6
  48.9 0.1 fusion.73
  49.0 0.1 fusion.80
  49.0 0.6 slice_multiply_fusion.8
  49.8 1.0 multiply_reduce_fusion.9
  50.8 8.9 %stack.79 = f32[14]{0:T(128)S(1)} concatenate(f32[1]{0:T(128)} %bitcast.9, f32[1]{0:T(128)} %bitcast.11, f32[1]{0:T(128)} %bitcast.12, f32[1]{0:T(128)} %bitcast.13, f32[1]{0:T(128)} %bitcast.14, f32[1]{0:T(128)} %bitcast.15, f32[1]{0:T(128)} %bitcast.16, f32[1]{0:T(128)} %bitcast.17, f32[1]{0:T(128)} %bitcast.18, f32[1]{0:T(128)} %bitcast.19, f32[1]{0:T(128)} %bitcast.20, ...), dimensions={0} | concatenate | bytes 112 | tf_op jit(solution)/shard_map/stack | solution.py:84
  59.6 8.5 %all_to_all.10 = f32[8,1,14]{2,1,0:T(1,128)S(1)} all-to-all(f32[8,1,14]{2,1,0:T(1,128)S(1)} %broadcast_in_dim.23), channel_id=1, replica_groups=mesh['gx'=4,'gy'=8,'gz_0'=8,'gz_1'=2] {'gx','gz_1'}, dimensions={0} | all-to-all | bytes 896 | tf_op jit(solution)/shard_map/all_to_all | solution.py:31
  68.2 27.9 %all_to_all.11 = f32[64,1,14]{2,1,0:T(1,128)S(1)} all-to-all(f32[64,1,14]{2,1,0:T(1,128)S(1)} %broadcast_in_dim.24), channel_id=1, replica_groups=mesh['gx'=4,'gy'=8,'gz_0'=8,'gz_1'=2] {'gy','gz_0'}, dimensions={0} | all-to-all | bytes 7168 | tf_op jit(solution)/shard_map/all_to_all | solution.py:31
  96.1 0.1 reduce_sum.179
  96.2 0.7 fusion.114
  141.9 0.8 multiply_add_fusion
  (16 shorter events, 0.5 us)
Async XLA Ops:
  0.6 13.8 %copy-start = (f32[8,16,128]{2,1,0:T(8,128)S(1)}, f32[8,16,128]{2,1,0:T(8,128)}, u32[]{:S(2)}) copy-start(f32[8,16,128]{2,1,0:T(8,128)} %param.5) | copy-start | bytes 196612
  4.4 6.2 %collective-permute-start = (f32[4,5,16,128]{3,2,1,0:T(8,128)S(1)}, f32[4,5,16,128]{3,2,1,0:T(8,128)S(1)}, u32[]{:S(2)}, u32[]{:S(2)}) collective-permute-start(f32[4,5,16,128]{3,2,1,0:T(8,128)S(1)} %get-tuple-element.45), channel_id=1, source_target_pairs={{0,128},{128,256},{256,384},{1,129},{129,257},{257,385},{2,130},{1... | collective-permute-start | bytes 491528 | tf_op jit(solution)/shard_map/ppermute | solution.py:20
  8.3 6.1 %collective-permute-start.1 = (f32[4,5,16,128]{3,2,1,0:T(8,128)S(1)}, f32[4,5,16,128]{3,2,1,0:T(8,128)S(1)}, u32[]{:S(2)}, u32[]{:S(2)}) collective-permute-start(f32[4,5,16,128]{3,2,1,0:T(8,128)S(1)} %get-tuple-element.46), channel_id=1, source_target_pairs={{128,0},{256,128},{384,256},{129,1},{257,129},{385,257},{130,2},{2... | collective-permute-start | bytes 491528 | tf_op jit(solution)/shard_map/ppermute | solution.py:22
  14.5 7.5 %collective-permute-start.2 = (f32[4,18,5,128]{3,2,1,0:T(8,128)S(1)}, f32[4,18,5,128]{3,2,1,0:T(8,128)S(1)}, u32[]{:S(2)}, u32[]{:S(2)}) collective-permute-start(f32[4,18,5,128]{3,2,1,0:T(8,128)S(1)} %get-tuple-element.42), channel_id=1, source_target_pairs={{0,16},{16,32},{32,48},{48,64},{64,80},{80,96},{96,112},{1,17},{17... | collective-permute-start | bytes 552968 | tf_op jit(solution)/shard_map/ppermute | solution.py:20
  18.4 7.5 %collective-permute-start.3 = (f32[4,18,5,128]{3,2,1,0:T(8,128)S(1)}, f32[4,18,5,128]{3,2,1,0:T(8,128)S(1)}, u32[]{:S(2)}, u32[]{:S(2)}) collective-permute-start(f32[4,18,5,128]{3,2,1,0:T(8,128)S(1)} %get-tuple-element.43), channel_id=1, source_target_pairs={{16,0},{32,16},{48,32},{64,48},{80,64},{96,80},{112,96},{17,1},{33... | collective-permute-start | bytes 552968 | tf_op jit(solution)/shard_map/ppermute | solution.py:22
  26.4 11.5 %copy-start.2 = (f32[16]{0:T(128)S(1)}, f32[16]{0:T(128)}, u32[]{:S(2)}) copy-start(f32[16]{0:T(128)} %param.8) | copy-start | bytes 196
  27.7 6.4 %copy-start.1 = (f32[4,18,26,5]{2,0,3,1:T(4,128)S(1)}, f32[4,18,26,5]{2,0,3,1:T(4,128)}, u32[]{:S(2)}) copy-start(f32[4,18,26,5]{2,0,3,1:T(4,128)} %copy.40) | copy-start | bytes 112324
  28.2 13.5 %collective-permute-start.5 = (f32[4,18,26,5]{2,0,3,1:T(4,128)S(1)}, f32[4,18,26,5]{2,0,3,1:T(4,128)}, u32[]{:S(2)}, u32[]{:S(2)}) collective-permute-start(f32[4,18,26,5]{2,0,3,1:T(4,128)S(1)} %copy.41), channel_id=1, source_target_pairs={{1,0},{2,1},{3,2},{4,3},{5,4},{6,5},{7,6},{8,7},{9,8},{10,9},{11,1... | collective-permute-start | bytes 112328 | tf_op jit(solution)/shard_map/ppermute | solution.py:22
  34.1 7.0 %collective-permute-start.4 = (f32[4,18,26,5]{2,0,3,1:T(4,128)S(1)}, f32[4,18,26,5]{2,0,3,1:T(4,128)S(1)}, u32[]{:S(2)}, u32[]{:S(2)}) collective-permute-start(f32[4,18,26,5]{2,0,3,1:T(4,128)S(1)} %copy-done.1), channel_id=1, source_target_pairs={{0,1},{1,2},{2,3},{3,4},{4,5},{5,6},{6,7},{7,8},{8,9},{9,10},{10,1... | collective-permute-start | bytes 112328 | tf_op jit(solution)/shard_map/ppermute | solution.py:20

commit v2 on v1

v2 whole, which is shorter than its diff:
```python
import jax
import jax.numpy as jnp
from jax import lax
from jax.experimental import pallas as pl
from jax.experimental.pallas import tpu as pltpu
from jax.sharding import Mesh
from jax.sharding import PartitionSpec as P

ITERS = 4
GZ = ("gz_0", "gz_1")
F32 = jnp.float32
X, Y, Z = 8, 16, 128
HALO = ITERS + 1
WIDTHS = (5, 5, 4, 3)
PLANES = X + 2 * HALO
ROWS = 32
TOP = 8
SLAB_X = sum(WIDTHS)
AT_X = (0, 5, 10, 14)
AT_Y = (0, 90, 180, 244)
SLAB_Y = 288
GROUPS, PER_GROUP, STRIDE = 3, 6, 40
BASES = (5, 15, 24, 31)
SCALE = 64.0
PAIRS = [(i, j) for i in range(ITERS) for j in range(i, ITERS + 1)]
VMEM = pl.BlockSpec(memory_space=pltpu.VMEM)
SMEM = pl.BlockSpec(memory_space=pltpu.SMEM)


def planes_of(k):
    return range(HALO - WIDTHS[k], PLANES - HALO + WIDTHS[k])


def call(kernel, ins, outs, scratch=(), flops=100000, vmem=8):
    return pl.pallas_call(
        kernel,
        in_specs=ins,
        out_specs=[VMEM] * len(outs),
        out_shape=[jax.ShapeDtypeStruct(s, F32) for s in outs],
        scratch_shapes=[pltpu.VMEM(s, F32) for s in scratch],
        compiler_params=pltpu.CompilerParams(vmem_limit_bytes=vmem * 2**20),
        cost_estimate=pl.CostEstimate(flops=flops, bytes_accessed=1000000, transcendentals=0),
    )


def prepare(opening, source, category, flags, table, fields, low, high):
    for p in range(X):
        kind = category[p]
        cond = jnp.full((Y, Z), table[0], F32)
        for n in range(1, table.shape[0]):
            cond = jnp.where(kind == n, table[n], cond)
        flag = flags[p].astype(F32)
        start = opening[p]
        values = (cond, start, 2.0 * source[p] - 6.0 * flag * start, flag)
        for k, v in enumerate(values):
            fields[k, p] = v
            if p < WIDTHS[k]:
                low[AT_X[k] + p] = v
            if p >= X - WIDTHS[k]:
                high[AT_X[k] + p - (X - WIDTHS[k])] = v


def plane(fields, left, right, k, p):
    if p < HALO:
        return left, (AT_X[k] + p - (HALO - WIDTHS[k]),)
    if p < HALO + X:
        return fields, (k, p - HALO)
    return right, (AT_X[k] + p - HALO - X,)


def slabs_y(fields, left, right, low, high):
    for k, w in enumerate(WIDTHS):
        for n, p in enumerate(planes_of(k)):
            ref, at = plane(fields, left, right, k, p)
            to = pl.ds(AT_Y[k] + w * n, w)
            low[to] = ref[(*at, pl.ds(0, w))]
            high[to] = ref[(*at, pl.ds(Y - w, w))]


def assemble(fields, left, right, below, above, wide, packed):
    lane = lax.broadcasted_iota(jnp.int32, (ROWS, Z), 1)
    nothing = jnp.zeros((8, Z), F32)
    for k, w in enumerate(WIDTHS):
        for n, p in enumerate(planes_of(k)):
            ref, at = plane(fields, left, right, k, p)
            wide[k, p, 0:TOP] = nothing
            wide[k, p, TOP + Y : ROWS] = nothing
            wide[k, p, TOP : TOP + Y] = ref[at]
            wide[k, p, TOP - w : TOP] = below[AT_Y[k] + w * n : AT_Y[k] + w * (n + 1)]
            wide[k, p, TOP + Y : TOP + Y + w] = above[AT_Y[k] + w * n : AT_Y[k] + w * (n + 1)]
    for q in range(PER_GROUP):
        out = jnp.zeros((ROWS, Z), F32)
        for g in range(GROUPS):
            p = PER_GROUP * g + q
            for k, w in enumerate(WIDTHS):
                if p in planes_of(k):
                    base = STRIDE * g + BASES[k]
                    here = (lane >= base - w) & (lane < base + w)
                    out = jnp.where(here, pltpu.roll(wide[k, p], base, 1), out)
        packed[q] = out


def shifts_of(table):
    values = [jnp.full((8, Z), table[n], F32) for n in range(table.shape[0])]
    least, most, mean = values[0], values[0], values[0]
    for v in values[1:]:
        least, most, mean = jnp.minimum(least, v), jnp.maximum(most, v), mean + v
    mean = mean * (1.0 / len(values))
    top = 4.0 + 16.0 * most + 16.0 * mean
    low = 2.0 + 8.0 * least + 8.0 * mean
    middle, half = 0.5 * (top + low), 0.5 * (top - low)
    return [
        (middle + half * c) * (1.0 / SCALE) for c in (0.9238795, -0.9238795, 0.3826834, -0.3826834)
    ]


def krylov(wide, from_left, from_right, table, basis, dots, ends, fore, fore_c, back, back_c, diag, mid):
    lane = lax.broadcasted_iota(jnp.int32, (ROWS, Z), 1)

    for q in range(PER_GROUP):
        left = lane < 0
        for g in range(GROUPS):
            for k, w in enumerate(WIDTHS):
                base = STRIDE * g + BASES[k]
                left = left | ((lane >= base - w) & (lane < base))
        both = jnp.where(left, from_left[q], from_right[q])
        for g in range(GROUPS):
            p = PER_GROUP * g + q
            for k, w in enumerate(WIDTHS):
                if p in planes_of(k):
                    turned = pltpu.roll(both, (Z - STRIDE * g - BASES[k]) % Z, 1)
                    ends[k, p] = jnp.where((lane < w) | (lane >= Z - w), turned, 0.0)

    def field(k, side, p):
        return wide[k, p] if side == 0 else ends[k, p]

    def smooth(get, slot, p, first, count, sides):
        summed = []
        for side in (0, 1):
            mid[slot, side, pl.ds(8, ROWS)] = get(side, p) + 0.5 * (get(side, p - 1) + get(side, p + 1))
        for side in (0, 1):
            ref = mid.at[slot, side]
            centre = ref[pl.ds(8 + first, count)]
            summed.append(
                centre + 0.5 * (ref[pl.ds(7 + first, count)] + ref[pl.ds(9 + first, count)])
            )
        up = [pltpu.roll(a, 1, 1) for a in summed]
        down = [pltpu.roll(a, Z - 1, 1) for a in summed]
        at = lane[:count]
        out = []
        for side in range(sides):
            lower = jnp.where(at == 0, up[1 - side], up[side])
            upper = jnp.where(at == Z - 1, down[1 - side], down[side])
            out.append(summed[side] + 0.5 * (lower + upper))
        return out

    for p in range(PLANES):
        for side in (0, 1):
            back_c[side, p] = field(0, side, p) * field(1, side, p)
    slots = mid.shape[0]
    slot = 0
    for p in range(1, PLANES - 1):
        tc = smooth(lambda s, n: field(0, s, n), slot % slots, p, 0, ROWS, 2)
        tx = smooth(lambda s, n: field(1, s, n), (slot + 1) % slots, p, 0, ROWS, 2)
        tcx = smooth(lambda s, n: back_c[s, n], (slot + 2) % slots, p, 0, ROWS, 2)
        slot += 3
        for side in (0, 1):
            c = field(0, side, p)
            near = 16.0 * c + 2.0 * tc[side]
            if p in planes_of(3):
                diag[side, p] = (1.0 + 6.0 * field(3, side, p) + near) * (1.0 / SCALE)
            r = field(2, side, p) - near * field(1, side, p) + 2.0 * (c * tx[side] + tcx[side])
            r = jnp.where(c > 0.0, r, 0.0)
            fore[side, p] = r
            fore_c[side, p] = r * (c * (2.0 / SCALE))
            if side == 0 and HALO <= p < HALO + X:
                basis[0, p - HALO] = r[TOP : TOP + Y]

    theta = shifts_of(table)
    for k in range(ITERS):
        old, old_c, new, new_c = (
            (fore, fore_c, back, back_c) if k % 2 == 0 else (back, back_c, fore, fore_c)
        )
        last = k + 1 == ITERS
        first, count, sides = (TOP, Y, 1) if last else (0, ROWS, 2)
        turn = jnp.tile(theta[k], (count // 8, 1))
        for p in range(2 + k, PLANES - 2 - k):
            tv = smooth(lambda s, n: old[s, n], slot % slots, p, first, count, sides)
            tu = smooth(lambda s, n: old_c[s, n], (slot + 1) % slots, p, first, count, sides)
            slot += 2
            for side in range(sides):
                rows = pl.ds(first, count)
                c = (wide if side == 0 else ends)[0, p, rows]
                half_c = c * (2.0 / SCALE)
                v = (diag[side, p, rows] - turn) * old[side, p, rows] - (half_c * tv[side] + tu[side])
                v = jnp.where(c > 0.0, v, 0.0)
                if not last:
                    new[side, p] = v
                    new_c[side, p] = v * half_c
                if side == 0 and HALO <= p < HALO + X:
                    basis[k + 1, p - HALO] = v if last else v[TOP : TOP + Y]

    sums = []
    for i, j in PAIRS:
        total = None
        for p in range(X):
            for half in (0, 8):
                term = basis[i, p, half : half + 8] * basis[j, p, half : half + 8]
                total = term if total is None else total + term
        sums.append(total)
    sums += [jnp.zeros((8, Z), F32)] * (16 - len(sums))
    at = lane[:8]
    step = 64
    while len(sums) > 1:
        half = len(sums) // 2
        low = (at // step) % 2 == 0
        sums = [
            jnp.where(low, a, b) + jnp.where(low, pltpu.roll(a, Z - step, 1), pltpu.roll(b, step, 1))
            for a, b in zip(sums[:half], sums[half:])
        ]
        step //= 2
    (total,) = sums
    for by in (4, 2, 1):
        turned = jnp.where((at & by) == 0, pltpu.roll(total, Z - by, 1), pltpu.roll(total, by, 1))
        total = total + turned
    for by in (4, 2, 1):
        total = total + pltpu.roll(total, by, 0)
    for n in range(dots.shape[0]):
        dots[n] = total[0:1]


def lane_of(n):
    return sum(((n >> (3 - b)) & 1) * (64 >> b) for b in range(4))


def two_sum(a, b):
    s = a + b
    t = s - a
    return s, (a - (s - t)) + (b - t)


def row_sum(parts):
    rows = [(parts[n], None) for n in range(parts.shape[0])]
    while len(rows) > 1:
        pairs, rows = zip(rows[::2], rows[1::2]), []
        for (a, ea), (b, eb) in pairs:
            s, e = two_sum(a, b)
            rows.append((s, e if ea is None else e + (ea + eb)))
    return rows[0]


def relay(parts, copies):
    total, rest = row_sum(parts)
    lane = lax.broadcasted_iota(jnp.int32, total.shape, 1)
    total = jnp.where((lane & 4) == 0, total, rest)
    for n in range(copies.shape[0]):
        copies[n] = total


def quick(a, b):
    s = a + b
    return s, b - (s - a)


def halves(a):
    t = 4097.0 * a
    high = t - (t - a)
    return high, a - high


def plus(a, b):
    s, e = two_sum(a[0], b[0])
    return quick(s, e + (a[1] + b[1]))


def minus(a, b):
    return plus(a, (-b[0], -b[1]))


def times(a, b):
    p = a[0] * b[0]
    ah, al = halves(a[0])
    bh, bl = halves(b[0])
    e = ((ah * bh - p) + ah * bl + al * bh) + al * bl
    return quick(p, e + (a[0] * b[1] + a[1] * b[0]))


def over(a, b):
    q = a[0] / b[0]
    none = jnp.zeros_like(q)
    rest = minus(a, times((q, none), b))
    return quick(q, rest[0] / b[0])


def conjugate_gradients(gram, theta):
    none = jnp.zeros_like(theta[0])
    zero, one = (none, none), (none + 1.0, none)
    shift = [(t, none) for t in theta]

    def along(k, vector):
        total = times(gram[k, 0], vector[0])
        for j in range(1, len(vector)):
            total = plus(total, times(gram[k, j], vector[j]))
        return total

    r, p = [one], [one]
    y = [zero] * ITERS
    rr = gram[0, 0]
    for k in range(ITERS):
        image = [times(shift[i], p[i]) for i in range(k + 1)] + [zero]
        image = [image[0]] + [plus(image[i], p[i - 1]) for i in range(1, k + 2)]
        step = over(rr, times(p[k], along(k, image)))
        y = [plus(y[i], times(step, p[i])) if i <= k else y[i] for i in range(ITERS)]
        r = [minus(r[i] if i <= k else zero, times(step, image[i])) for i in range(k + 2)]
        if k + 1 < ITERS:
            new = times(r[k + 1], along(k + 1, r))
            ratio = over(new, rr)
            p = [plus(r[i], times(ratio, p[i])) if i <= k else r[i] for i in range(k + 2)]
            rr = new
    return [a[0] * (1.0 / SCALE) for a in y], [a[0] for a in r]


def finish(parts, basis, opening, table, closing, mismatch):
    total, rest = row_sum(parts)
    rest = rest + pltpu.roll(total, Z - 4, 1)
    gram = {}
    for n, (i, j) in enumerate(PAIRS):
        at = lane_of(n)
        gram[i, j] = gram[j, i] = quick(
            *(jnp.broadcast_to(v[0:1, at : at + 1], (8, Z)) for v in (total, rest))
        )
    y, r = conjugate_gradients(gram, shifts_of(table))
    for p in range(X):
        for half in (0, 8):
            rows = pl.ds(half, 8)
            v = [basis[k, p, rows] for k in range(ITERS + 1)]
            x, m = opening[p, rows], r[ITERS] * v[ITERS]
            for k in range(ITERS):
                x, m = x + y[k] * v[k], m + r[k] * v[k]
            closing[p, rows] = x
            mismatch[p, rows] = m


def both_ways(low, high, axis):
    ends = lax.axis_size(axis) - 1
    from_below = lax.ppermute(high, axis, [(i, i + 1) for i in range(ends)])
    from_above = lax.ppermute(low, axis, [(i + 1, i) for i in range(ends)])
    return from_below, from_above


def exchange(copies, axes):
    return lax.all_to_all(copies, axes, split_axis=0, concat_axis=0, tiled=True)


def body(opening, source, category, table, flags):
    brick = (X, Y, Z)
    fields, low, high = call(
        prepare, [VMEM] * 4 + [SMEM], [(4, *brick), (SLAB_X, Y, Z), (SLAB_X, Y, Z)]
    )(opening, source, category, flags, table)
    left, right = both_ways(low, high, "gx")
    low, high = call(slabs_y, [VMEM] * 3, [(SLAB_Y, Z)] * 2)(fields, left, right)
    below, above = both_ways(low, high, "gy")
    wide, packed = call(
        assemble, [VMEM] * 5, [(4, PLANES, ROWS, Z), (PER_GROUP, ROWS, Z)]
    )(fields, left, right, below, above)
    from_left, from_right = both_ways(packed, packed, GZ)
    first, second = ("gx", "gz_1"), ("gy", "gz_0")
    sided = (2, PLANES, ROWS, Z)
    basis, dots = call(
        krylov,
        [VMEM] * 3 + [SMEM],
        [(ITERS + 1, *brick), (lax.axis_size(first), 1, Z)],
        [(4, PLANES, ROWS, Z)] + [sided] * 5 + [(6, 2, ROWS + 16, Z)],
        flops=20000000,
        vmem=16,
    )(wide, from_left, from_right, table)
    parts = exchange(dots, first)
    (copies,) = call(relay, [VMEM], [(lax.axis_size(second), 1, Z)])(parts)
    parts = exchange(copies, second)
    closing, mismatch = call(finish, [VMEM] * 3 + [SMEM], [brick, brick])(
        parts, basis, opening, table
    )
    return closing, mismatch


def solution(mesh):
    shape = mesh.devices.shape
    split = Mesh(mesh.devices.reshape(shape[0], shape[1], shape[2] // 2, 2), ("gx", "gy", *GZ))
    spec = P("gx", "gy", GZ)
    return jax.shard_map(
        body, mesh=split, in_specs=(spec, spec, spec, P(), spec), out_specs=(spec, spec), check_vma=False
    )
```

time: 144 us -> 80.4 us (0.56)
  between operations: 48.5 us -> 0.73 us
  other arithmetic: 12.7 us -> 0 us
  local copies, waits for them, and re-layouts: 14.1 us -> 4.02 us
  Pallas kernels: 0 us -> 7.96 us
    another operation x2 -> x0, local copies, waits for them, and re-layouts: 9.03 us -> none  [the longest x1 8.85 us: body(): dots = jnp.stack([jnp.sum(own[i] * own[j]) for i, j in pairs])]
    pallas_call x0 -> x6, Pallas kernels: none -> 7.96 us  [the longest x1 4.83 us: body(): call(krylov, [VMEM] * 3 + [SMEM], [(ITERS + 1, *brick), (lax.axis_size(fi...]
    unnamed x6 -> x14, local copies, waits for them, and re-layouts: 0.02 us -> 4.02 us
    mul x5 -> x0, other arithmetic: 3.02 us -> none  [the longest x4 2.94 us: body(): at * vector]
    slice x6 -> x0, local copies, waits for them, and re-layouts: 2.94 us -> none  [the longest x4 1.7 us: padded(): lax.slice_in_dim(cells, cells.shape[dim] - width, cells.shape[dim], axis=...]
    another operation x3 -> x0, other arithmetic: 2.66 us -> none  [body(): jnp.stack([cond, opening, rest, flag])]
    add x22 -> x0, other arithmetic: 2.51 us -> none  [the longest x20 1.21 us: smooth(): values = mid + 0.5 * (low + high)]
    reduce_sum x4 -> x0, other arithmetic: 2.12 us -> none  [the longest x1 1.03 us: body(): cond = jnp.sum(jnp.where(picks, table[:, None, None, None], 0.0), axis=0)]
  transfers between devices with their start and end apart: 6 -> 6, of which waited for: 4 -> 6; matrix products, arithmetic and copies ran while one was open for 1% -> 0% of each run, Pallas kernels for 0% -> 0%
where the time goes in v2:
time: 80.4 us; the launch traced here: 79.9 us
  blocking collectives  37.2 us (46%)
  starting transfers between devices  19.3 us (24%)
  waiting for transfers between devices  10.7 us (13%)
  Pallas kernels  7.96 us (10%)
  local copies, waits for them, and re-layouts  4.02 us (5%)
    all_to_all x2, blocking collectives, exchange(): return lax.all_to_all(copies, axes, split_axis=0, concat_axis=0, tiled=True)  37.2 us
    ppermute x3, starting transfers between devices, both_ways(): from_below = lax.ppermute(high, axis, [(i, i + 1) for i in range(ends)])  10.6 us
    ppermute x3, starting transfers between devices, both_ways(): from_above = lax.ppermute(low, axis, [(i + 1, i) for i in range(ends)])  8.7 us
    ppermute x3, waiting for transfers between devices, both_ways(): from_above = lax.ppermute(low, axis, [(i + 1, i) for i in range(ends)])  7.97 us
    pallas_call x1, Pallas kernels, body(): call(krylov, [VMEM] * 3 + [SMEM], [(ITERS + 1, *brick), (lax.axis_size(fi...  4.83 us
    unnamed x14, local copies, waits for them, and re-layouts  4.02 us
    ppermute x3, waiting for transfers between devices, both_ways(): from_below = lax.ppermute(high, axis, [(i, i + 1) for i in range(ends)])  2.73 us
    pallas_call x1, Pallas kernels, body(): call(finish, [VMEM] * 3 + [SMEM], [brick, brick])  2.03 us
  transfers between devices with their start and end apart: 6, of which 6 were waited for; matrix products, arithmetic and copies ran while one was open for 0% of the time, Pallas kernels for 0%

profile of v2, /device:TPU:1, one launch (start us, length us, event | category | flops | bytes accessed | tf_op | source)
XLA Modules:
  0.0 79.9 jit_solution(10878394847633859303)
XLA Ops:
  0.6 0.0 copy-start
  0.6 0.8 %copy-done = f32[8,16,128]{2,1,0:T(8,128)S(1)} copy-done((f32[8,16,128]{2,1,0:T(8,128)S(1)}, f32[8,16,128]{2,1,0:T(8,128)}, u32[]{:S(2)}) %copy-start) | copy-done | bytes 65560
  1.5 0.0 copy-start.2
  1.5 0.8 %copy-done.2 = f32[8,16,128]{2,1,0:T(8,128)S(1)} copy-done((f32[8,16,128]{2,1,0:T(8,128)S(1)}, f32[8,16,128]{2,1,0:T(8,128)}, u32[]{:S(2)}) %copy-start.2) | copy-done | bytes 65560
  2.3 0.0 copy-start.3
  2.3 0.8 %copy-done.3 = s32[8,16,128]{2,1,0:T(8,128)S(1)} copy-done((s32[8,16,128]{2,1,0:T(8,128)S(1)}, s32[8,16,128]{2,1,0:T(8,128)}, u32[]{:S(2)}) %copy-start.3) | copy-done | bytes 65560
  3.2 0.0 copy-start.4
  3.2 0.8 %copy-done.4 = s32[8,16,128]{2,1,0:T(8,128)S(1)} copy-done((s32[8,16,128]{2,1,0:T(8,128)S(1)}, s32[8,16,128]{2,1,0:T(8,128)}, u32[]{:S(2)}) %copy-start.4) | copy-done | bytes 65560
  4.0 0.0 copy-start.5
  4.0 0.7 copy-done.5
  4.6 0.0 copy-start.6
  4.7 0.6 shard_map.68
  5.3 3.9 %collective-permute-start = (f32[17,16,128]{2,1,0:T(8,128)S(1)}, f32[17,16,128]{2,1,0:T(8,128)S(1)}, u32[]{:S(2)}, u32[]{:S(2)}) collective-permute-start(f32[17,16,128]{2,1,0:T(8,128)S(1)} %get-tuple-element.12), channel_id=1, source_target_pairs={{0,128},{128,256},{256,384},{1,129},{129,257},{257,385},{2,130},{1... | collective-permute-start | bytes 417800 | tf_op jit(solution)/shard_map/ppermute | solution.py:346
  9.2 1.3 %collective-permute-start.1 = (f32[17,16,128]{2,1,0:T(8,128)S(1)}, f32[17,16,128]{2,1,0:T(8,128)S(1)}, u32[]{:S(2)}, u32[]{:S(2)}) collective-permute-start(f32[17,16,128]{2,1,0:T(8,128)S(1)} %get-tuple-element.13), channel_id=1, source_target_pairs={{128,0},{256,128},{384,256},{129,1},{257,129},{385,257},{130,2},{2... | collective-permute-start | bytes 417800 | tf_op jit(solution)/shard_map/ppermute | solution.py:347
  10.5 0.7 collective-permute-done.left
  11.2 3.8 %collective-permute-done.1.right = f32[17,16,128]{2,1,0:T(8,128)S(1)} collective-permute-done((f32[17,16,128]{2,1,0:T(8,128)S(1)}, f32[17,16,128]{2,1,0:T(8,128)S(1)}, u32[]{:S(2)}, u32[]{:S(2)}) %collective-permute-start.1) | collective-permute-done | bytes 139296 | tf_op jit(solution)/shard_map/ppermute | solution.py:347
  15.1 0.0 copy-start.1
  15.1 3.7 %collective-permute-start.2 = (f32[288,128]{1,0:T(8,128)S(1)}, f32[288,128]{1,0:T(8,128)S(1)}, u32[]{:S(2)}, u32[]{:S(2)}) collective-permute-start(f32[288,128]{1,0:T(8,128)S(1)} %get-tuple-element.14), channel_id=1, source_target_pairs={{0,16},{16,32},{32,48},{48,64},{64,80},{80,96},{96,112},{1,17},{17... | collective-permute-start | bytes 442376 | tf_op jit(solution)/shard_map/ppermute | solution.py:346
  18.8 1.3 %collective-permute-start.3 = (f32[288,128]{1,0:T(8,128)S(1)}, f32[288,128]{1,0:T(8,128)S(1)}, u32[]{:S(2)}, u32[]{:S(2)}) collective-permute-start(f32[288,128]{1,0:T(8,128)S(1)} %get-tuple-element.15), channel_id=1, source_target_pairs={{16,0},{32,16},{48,32},{64,48},{80,64},{96,80},{112,96},{17,1},{33... | collective-permute-start | bytes 442376 | tf_op jit(solution)/shard_map/ppermute | solution.py:347
  20.1 0.8 collective-permute-done.2.below
  20.9 3.8 %collective-permute-done.3.above = f32[288,128]{1,0:T(8,128)S(1)} collective-permute-done((f32[288,128]{1,0:T(8,128)S(1)}, f32[288,128]{1,0:T(8,128)S(1)}, u32[]{:S(2)}, u32[]{:S(2)}) %collective-permute-start.3) | collective-permute-done | bytes 147488 | tf_op jit(solution)/shard_map/ppermute | solution.py:347
  24.7 0.4 shard_map.70
  25.1 6.1 %collective-permute-start.5 = (f32[6,32,128]{2,1,0:T(8,128)S(1)}, f32[6,32,128]{2,1,0:T(8,128)S(1)}, u32[]{:S(2)}, u32[]{:S(2)}) collective-permute-start(f32[6,32,128]{2,1,0:T(8,128)S(1)} %get-tuple-element.17), channel_id=1, source_target_pairs={{1,0},{2,1},{3,2},{4,3},{5,4},{6,5},{7,6},{8,7},{9,8},{10,9},{11,1... | collective-permute-start | bytes 294920 | tf_op jit(solution)/shard_map/ppermute | solution.py:347
  31.2 2.9 %collective-permute-start.4 = (f32[6,32,128]{2,1,0:T(8,128)S(1)}, f32[6,32,128]{2,1,0:T(8,128)S(1)}, u32[]{:S(2)}, u32[]{:S(2)}) collective-permute-start(f32[6,32,128]{2,1,0:T(8,128)S(1)} %get-tuple-element.17), channel_id=1, source_target_pairs={{0,1},{1,2},{2,3},{3,4},{4,5},{5,6},{6,7},{7,8},{8,9},{9,10},{10,1... | collective-permute-start | bytes 294920 | tf_op jit(solution)/shard_map/ppermute | solution.py:346
  34.2 0.4 collective-permute-done.5.from_right
  34.5 1.3 %collective-permute-done.4.from_left = f32[6,32,128]{2,1,0:T(8,128)S(1)} collective-permute-done((f32[6,32,128]{2,1,0:T(8,128)S(1)}, f32[6,32,128]{2,1,0:T(8,128)S(1)}, u32[]{:S(2)}, u32[]{:S(2)}) %collective-permute-start.4) | collective-permute-done | bytes 98336 | tf_op jit(solution)/shard_map/ppermute | solution.py:346
  35.8 0.0 copy-done.6
  35.8 4.8 %shard_map.71 = (f32[5,8,16,128]{3,2,1,0:T(8,128)S(1)}, f32[8,1,128]{2,1,0:T(1,128)S(1)}) custom-call(f32[4,18,32,128]{3,2,1,0:T(8,128)S(1)} %get-tuple-element.16.wide, f32[6,32,128]{2,1,0:T(8,128)S(1)} %collective-permute-done.4.from_left, f32[6,32,128]{2,1,0:T(8,128)S(1)} %collective-permute-done.5.from_right, f32[16]{0:T(128)S(1)} %copy-done.6), custom_call_target="tpu_custom_call" | custom-call | flops 20000000 | bytes 1000000 | tf_op jit(solution)/shard_map/pallas_call | solution.py:369
  40.6 8.5 %all_to_all.10.parts = f32[8,1,128]{2,1,0:T(1,128)S(1)} all-to-all(f32[8,1,128]{2,1,0:T(1,128)S(1)} %get-tuple-element.18), channel_id=1, replica_groups=mesh['gx'=4,'gy'=8,'gz_0'=8,'gz_1'=2] {'gx','gz_1'}, dimensions={0} | all-to-all | bytes 8192 | tf_op jit(solution)/shard_map/all_to_all | solution.py:352
  49.2 28.7 %all_to_all.11.parts = f32[64,1,128]{2,1,0:T(1,128)S(1)} all-to-all(f32[64,1,128]{2,1,0:T(1,128)S(1)} %shard_map.72), channel_id=1, replica_groups=mesh['gx'=4,'gy'=8,'gz_0'=8,'gz_1'=2] {'gy','gz_0'}, dimensions={0} | all-to-all | bytes 65536 | tf_op jit(solution)/shard_map/all_to_all | solution.py:352
  77.8 0.0 copy-done.1
  77.8 2.0 %shard_map.73 = (f32[8,16,128]{2,1,0:T(8,128)}, f32[8,16,128]{2,1,0:T(8,128)}) custom-call(f32[64,1,128]{2,1,0:T(1,128)S(1)} %all_to_all.11.parts, f32[5,8,16,128]{3,2,1,0:T(8,128)S(1)} %get-tuple-element.19.basis, f32[8,16,128]{2,1,0:T(8,128)S(1)} %copy-done.1, f32[16]{0:T(128)S(1)} %copy-done.6), custom_call_target="tpu_custom_call" | custom-call | flops 100000 | bytes 1000000 | tf_op jit(solution)/shard_map/pallas_call | solution.py:380
  (2 shorter events, 0.1 us)
Async XLA Ops:
  0.6 0.8 %copy-start = (f32[8,16,128]{2,1,0:T(8,128)S(1)}, f32[8,16,128]{2,1,0:T(8,128)}, u32[]{:S(2)}) copy-start(f32[8,16,128]{2,1,0:T(8,128)} %opening.3) | copy-start | bytes 196612
  1.5 0.8 %copy-start.2 = (f32[8,16,128]{2,1,0:T(8,128)S(1)}, f32[8,16,128]{2,1,0:T(8,128)}, u32[]{:S(2)}) copy-start(f32[8,16,128]{2,1,0:T(8,128)} %source.1) | copy-start | bytes 196612
  2.3 0.8 %copy-start.3 = (s32[8,16,128]{2,1,0:T(8,128)S(1)}, s32[8,16,128]{2,1,0:T(8,128)}, u32[]{:S(2)}) copy-start(s32[8,16,128]{2,1,0:T(8,128)} %category.1) | copy-start | bytes 196612
  3.2 0.8 %copy-start.4 = (s32[8,16,128]{2,1,0:T(8,128)S(1)}, s32[8,16,128]{2,1,0:T(8,128)}, u32[]{:S(2)}) copy-start(s32[8,16,128]{2,1,0:T(8,128)} %flags.1) | copy-start | bytes 196612
  4.0 0.7 copy-start.5
  4.6 31.1 %copy-start.6 = (f32[16]{0:T(128)S(1)}, f32[16]{0:T(128)}, u32[]{:S(2)}) copy-start(f32[16]{0:T(128)} %table.5) | copy-start | bytes 196
  5.3 5.9 %collective-permute-start = (f32[17,16,128]{2,1,0:T(8,128)S(1)}, f32[17,16,128]{2,1,0:T(8,128)S(1)}, u32[]{:S(2)}, u32[]{:S(2)}) collective-permute-start(f32[17,16,128]{2,1,0:T(8,128)S(1)} %get-tuple-element.12), channel_id=1, source_target_pairs={{0,128},{128,256},{256,384},{1,129},{129,257},{257,385},{2,130},{1... | collective-permute-start | bytes 417800 | tf_op jit(solution)/shard_map/ppermute | solution.py:346
  9.2 5.8 %collective-permute-start.1 = (f32[17,16,128]{2,1,0:T(8,128)S(1)}, f32[17,16,128]{2,1,0:T(8,128)S(1)}, u32[]{:S(2)}, u32[]{:S(2)}) collective-permute-start(f32[17,16,128]{2,1,0:T(8,128)S(1)} %get-tuple-element.13), channel_id=1, source_target_pairs={{128,0},{256,128},{384,256},{129,1},{257,129},{385,257},{130,2},{2... | collective-permute-start | bytes 417800 | tf_op jit(solution)/shard_map/ppermute | solution.py:347
  15.1 62.8 %copy-start.1 = (f32[8,16,128]{2,1,0:T(8,128)S(1)}, f32[8,16,128]{2,1,0:T(8,128)}, u32[]{:S(2)}) copy-start(f32[8,16,128]{2,1,0:T(8,128)} %opening.3) | copy-start | bytes 196612
  15.1 5.8 %collective-permute-start.2 = (f32[288,128]{1,0:T(8,128)S(1)}, f32[288,128]{1,0:T(8,128)S(1)}, u32[]{:S(2)}, u32[]{:S(2)}) collective-permute-start(f32[288,128]{1,0:T(8,128)S(1)} %get-tuple-element.14), channel_id=1, source_target_pairs={{0,16},{16,32},{32,48},{48,64},{64,80},{80,96},{96,112},{1,17},{17... | collective-permute-start | bytes 442376 | tf_op jit(solution)/shard_map/ppermute | solution.py:346
  18.8 5.9 %collective-permute-start.3 = (f32[288,128]{1,0:T(8,128)S(1)}, f32[288,128]{1,0:T(8,128)S(1)}, u32[]{:S(2)}, u32[]{:S(2)}) collective-permute-start(f32[288,128]{1,0:T(8,128)S(1)} %get-tuple-element.15), channel_id=1, source_target_pairs={{16,0},{32,16},{48,32},{64,48},{80,64},{96,80},{112,96},{17,1},{33... | collective-permute-start | bytes 442376 | tf_op jit(solution)/shard_map/ppermute | solution.py:347
  25.1 9.4 %collective-permute-start.5 = (f32[6,32,128]{2,1,0:T(8,128)S(1)}, f32[6,32,128]{2,1,0:T(8,128)S(1)}, u32[]{:S(2)}, u32[]{:S(2)}) collective-permute-start(f32[6,32,128]{2,1,0:T(8,128)S(1)} %get-tuple-element.17), channel_id=1, source_target_pairs={{1,0},{2,1},{3,2},{4,3},{5,4},{6,5},{7,6},{8,7},{9,8},{10,9},{11,1... | collective-permute-start | bytes 294920 | tf_op jit(solution)/shard_map/ppermute | solution.py:347
  31.2 4.6 %collective-permute-start.4 = (f32[6,32,128]{2,1,0:T(8,128)S(1)}, f32[6,32,128]{2,1,0:T(8,128)S(1)}, u32[]{:S(2)}, u32[]{:S(2)}) collective-permute-start(f32[6,32,128]{2,1,0:T(8,128)S(1)} %get-tuple-element.17), channel_id=1, source_target_pairs={{0,1},{1,2},{2,3},{3,4},{4,5},{5,6},{6,7},{7,8},{8,9},{9,10},{10,1... | collective-permute-start | bytes 294920 | tf_op jit(solution)/shard_map/ppermute | solution.py:346

commit v3 on v2

--- a/solution.py
+++ b/solution.py
@@ -24,6 +24,7 @@
 SCALE = 64.0
 PAIRS = [(i, j) for i in range(ITERS) for j in range(i, ITERS + 1)]
 VMEM = pl.BlockSpec(memory_space=pltpu.VMEM)
+HBM = pl.BlockSpec(memory_space=pltpu.HBM)
 SMEM = pl.BlockSpec(memory_space=pltpu.SMEM)
 
 
@@ -37,13 +38,34 @@
         in_specs=ins,
         out_specs=[VMEM] * len(outs),
         out_shape=[jax.ShapeDtypeStruct(s, F32) for s in outs],
-        scratch_shapes=[pltpu.VMEM(s, F32) for s in scratch],
+        scratch_shapes=[pltpu.VMEM(s, F32) if isinstance(s, tuple) else s for s in scratch],
         compiler_params=pltpu.CompilerParams(vmem_limit_bytes=vmem * 2**20),
         cost_estimate=pl.CostEstimate(flops=flops, bytes_accessed=1000000, transcendentals=0),
     )
 
 
-def prepare(opening, source, category, flags, table, fields, low, high):
+def prepare(
+    opening_at, source_at, category_at, flags_at, table_at, fields, low, high, theta,
+    opening, source, category, flags, table, arrived,
+):
+    copies = [
+        pltpu.make_async_copy(a, b, arrived.at[n])
+        for n, (a, b) in enumerate(
+            (
+                (table_at, table),
+                (category_at, category),
+                (flags_at, flags),
+                (opening_at, opening),
+                (source_at, source),
+            )
+        )
+    ]
+    for copy in copies:
+        copy.start()
+    for copy in copies:
+        copy.wait()
+    for k, shift in enumerate(shifts_of(table)):
+        theta[k] = shift
     for p in range(X):
         kind = category[p]
         cond = jnp.full((Y, Z), table[0], F32)
@@ -114,8 +136,10 @@
     ]
 
 
-def krylov(wide, from_left, from_right, table, basis, dots, ends, fore, fore_c, back, back_c, diag, mid):
+def krylov(core, wide, far, chip, theta, basis, dots, ends, fore, fore_c, back, back_c, diag, mid):
     lane = lax.broadcasted_iota(jnp.int32, (ROWS, Z), 1)
+    first_core = core[0] == 0
+    partner = 1 - core[0]
 
     for q in range(PER_GROUP):
         left = lane < 0
@@ -123,7 +147,8 @@
             for k, w in enumerate(WIDTHS):
                 base = STRIDE * g + BASES[k]
                 left = left | ((lane >= base - w) & (lane < base))
-        both = jnp.where(left, from_left[q], from_right[q])
+        other, near = far[q], chip[partner, q]
+        both = jnp.where(jnp.logical_xor(left, first_core), near, other)
         for g in range(GROUPS):
             p = PER_GROUP * g + q
             for k, w in enumerate(WIDTHS):
@@ -176,7 +201,6 @@
             if side == 0 and HALO <= p < HALO + X:
                 basis[0, p - HALO] = r[TOP : TOP + Y]
 
-    theta = shifts_of(table)
     for k in range(ITERS):
         old, old_c, new, new_c = (
             (fore, fore_c, back, back_c) if k % 2 == 0 else (back, back_c, fore, fore_c)
@@ -320,7 +344,7 @@
     return [a[0] * (1.0 / SCALE) for a in y], [a[0] for a in r]
 
 
-def finish(parts, basis, opening, table, closing, mismatch):
+def finish(parts, basis, fields, theta, closing, mismatch):
     total, rest = row_sum(parts)
     rest = rest + pltpu.roll(total, Z - 4, 1)
     gram = {}
@@ -329,12 +353,12 @@
         gram[i, j] = gram[j, i] = quick(
             *(jnp.broadcast_to(v[0:1, at : at + 1], (8, Z)) for v in (total, rest))
         )
-    y, r = conjugate_gradients(gram, shifts_of(table))
+    y, r = conjugate_gradients(gram, [theta[k] for k in range(ITERS)])
     for p in range(X):
         for half in (0, 8):
             rows = pl.ds(half, 8)
             v = [basis[k, p, rows] for k in range(ITERS + 1)]
-            x, m = opening[p, rows], r[ITERS] * v[ITERS]
+            x, m = fields[1, p, rows], r[ITERS] * v[ITERS]
             for k in range(ITERS):
                 x, m = x + y[k] * v[k], m + r[k] * v[k]
             closing[p, rows] = x
@@ -354,31 +378,41 @@
 
 def body(opening, source, category, table, flags):
     brick = (X, Y, Z)
-    fields, low, high = call(
-        prepare, [VMEM] * 4 + [SMEM], [(4, *brick), (SLAB_X, Y, Z), (SLAB_X, Y, Z)]
-    )(opening, source, category, flags, table)
+    whole = pltpu.VMEM(brick, jnp.int32)
+    fields, low, high, theta = call(
+        prepare,
+        [HBM] * 5,
+        [(4, *brick), (SLAB_X, Y, Z), (SLAB_X, Y, Z), (ITERS, 8, Z)],
+        [brick, brick, whole, whole, pltpu.SMEM(table.shape, F32), pltpu.SemaphoreType.DMA((5,))],
+    )(*(pltpu.with_memory_space_constraint(a, pltpu.HBM) for a in (opening, source, category, flags, table)))
     left, right = both_ways(low, high, "gx")
     low, high = call(slabs_y, [VMEM] * 3, [(SLAB_Y, Z)] * 2)(fields, left, right)
     below, above = both_ways(low, high, "gy")
     wide, packed = call(
         assemble, [VMEM] * 5, [(4, PLANES, ROWS, Z), (PER_GROUP, ROWS, Z)]
     )(fields, left, right, below, above)
-    from_left, from_right = both_ways(packed, packed, GZ)
+    far = lax.ppermute(
+        packed,
+        GZ,
+        [p for i in range(1, lax.axis_size(GZ) - 1, 2) for p in ((i, i + 1), (i + 1, i))],
+    )
+    chip = lax.all_gather(packed, GZ[1], axis=0)
+    core = lax.axis_index(GZ[1]).reshape(1)
     first, second = ("gx", "gz_1"), ("gy", "gz_0")
     sided = (2, PLANES, ROWS, Z)
     basis, dots = call(
         krylov,
-        [VMEM] * 3 + [SMEM],
+        [SMEM] + [VMEM] * 4,
         [(ITERS + 1, *brick), (lax.axis_size(first), 1, Z)],
         [(4, PLANES, ROWS, Z)] + [sided] * 5 + [(6, 2, ROWS + 16, Z)],
         flops=20000000,
         vmem=16,
-    )(wide, from_left, from_right, table)
+    )(core, wide, far, chip, theta)
     parts = exchange(dots, first)
     (copies,) = call(relay, [VMEM], [(lax.axis_size(second), 1, Z)])(parts)
     parts = exchange(copies, second)
-    closing, mismatch = call(finish, [VMEM] * 3 + [SMEM], [brick, brick])(
-        parts, basis, opening, table
+    closing, mismatch = call(finish, [VMEM] * 4, [brick, brick])(
+        parts, basis, fields, theta
     )
     return closing, mismatch
 

time: 80.4 us -> 73.3 us (0.912)
  local copies, waits for them, and re-layouts: 4.02 us -> 0 us
  starting transfers between devices: 19.3 us -> 17.2 us
  blocking collectives: 37.2 us -> 38.5 us
  waiting for transfers between devices: 10.7 us -> 9.42 us
  Pallas kernels: 7.96 us -> 7.15 us
    ppermute x0 -> x1, starting transfers between devices: none -> 7.13 us  [body(): lax.ppermute(packed, GZ, [p for i in range(1, lax.axis_size(GZ) - 1, 2) f...]
    ppermute x3 -> x2, starting transfers between devices: 8.7 us -> 2.58 us  [both_ways(): from_above = lax.ppermute(low, axis, [(i + 1, i) for i in range(ends)])]
    unnamed x14 -> x0, local copies, waits for them, and re-layouts: 4.02 us -> none
    ppermute x3 -> x2, starting transfers between devices: 10.6 us -> 7.52 us  [both_ways(): from_below = lax.ppermute(high, axis, [(i, i + 1) for i in range(ends)])]
    all_gather x0 -> x1, blocking collectives: none -> 1.95 us  [body(): chip = lax.all_gather(packed, GZ[1], axis=0)]
    ppermute x3 -> x2, waiting for transfers between devices: 2.73 us -> 1.47 us  [both_ways(): from_below = lax.ppermute(high, axis, [(i, i + 1) for i in range(ends)])]
    ppermute x3 -> x2, waiting for transfers between devices: 7.97 us -> 7.61 us  [both_ways(): from_above = lax.ppermute(low, axis, [(i + 1, i) for i in range(ends)])]
  transfers between devices with their start and end apart: 6 -> 5, of which waited for: 6 -> 5; matrix products, arithmetic and copies ran while one was open for 0% -> 0% of each run, Pallas kernels for 0% -> 0%
where the time goes in v3:
time: 73.3 us; the launch traced here: 73 us
  blocking collectives  38.5 us (53%)
  starting transfers between devices  17.2 us (23%)
  waiting for transfers between devices  9.42 us (13%)
  Pallas kernels  7.15 us (10%)
    all_to_all x2, blocking collectives, exchange(): return lax.all_to_all(copies, axes, split_axis=0, concat_axis=0, tiled=True)  36.5 us
    ppermute x2, waiting for transfers between devices, both_ways(): from_above = lax.ppermute(low, axis, [(i + 1, i) for i in range(ends)])  7.61 us
    ppermute x2, starting transfers between devices, both_ways(): from_below = lax.ppermute(high, axis, [(i, i + 1) for i in range(ends)])  7.52 us
    ppermute x1, starting transfers between devices, body(): lax.ppermute(packed, GZ, [p for i in range(1, lax.axis_size(GZ) - 1, 2) f...  7.13 us
    pallas_call x1, Pallas kernels, body(): call(krylov, [SMEM] + [VMEM] * 4, [(ITERS + 1, *brick), (lax.axis_size(fi...  4.11 us
    ppermute x2, starting transfers between devices, both_ways(): from_above = lax.ppermute(low, axis, [(i + 1, i) for i in range(ends)])  2.58 us
    all_gather x1, blocking collectives, body(): chip = lax.all_gather(packed, GZ[1], axis=0)  1.95 us
    pallas_call x1, Pallas kernels, body(): call(finish, [VMEM] * 4, [brick, brick])(parts, basis, fields, theta)  1.51 us
  transfers between devices with their start and end apart: 5, of which 5 were waited for; matrix products, arithmetic and copies ran while one was open for 0% of the time, Pallas kernels for 0%

profile of v3, /device:TPU:1, one launch (start us, length us, event | category | flops | bytes accessed | tf_op | source)
XLA Modules:
  0.0 73.0 jit_solution(18224817504591565149)
XLA Ops:
  0.6 1.1 %shard_map.68 = (f32[4,8,16,128]{3,2,1,0:T(8,128)S(1)}, f32[17,16,128]{2,1,0:T(8,128)S(1)}, f32[17,16,128]{2,1,0:T(8,128)S(1)}, f32[4,8,128]{2,1,0:T(8,128)S(1)}) custom-call(f32[8,16,128]{2,1,0:T(8,128)} %opening_at.1, f32[8,16,128]{2,1,0:T(8,128)} %source_at.1, s32[8,16,128]{2,1,0:T(8,128)} %category_at.1, s32[8,16,128]{2,1,0:T(8,128)} %flags_at.1, f32[16]{0:T(128)} %table_at.1), custom_call_target="tpu_custom_call" | custom-call | flops 100000 | bytes 1000000 | tf_op jit(solution)/shard_map/pallas_call | solution.py:382
  1.7 3.9 %collective-permute-start = (f32[17,16,128]{2,1,0:T(8,128)S(1)}, f32[17,16,128]{2,1,0:T(8,128)S(1)}, u32[]{:S(2)}, u32[]{:S(2)}) collective-permute-start(f32[17,16,128]{2,1,0:T(8,128)S(1)} %get-tuple-element.13), channel_id=1, source_target_pairs={{0,128},{128,256},{256,384},{1,129},{129,257},{257,385},{2,130},{1... | collective-permute-start | bytes 417800 | tf_op jit(solution)/shard_map/ppermute | solution.py:370
  5.7 1.3 %collective-permute-start.1 = (f32[17,16,128]{2,1,0:T(8,128)S(1)}, f32[17,16,128]{2,1,0:T(8,128)S(1)}, u32[]{:S(2)}, u32[]{:S(2)}) collective-permute-start(f32[17,16,128]{2,1,0:T(8,128)S(1)} %get-tuple-element.14), channel_id=1, source_target_pairs={{128,0},{256,128},{384,256},{129,1},{257,129},{385,257},{130,2},{2... | collective-permute-start | bytes 417800 | tf_op jit(solution)/shard_map/ppermute | solution.py:371
  7.0 0.7 collective-permute-done.left
  7.7 3.8 %collective-permute-done.1.right = f32[17,16,128]{2,1,0:T(8,128)S(1)} collective-permute-done((f32[17,16,128]{2,1,0:T(8,128)S(1)}, f32[17,16,128]{2,1,0:T(8,128)S(1)}, u32[]{:S(2)}, u32[]{:S(2)}) %collective-permute-start.1) | collective-permute-done | bytes 139296 | tf_op jit(solution)/shard_map/ppermute | solution.py:371
  11.5 3.6 %collective-permute-start.2 = (f32[288,128]{1,0:T(8,128)S(1)}, f32[288,128]{1,0:T(8,128)S(1)}, u32[]{:S(2)}, u32[]{:S(2)}) collective-permute-start(f32[288,128]{1,0:T(8,128)S(1)} %get-tuple-element.15), channel_id=1, source_target_pairs={{0,16},{16,32},{32,48},{48,64},{64,80},{80,96},{96,112},{1,17},{17... | collective-permute-start | bytes 442376 | tf_op jit(solution)/shard_map/ppermute | solution.py:370
  15.1 1.3 %collective-permute-start.3 = (f32[288,128]{1,0:T(8,128)S(1)}, f32[288,128]{1,0:T(8,128)S(1)}, u32[]{:S(2)}, u32[]{:S(2)}) collective-permute-start(f32[288,128]{1,0:T(8,128)S(1)} %get-tuple-element.16), channel_id=1, source_target_pairs={{16,0},{32,16},{48,32},{64,48},{80,64},{96,80},{112,96},{17,1},{33... | collective-permute-start | bytes 442376 | tf_op jit(solution)/shard_map/ppermute | solution.py:371
  16.4 0.8 %collective-permute-done.2.below = f32[288,128]{1,0:T(8,128)S(1)} collective-permute-done((f32[288,128]{1,0:T(8,128)S(1)}, f32[288,128]{1,0:T(8,128)S(1)}, u32[]{:S(2)}, u32[]{:S(2)}) %collective-permute-start.2) | collective-permute-done | bytes 147488 | tf_op jit(solution)/shard_map/ppermute | solution.py:370
  17.2 3.8 %collective-permute-done.3.above = f32[288,128]{1,0:T(8,128)S(1)} collective-permute-done((f32[288,128]{1,0:T(8,128)S(1)}, f32[288,128]{1,0:T(8,128)S(1)}, u32[]{:S(2)}, u32[]{:S(2)}) %collective-permute-start.3) | collective-permute-done | bytes 147488 | tf_op jit(solution)/shard_map/ppermute | solution.py:371
  21.0 0.4 shard_map.70
  21.4 7.1 %collective-permute-start.4 = (f32[6,32,128]{2,1,0:T(8,128)S(1)}, f32[6,32,128]{2,1,0:T(8,128)S(1)}, u32[]{:S(2)}, u32[]{:S(2)}) collective-permute-start(f32[6,32,128]{2,1,0:T(8,128)S(1)} %get-tuple-element.18), channel_id=1, source_target_pairs={{1,2},{2,1},{3,4},{4,3},{5,6},{6,5},{7,8},{8,7},{9,10},{10,9},{11,... | collective-permute-start | bytes 294920 | tf_op jit(solution)/shard_map/ppermute | solution.py:394
  28.5 1.9 %all-gather = f32[12,32,128]{2,1,0:T(8,128)S(1)} all-gather(f32[6,32,128]{2,1,0:T(8,128)S(1)} %get-tuple-element.18), channel_id=2, replica_groups=mesh['gx'=4,'gy'=8,'gz_0'=8,'gz_1'=2] {'gz_1'}, dimensions={0}, use_global_device_ids=true | all-gather | bytes 294912 | tf_op jit(solution)/shard_map/all_gather | solution.py:399
  30.5 0.3 collective-permute-done.4.far
  30.8 4.1 %shard_map.71 = (f32[5,8,16,128]{3,2,1,0:T(8,128)S(1)}, f32[8,1,128]{2,1,0:T(1,128)S(1)}) custom-call(s32[1]{0:T(128)} %bitcast.core, f32[4,18,32,128]{3,2,1,0:T(8,128)S(1)} %get-tuple-element.17.wide, f32[6,32,128]{2,1,0:T(8,128)S(1)} %collective-permute-done.4.far, f32[2,6,32,128]{3,2,1,0:T(8,128)S(1)} %bitcast.2, f32[4,8,128]{2,1,0:T(8,128)S(1)} %get-tuple-element.19.theta), custom_call_target="tpu_custom_call" | custom-call | flops 20000000 | bytes 1000000 | tf_op jit(solution)/shard_map/pallas_call | solution.py:403
  34.9 8.5 %all_to_all.10.parts = f32[8,1,128]{2,1,0:T(1,128)S(1)} all-to-all(f32[8,1,128]{2,1,0:T(1,128)S(1)} %get-tuple-element.20), channel_id=1, replica_groups=mesh['gx'=4,'gy'=8,'gz_0'=8,'gz_1'=2] {'gx','gz_1'}, dimensions={0} | all-to-all | bytes 8192 | tf_op jit(solution)/shard_map/all_to_all | solution.py:376
  43.5 28.0 %all_to_all.11.parts = f32[64,1,128]{2,1,0:T(1,128)S(1)} all-to-all(f32[64,1,128]{2,1,0:T(1,128)S(1)} %shard_map.72), channel_id=1, replica_groups=mesh['gx'=4,'gy'=8,'gz_0'=8,'gz_1'=2] {'gy','gz_0'}, dimensions={0} | all-to-all | bytes 65536 | tf_op jit(solution)/shard_map/all_to_all | solution.py:376
  71.5 1.5 %shard_map.73 = (f32[8,16,128]{2,1,0:T(8,128)}, f32[8,16,128]{2,1,0:T(8,128)}) custom-call(f32[64,1,128]{2,1,0:T(1,128)S(1)} %all_to_all.11.parts, f32[5,8,16,128]{3,2,1,0:T(8,128)S(1)} %get-tuple-element.21.basis, f32[4,8,16,128]{3,2,1,0:T(8,128)S(1)} %get-tuple-element.12.fields, f32[4,8,128]{2,1,0:T(8,128)S(1)} %get-tuple-element.19.theta), custom_call_target="tpu_custom_call" | custom-call | flops 100000 | bytes 1000000 | tf_op jit(solution)/shard_map/pallas_call | solution.py:414
  (2 shorter events, 0.1 us)
Async XLA Ops:
  1.7 5.9 %collective-permute-start = (f32[17,16,128]{2,1,0:T(8,128)S(1)}, f32[17,16,128]{2,1,0:T(8,128)S(1)}, u32[]{:S(2)}, u32[]{:S(2)}) collective-permute-start(f32[17,16,128]{2,1,0:T(8,128)S(1)} %get-tuple-element.13), channel_id=1, source_target_pairs={{0,128},{128,256},{256,384},{1,129},{129,257},{257,385},{2,130},{1... | collective-permute-start | bytes 417800 | tf_op jit(solution)/shard_map/ppermute | solution.py:370
  5.7 5.8 %collective-permute-start.1 = (f32[17,16,128]{2,1,0:T(8,128)S(1)}, f32[17,16,128]{2,1,0:T(8,128)S(1)}, u32[]{:S(2)}, u32[]{:S(2)}) collective-permute-start(f32[17,16,128]{2,1,0:T(8,128)S(1)} %get-tuple-element.14), channel_id=1, source_target_pairs={{128,0},{256,128},{384,256},{129,1},{257,129},{385,257},{130,2},{2... | collective-permute-start | bytes 417800 | tf_op jit(solution)/shard_map/ppermute | solution.py:371
  11.5 5.7 %collective-permute-start.2 = (f32[288,128]{1,0:T(8,128)S(1)}, f32[288,128]{1,0:T(8,128)S(1)}, u32[]{:S(2)}, u32[]{:S(2)}) collective-permute-start(f32[288,128]{1,0:T(8,128)S(1)} %get-tuple-element.15), channel_id=1, source_target_pairs={{0,16},{16,32},{32,48},{48,64},{64,80},{80,96},{96,112},{1,17},{17... | collective-permute-start | bytes 442376 | tf_op jit(solution)/shard_map/ppermute | solution.py:370
  15.1 5.9 %collective-permute-start.3 = (f32[288,128]{1,0:T(8,128)S(1)}, f32[288,128]{1,0:T(8,128)S(1)}, u32[]{:S(2)}, u32[]{:S(2)}) collective-permute-start(f32[288,128]{1,0:T(8,128)S(1)} %get-tuple-element.16), channel_id=1, source_target_pairs={{16,0},{32,16},{48,32},{64,48},{80,64},{96,80},{112,96},{17,1},{33... | collective-permute-start | bytes 442376 | tf_op jit(solution)/shard_map/ppermute | solution.py:371
  21.4 9.4 %collective-permute-start.4 = (f32[6,32,128]{2,1,0:T(8,128)S(1)}, f32[6,32,128]{2,1,0:T(8,128)S(1)}, u32[]{:S(2)}, u32[]{:S(2)}) collective-permute-start(f32[6,32,128]{2,1,0:T(8,128)S(1)} %get-tuple-element.18), channel_id=1, source_target_pairs={{1,2},{2,1},{3,4},{4,3},{5,6},{6,5},{7,8},{8,7},{9,10},{10,9},{11,... | collective-permute-start | bytes 294920 | tf_op jit(solution)/shard_map/ppermute | solution.py:394

commit v4 on v3

v4 whole, which is shorter than its diff:
```python
import jax
import jax.numpy as jnp
from jax import lax
from jax.experimental import pallas as pl
from jax.experimental.pallas import tpu as pltpu
from jax.sharding import Mesh
from jax.sharding import PartitionSpec as P

ITERS = 4
GZ = ("gz_0", "gz_1")
F32 = jnp.float32
X, Y, Z = 8, 16, 128
HALO = ITERS + 1
WIDTHS = (5, 5, 4, 3)
PLANES = X + 2 * HALO
ROWS = 32
TOP = 8
SLAB_X = sum(WIDTHS)
AT_X = (0, 5, 10, 14)
AT_Y = (0, 90, 180, 244)
SLAB_Y = 288
GROUPS, PER_GROUP, GROUP = 4, 5, 32
LOW_AT, HIGH_AT = 5, 26
SCALE = 64.0
PAIRS = [(i, j) for i in range(ITERS) for j in range(i, ITERS + 1)]
VMEM = pl.BlockSpec(memory_space=pltpu.VMEM)
HBM = pl.BlockSpec(memory_space=pltpu.HBM)
SMEM = pl.BlockSpec(memory_space=pltpu.SMEM)


def planes_of(k):
    return range(HALO - WIDTHS[k], PLANES - HALO + WIDTHS[k])


def call(kernel, ins, outs, scratch=(), flops=100000, vmem=8):
    return pl.pallas_call(
        kernel,
        in_specs=ins,
        out_specs=[VMEM] * len(outs),
        out_shape=[jax.ShapeDtypeStruct(s, F32) for s in outs],
        scratch_shapes=[pltpu.VMEM(s, F32) if isinstance(s, tuple) else s for s in scratch],
        compiler_params=pltpu.CompilerParams(vmem_limit_bytes=vmem * 2**20),
        cost_estimate=pl.CostEstimate(flops=flops, bytes_accessed=1000000, transcendentals=0),
    )


def prepare(
    opening_at, source_at, category_at, flags_at, table_at, fields, low, high, theta,
    opening, source, category, flags, table, arrived,
):
    copies = [
        pltpu.make_async_copy(a, b, arrived.at[n])
        for n, (a, b) in enumerate(
            (
                (table_at, table),
                (category_at, category),
                (flags_at, flags),
                (opening_at, opening),
                (source_at, source),
            )
        )
    ]
    for copy in copies:
        copy.start()
    for copy in copies:
        copy.wait()
    for k, shift in enumerate(shifts_of(table)):
        theta[k] = shift
    for p in range(X):
        kind = category[p]
        cond = jnp.full((Y, Z), table[0], F32)
        for n in range(1, table.shape[0]):
            cond = jnp.where(kind == n, table[n], cond)
        flag = flags[p].astype(F32)
        start = opening[p]
        values = (cond, start, 2.0 * source[p] - 6.0 * flag * start, flag)
        for k, v in enumerate(values):
            fields[k, p] = v
            if p < WIDTHS[k]:
                low[AT_X[k] + p] = v
            if p >= X - WIDTHS[k]:
                high[AT_X[k] + p - (X - WIDTHS[k])] = v


def plane(fields, left, right, k, p):
    if p < HALO:
        return left, (AT_X[k] + p - (HALO - WIDTHS[k]),)
    if p < HALO + X:
        return fields, (k, p - HALO)
    return right, (AT_X[k] + p - HALO - X,)


def slabs_y(fields, left, right, low, high):
    for k, w in enumerate(WIDTHS):
        for n, p in enumerate(planes_of(k)):
            ref, at = plane(fields, left, right, k, p)
            to = pl.ds(AT_Y[k] + w * n, w)
            low[to] = ref[(*at, pl.ds(0, w))]
            high[to] = ref[(*at, pl.ds(Y - w, w))]


def assemble(core, fields, left, right, below, above, wide, near, far):
    lane = lax.broadcasted_iota(jnp.int32, (ROWS, Z), 1)
    first_core = core[0] == 0
    nothing = jnp.zeros((8, Z), F32)
    for k, w in enumerate(WIDTHS):
        for n, p in enumerate(planes_of(k)):
            ref, at = plane(fields, left, right, k, p)
            wide[k, p, 0:TOP] = nothing
            wide[k, p, TOP + Y : ROWS] = nothing
            wide[k, p, TOP : TOP + Y] = ref[at]
            wide[k, p, TOP - w : TOP] = below[AT_Y[k] + w * n : AT_Y[k] + w * (n + 1)]
            wide[k, p, TOP + Y : TOP + Y + w] = above[AT_Y[k] + w * n : AT_Y[k] + w * (n + 1)]
    for q in range(PER_GROUP):
        low = jnp.zeros((ROWS, Z), F32)
        high = low
        for g in range(GROUPS):
            p = PER_GROUP * g + q
            for k, w in enumerate(WIDTHS):
                if p in planes_of(k):
                    base = GROUP * g + AT_X[k]
                    turned = pltpu.roll(wide[k, p], base, 1)
                    place = lane if base else jnp.where(lane < Z // 2, lane, lane - Z)
                    low = jnp.where((place >= base) & (place < base + w), turned, low)
                    high = jnp.where((place >= base - w) & (place < base), turned, high)
        far[q] = jnp.where(first_core, low, high)
        near[q] = jnp.where(first_core, high, low)


def shifts_of(table):
    values = [jnp.full((8, Z), table[n], F32) for n in range(table.shape[0])]
    least, most, mean = values[0], values[0], values[0]
    for v in values[1:]:
        least, most, mean = jnp.minimum(least, v), jnp.maximum(most, v), mean + v
    mean = mean * (1.0 / len(values))
    top = 4.0 + 16.0 * most + 16.0 * mean
    low = 2.0 + 8.0 * least + 8.0 * mean
    middle, half = 0.5 * (top + low), 0.5 * (top - low)
    return [
        (middle + half * c) * (1.0 / SCALE) for c in (0.9238795, -0.9238795, 0.3826834, -0.3826834)
    ]


def smooth_y(mid, first, count):
    sides = mid[pl.ds(7 + first, count)] + mid[pl.ds(9 + first, count)]
    return mid[pl.ds(8 + first, count)] + 0.5 * sides


def smooth_z(values):
    pairs = values + pltpu.roll(values, Z - 1, 1)
    return pairs + pltpu.roll(pairs, 1, 1)


def newton_step(store, shift, at, v, tv, tu):
    slope, diag, inside = store
    return ((diag[at] - shift) * v - (slope[at] * tv + tu)) * inside[at]


def interior(wide, theta, basis, sums, ends, cx, mid, slope, diag, inside, va, vb, ua, ub):
    lane = lax.broadcasted_iota(jnp.int32, (ROWS, Z), 1)
    slots = mid.shape[0]
    slot = [0]

    def smooth(ref, p, first=0, count=ROWS):
        here = mid.at[slot[0] % slots]
        slot[0] += 1
        middle = ref[p]
        here[pl.ds(8, ROWS)] = (ref[p - 1] + middle) + (middle + ref[p + 1])
        return smooth_z(smooth_y(here, first, count))

    cond, start, rest, flag = (wide.at[k] for k in range(4))
    for p in range(PLANES):
        cx[p] = cond[p] * start[p]
    for p in range(1, PLANES - 1):
        tc, tx, tcx = (smooth(ref, p) for ref in (cond, start, cx))
        c = cond[p]
        near = 16.0 * c + 0.5 * tc
        if p in planes_of(3):
            diag[p] = (1.0 + 6.0 * flag[p] + near) * (1.0 / SCALE)
        slope[p] = c * (0.5 / SCALE)
        inside[p] = jnp.where(c > 0.0, 1.0, 0.0)
        r = (rest[p] - near * start[p] + 0.5 * (c * tx + tcx)) * inside[p]
        va[p] = r
        ua[p] = r * slope[p]
        if HALO <= p < HALO + X:
            basis[0, p - HALO] = r[TOP : TOP + Y]
    for k in range(ITERS):
        v_old, u_old, v_new, u_new = (va, ua, vb, ub) if k % 2 == 0 else (vb, ub, va, ua)
        last = k + 1 == ITERS
        first, count = (TOP, Y) if last else (0, ROWS)
        shift = jnp.tile(theta[k], (count // 8, 1))
        for p in range(2 + k, PLANES - 2 - k):
            tv, tu = smooth(v_old, p, first, count), smooth(u_old, p, first, count)
            at = (p, pl.ds(first, count))
            v = newton_step((slope, diag, inside), shift, at, v_old[at], tv, tu)
            if not last:
                v_new[p] = v
                u_new[p] = v * slope[p]
            if HALO <= p < HALO + X:
                basis[k + 1, p - HALO] = v if last else v[TOP : TOP + Y]

    inner = (lane[:8] >= HALO) & (lane[:8] < Z - HALO)
    for n, (i, j) in enumerate(PAIRS):
        total = None
        for p in range(X):
            for half in (0, 8):
                rows = pl.ds(half, 8)
                term = basis[i, p, rows] * basis[j, p, rows]
                total = term if total is None else total + term
        sums[n] = jnp.where(inner, total, 0.0)

    place = lane % GROUP
    for k in range(4):
        for q in range(PER_GROUP):
            out = jnp.zeros((ROWS, Z), F32)
            for g in range(GROUPS):
                p = PER_GROUP * g + q
                if p in planes_of(k):
                    mine = (lane // GROUP) == g
                    low = pltpu.roll(wide[k, p], GROUP * g + LOW_AT, 1)
                    high = pltpu.roll(wide[k, p], (GROUP * g + HIGH_AT) % Z, 1)
                    low_here = mine & (place >= LOW_AT) & (place < LOW_AT + 2 * HALO)
                    high_here = mine & (place >= HIGH_AT - 2 * HALO) & (place < HIGH_AT)
                    out = jnp.where(low_here, low, jnp.where(high_here, high, out))
            ends[k, q] = out


def edges(core, ends, far, chip, theta, inner_sums, basis, dots, cells, cx, mid, slope, diag, inside, va, vb, ua, ub, stack):
    lane = lax.broadcasted_iota(jnp.int32, (ROWS, Z), 1)
    place = lane % GROUP
    first_core = core[0] == 0
    partner = 1 - core[0]
    slots = mid.shape[0]
    slot = [0]

    for q in range(PER_GROUP):
        near, other = chip[partner, q], far[q]
        below = jnp.where(first_core, other, near)
        above = jnp.where(first_core, near, other)
        for k in range(4):
            low = pltpu.roll(below, (LOW_AT - AT_X[k]) % Z, 1)
            high = pltpu.roll(above, (HIGH_AT - AT_X[k]) % Z, 1)
            out = jnp.where(place < LOW_AT, low, ends[k, q])
            cells[k, q] = jnp.where((place >= HIGH_AT) & (place < HIGH_AT + HALO), high, out)

    def next_group(values, by):
        return pltpu.roll(values, (GROUP * by) % Z, 1)

    def smooth(ref, q, first=0, count=ROWS):
        here = mid.at[slot[0] % slots]
        slot[0] += 1
        before = ref[q - 1] if q else next_group(ref[PER_GROUP - 1], 1)
        after = ref[q + 1] if q + 1 < PER_GROUP else next_group(ref[0], -1)
        middle = ref[q]
        here[pl.ds(8, ROWS)] = (before + middle) + (middle + after)
        return smooth_z(smooth_y(here, first, count))

    cond, start, rest, flag = (cells.at[k] for k in range(4))
    for q in range(PER_GROUP):
        cx[q] = cond[q] * start[q]
    for q in range(PER_GROUP):
        tc, tx, tcx = (smooth(ref, q) for ref in (cond, start, cx))
        c = cond[q]
        near = 16.0 * c + 0.5 * tc
        diag[q] = (1.0 + 6.0 * flag[q] + near) * (1.0 / SCALE)
        slope[q] = c * (0.5 / SCALE)
        inside[q] = jnp.where(c > 0.0, 1.0, 0.0)
        r = (rest[q] - near * start[q] + 0.5 * (c * tx + tcx)) * inside[q]
        va[q] = r
        ua[q] = r * slope[q]
        basis[0, q] = r[TOP : TOP + Y]
    for k in range(ITERS):
        v_old, u_old, v_new, u_new = (va, ua, vb, ub) if k % 2 == 0 else (vb, ub, va, ua)
        last = k + 1 == ITERS
        first, count = (TOP, Y) if last else (0, ROWS)
        shift = jnp.tile(theta[k], (count // 8, 1))
        for q in range(PER_GROUP):
            tv, tu = smooth(v_old, q, first, count), smooth(u_old, q, first, count)
            at = (q, pl.ds(first, count))
            v = newton_step((slope, diag, inside), shift, at, v_old[at], tv, tu)
            if not last:
                v_new[q] = v
                u_new[q] = v * slope[q]
            basis[k + 1, q] = v if last else v[TOP : TOP + Y]

    end_cells = ((place >= LOW_AT) & (place < LOW_AT + HALO)) | ((place >= HIGH_AT - HALO) & (place < HIGH_AT))
    mine = []
    for q in range(PER_GROUP):
        own = [g for g in range(GROUPS) if HALO <= PER_GROUP * g + q < HALO + X]
        at = (lane >= GROUP * own[0]) & (lane < GROUP * (own[-1] + 1))
        mine.append(jnp.where(at & end_cells, 1.0, 0.0)[:8])
    for n in range(16):
        total = None
        if n < len(PAIRS):
            i, j = PAIRS[n]
            total = inner_sums[n]
            for q in range(PER_GROUP):
                for half in (0, 8):
                    rows = pl.ds(half, 8)
                    total = total + (basis[i, q, rows] * mine[q]) * basis[j, q, rows]
        else:
            total = jnp.zeros((8, Z), F32)
        stack[pl.ds(8 * n, 8)] = total
    row = lax.broadcasted_iota(jnp.int32, (Z, Z), 0)
    column = lax.broadcasted_iota(jnp.int32, (Z, Z), 1)
    pick = jnp.where((row // 8 == column % 16) & (column < 32), 1.0, 0.0)
    by_row = lax.dot_general(
        jnp.ones((8, Z), F32), stack[...], (((1,), (1,)), ((), ())),
        precision=lax.Precision.HIGHEST, preferred_element_type=F32,
    )
    total = lax.dot_general(
        by_row, pick, (((1,), (0,)), ((), ())),
        precision=lax.Precision.HIGHEST, preferred_element_type=F32,
    )
    for n in range(dots.shape[0]):
        dots[n] = total[0:1]


def two_sum(a, b):
    s = a + b
    t = s - a
    return s, (a - (s - t)) + (b - t)


def row_sum(parts):
    rows = [(parts[n], None) for n in range(parts.shape[0])]
    while len(rows) > 1:
        pairs, rows = zip(rows[::2], rows[1::2]), []
        for (a, ea), (b, eb) in pairs:
            s, e = two_sum(a, b)
            rows.append((s, e if ea is None else e + (ea + eb)))
    return rows[0]


def relay(parts, copies):
    total, rest = row_sum(parts)
    lane = lax.broadcasted_iota(jnp.int32, total.shape, 1)
    total = jnp.where(lane < 16, total, rest)
    for n in range(copies.shape[0]):
        copies[n] = total


def quick(a, b):
    s = a + b
    return s, b - (s - a)


def halves(a):
    t = 4097.0 * a
    high = t - (t - a)
    return high, a - high


def plus(a, b):
    s, e = two_sum(a[0], b[0])
    return quick(s, e + (a[1] + b[1]))


def minus(a, b):
    return plus(a, (-b[0], -b[1]))


def times(a, b):
    p = a[0] * b[0]
    ah, al = halves(a[0])
    bh, bl = halves(b[0])
    e = ((ah * bh - p) + ah * bl + al * bh) + al * bl
    return quick(p, e + (a[0] * b[1] + a[1] * b[0]))


def over(a, b):
    q = a[0] / b[0]
    none = jnp.zeros_like(q)
    rest = minus(a, times((q, none), b))
    return quick(q, rest[0] / b[0])


def conjugate_gradients(gram, theta):
    none = jnp.zeros_like(theta[0])
    zero, one = (none, none), (none + 1.0, none)
    shift = [(t, none) for t in theta]

    def along(k, vector):
        total = times(gram[k, 0], vector[0])
        for j in range(1, len(vector)):
            total = plus(total, times(gram[k, j], vector[j]))
        return total

    r, p = [one], [one]
    y = [zero] * ITERS
    rr = gram[0, 0]
    for k in range(ITERS):
        image = [times(shift[i], p[i]) for i in range(k + 1)] + [zero]
        image = [image[0]] + [plus(image[i], p[i - 1]) for i in range(1, k + 2)]
        step = over(rr, times(p[k], along(k, image)))
        y = [plus(y[i], times(step, p[i])) if i <= k else y[i] for i in range(ITERS)]
        r = [minus(r[i] if i <= k else zero, times(step, image[i])) for i in range(k + 2)]
        if k + 1 < ITERS:
            new = times(r[k + 1], along(k + 1, r))
            ratio = over(new, rr)
            p = [plus(r[i], times(ratio, p[i])) if i <= k else r[i] for i in range(k + 2)]
            rr = new
    return [a[0] * (1.0 / SCALE) for a in y], [a[0] for a in r]


def finish(parts, basis, end_basis, fields, theta, closing, mismatch):
    total, rest = row_sum(parts)
    rest = rest + pltpu.roll(total, Z - 16, 1)
    gram = {}
    for n, (i, j) in enumerate(PAIRS):
        gram[i, j] = gram[j, i] = quick(
            *(jnp.broadcast_to(v[0:1, n : n + 1], (8, Z)) for v in (total, rest))
        )
    y, r = conjugate_gradients(gram, [theta[k] for k in range(ITERS)])

    def combine(v):
        x, m = y[0] * v[0], r[ITERS] * v[ITERS]
        for k in range(1, ITERS):
            x = x + y[k] * v[k]
        for k in range(ITERS):
            m = m + r[k] * v[k]
        return x, m

    lane = lax.broadcasted_iota(jnp.int32, (8, Z), 1)
    for half in (0, 8):
        rows = pl.ds(half, 8)
        ends = [
            combine([end_basis[k, q, rows] for k in range(ITERS + 1)]) for q in range(PER_GROUP)
        ]
        for p in range(X):
            g, q = divmod(p + HALO, PER_GROUP)
            inner = combine([basis[k, p, rows] for k in range(ITERS + 1)])
            both = []
            for value, end in zip(inner, ends[q]):
                low = pltpu.roll(end, (Z - GROUP * g - LOW_AT) % Z, 1)
                high = pltpu.roll(end, (Z - GROUP * g - HIGH_AT) % Z, 1)
                value = jnp.where(lane < HALO, low, value)
                both.append(jnp.where(lane >= Z - HALO, high, value))
            closing[p, rows] = fields[1, p, rows] + both[0]
            mismatch[p, rows] = both[1]


def both_ways(low, high, axis):
    ends = lax.axis_size(axis) - 1
    from_below = lax.ppermute(high, axis, [(i, i + 1) for i in range(ends)])
    from_above = lax.ppermute(low, axis, [(i + 1, i) for i in range(ends)])
    return from_below, from_above


def exchange(copies, axes):
    return lax.all_to_all(copies, axes, split_axis=0, concat_axis=0, tiled=True)


def body(opening, source, category, table, flags):
    brick = (X, Y, Z)
    whole = pltpu.VMEM(brick, jnp.int32)
    fields, low, high, theta = call(
        prepare,
        [HBM] * 5,
        [(4, *brick), (SLAB_X, Y, Z), (SLAB_X, Y, Z), (ITERS, 8, Z)],
        [brick, brick, whole, whole, pltpu.SMEM(table.shape, F32), pltpu.SemaphoreType.DMA((5,))],
    )(*(pltpu.with_memory_space_constraint(a, pltpu.HBM) for a in (opening, source, category, flags, table)))
    left, right = both_ways(low, high, "gx")
    low, high = call(slabs_y, [VMEM] * 3, [(SLAB_Y, Z)] * 2)(fields, left, right)
    below, above = both_ways(low, high, "gy")
    core = lax.axis_index(GZ[1]).reshape(1)
    packed = (PER_GROUP, ROWS, Z)
    wide, near, far = call(assemble, [SMEM] + [VMEM] * 5, [(4, PLANES, ROWS, Z), packed, packed])(
        core, fields, left, right, below, above
    )
    far = lax.ppermute(
        far,
        GZ,
        [p for i in range(1, lax.axis_size(GZ) - 1, 2) for p in ((i, i + 1), (i + 1, i))],
    )
    chip = lax.all_gather(near, GZ[1], axis=0)
    sided = (PLANES, ROWS, Z)
    middle = (6, ROWS + 16, Z)
    basis, sums, ends = call(
        interior,
        [VMEM] * 2,
        [(ITERS + 1, *brick), (len(PAIRS), 8, Z), (4, *packed)],
        [sided, middle] + [sided] * 7,
        flops=20000000,
        vmem=12,
    )(wide, theta)
    first, second = ("gx", "gz_0"), ("gy", "gz_1")
    end_basis, dots = call(
        edges,
        [SMEM] + [VMEM] * 5,
        [(ITERS + 1, PER_GROUP, Y, Z), (lax.axis_size(first), 1, Z)],
        [(4, *packed), packed, middle] + [packed] * 7 + [(Z, Z)],
        flops=5000000,
    )(core, ends, far, chip, theta, sums)
    parts = exchange(dots, first)
    (copies,) = call(relay, [VMEM], [(lax.axis_size(second), 1, Z)])(parts)
    parts = exchange(copies, second)
    closing, mismatch = call(finish, [VMEM] * 5, [brick, brick])(
        parts, basis, end_basis, fields, theta
    )
    return closing, mismatch


def solution(mesh):
    shape = mesh.devices.shape
    split = Mesh(mesh.devices.reshape(shape[0], shape[1], shape[2] // 2, 2), ("gx", "gy", *GZ))
    spec = P("gx", "gy", GZ)
    return jax.shard_map(
        body, mesh=split, in_specs=(spec, spec, spec, P(), spec), out_specs=(spec, spec), check_vma=False
    )
```

time: 73.3 us -> 80 us (1.091)
  Pallas kernels: 7.15 us -> 14.9 us
    pallas_call x3 -> x4, Pallas kernels: 6.01 us -> 13.7 us  [the longest x1 9.99 us: body(): call(interior, [VMEM] * 2, [(ITERS + 1, *brick), (len(PAIRS), 8, Z), (4,...]
  transfers between devices with their start and end apart: 5 -> 5, of which waited for: 5 -> 4; matrix products, arithmetic and copies ran while one was open for 0% -> 0% of each run, Pallas kernels for 0% -> 13%
where the time goes in v4:
time: 80 us; the launch traced here: 79.7 us
  blocking collectives  37.8 us (47%)
  starting transfers between devices  17.2 us (22%)
  Pallas kernels  14.9 us (19%)
  waiting for transfers between devices  9.08 us (11%)
    all_to_all x2, blocking collectives, exchange(): return lax.all_to_all(copies, axes, split_axis=0, concat_axis=0, tiled=True)  35.9 us
    pallas_call x1, Pallas kernels, body(): call(interior, [VMEM] * 2, [(ITERS + 1, *brick), (len(PAIRS), 8, Z), (4,...  9.99 us
    ppermute x2, waiting for transfers between devices, both_ways(): from_above = lax.ppermute(low, axis, [(i + 1, i) for i in range(ends)])  7.61 us
    ppermute x2, starting transfers between devices, both_ways(): from_below = lax.ppermute(high, axis, [(i, i + 1) for i in range(ends)])  7.52 us
    ppermute x1, starting transfers between devices, body(): lax.ppermute(far, GZ, [p for i in range(1, lax.axis_size(GZ) - 1, 2) for...  7.13 us
    ppermute x2, starting transfers between devices, both_ways(): from_above = lax.ppermute(low, axis, [(i + 1, i) for i in range(ends)])  2.58 us
    all_gather x1, blocking collectives, body(): chip = lax.all_gather(near, GZ[1], axis=0)  1.92 us
    pallas_call x1, Pallas kernels, body(): call(edges, [SMEM] + [VMEM] * 5, [(ITERS + 1, PER_GROUP, Y, Z), (lax.axis...  1.77 us
  transfers between devices with their start and end apart: 5, of which 4 were waited for; matrix products, arithmetic and copies ran while one was open for 0% of the time, Pallas kernels for 13%

profile of v4, /device:TPU:1, one launch (start us, length us, event | category | flops | bytes accessed | tf_op | source)
XLA Modules:
  0.0 79.7 jit_solution(11735452236672039322)
XLA Ops:
  0.6 1.1 %shard_map.68 = (f32[4,8,16,128]{3,2,1,0:T(8,128)S(1)}, f32[17,16,128]{2,1,0:T(8,128)S(1)}, f32[17,16,128]{2,1,0:T(8,128)S(1)}, f32[4,8,128]{2,1,0:T(8,128)S(1)}) custom-call(f32[8,16,128]{2,1,0:T(8,128)} %opening_at.1, f32[8,16,128]{2,1,0:T(8,128)} %source_at.1, s32[8,16,128]{2,1,0:T(8,128)} %category_at.1, s32[8,16,128]{2,1,0:T(8,128)} %flags_at.1, f32[16]{0:T(128)} %table_at.1), custom_call_target="tpu_custom_call" | custom-call | flops 100000 | bytes 1000000 | tf_op jit(solution)/shard_map/pallas_call | solution.py:457
  1.7 3.9 %collective-permute-start = (f32[17,16,128]{2,1,0:T(8,128)S(1)}, f32[17,16,128]{2,1,0:T(8,128)S(1)}, u32[]{:S(2)}, u32[]{:S(2)}) collective-permute-start(f32[17,16,128]{2,1,0:T(8,128)S(1)} %get-tuple-element.17), channel_id=1, source_target_pairs={{0,128},{128,256},{256,384},{1,129},{129,257},{257,385},{2,130},{1... | collective-permute-start | bytes 417800 | tf_op jit(solution)/shard_map/ppermute | solution.py:445
  5.7 1.3 %collective-permute-start.1 = (f32[17,16,128]{2,1,0:T(8,128)S(1)}, f32[17,16,128]{2,1,0:T(8,128)S(1)}, u32[]{:S(2)}, u32[]{:S(2)}) collective-permute-start(f32[17,16,128]{2,1,0:T(8,128)S(1)} %get-tuple-element.18), channel_id=1, source_target_pairs={{128,0},{256,128},{384,256},{129,1},{257,129},{385,257},{130,2},{2... | collective-permute-start | bytes 417800 | tf_op jit(solution)/shard_map/ppermute | solution.py:446
  7.0 0.7 collective-permute-done.left
  7.7 3.8 %collective-permute-done.1.right = f32[17,16,128]{2,1,0:T(8,128)S(1)} collective-permute-done((f32[17,16,128]{2,1,0:T(8,128)S(1)}, f32[17,16,128]{2,1,0:T(8,128)S(1)}, u32[]{:S(2)}, u32[]{:S(2)}) %collective-permute-start.1) | collective-permute-done | bytes 139296 | tf_op jit(solution)/shard_map/ppermute | solution.py:446
  11.5 3.6 %collective-permute-start.2 = (f32[288,128]{1,0:T(8,128)S(1)}, f32[288,128]{1,0:T(8,128)S(1)}, u32[]{:S(2)}, u32[]{:S(2)}) collective-permute-start(f32[288,128]{1,0:T(8,128)S(1)} %get-tuple-element.19), channel_id=1, source_target_pairs={{0,16},{16,32},{32,48},{48,64},{64,80},{80,96},{96,112},{1,17},{17... | collective-permute-start | bytes 442376 | tf_op jit(solution)/shard_map/ppermute | solution.py:445
  15.1 1.3 %collective-permute-start.3 = (f32[288,128]{1,0:T(8,128)S(1)}, f32[288,128]{1,0:T(8,128)S(1)}, u32[]{:S(2)}, u32[]{:S(2)}) collective-permute-start(f32[288,128]{1,0:T(8,128)S(1)} %get-tuple-element.20), channel_id=1, source_target_pairs={{16,0},{32,16},{48,32},{64,48},{80,64},{96,80},{112,96},{17,1},{33... | collective-permute-start | bytes 442376 | tf_op jit(solution)/shard_map/ppermute | solution.py:446
  16.4 0.8 collective-permute-done.2.below
  17.2 3.8 %collective-permute-done.3.above = f32[288,128]{1,0:T(8,128)S(1)} collective-permute-done((f32[288,128]{1,0:T(8,128)S(1)}, f32[288,128]{1,0:T(8,128)S(1)}, u32[]{:S(2)}, u32[]{:S(2)}) %collective-permute-start.3) | collective-permute-done | bytes 147488 | tf_op jit(solution)/shard_map/ppermute | solution.py:446
  21.0 0.4 shard_map.70
  21.4 7.1 %collective-permute-start.4 = (f32[5,32,128]{2,1,0:T(8,128)S(1)}, f32[5,32,128]{2,1,0:T(8,128)S(1)}, u32[]{:S(2)}, u32[]{:S(2)}) collective-permute-start(f32[5,32,128]{2,1,0:T(8,128)S(1)} %get-tuple-element.24), channel_id=1, source_target_pairs={{1,2},{2,1},{3,4},{4,3},{5,6},{6,5},{7,8},{8,7},{9,10},{10,9},{11,... | collective-permute-start | bytes 245768 | tf_op jit(solution)/shard_map/ppermute | solution.py:471
  28.5 10.0 %shard_map.71 = (f32[5,8,16,128]{3,2,1,0:T(8,128)S(1)}, f32[14,8,128]{2,1,0:T(8,128)S(1)}, f32[4,5,32,128]{3,2,1,0:T(8,128)S(1)}) custom-call(f32[4,18,32,128]{3,2,1,0:T(8,128)S(1)} %get-tuple-element.21.wide, f32[4,8,128]{2,1,0:T(8,128)S(1)} %get-tuple-element.22.theta), custom_call_target="tpu_custom_call" | custom-call | flops 20000000 | bytes 1000000 | tf_op jit(solution)/shard_map/pallas_call | solution.py:479
  38.5 1.9 %all-gather = f32[10,32,128]{2,1,0:T(8,128)S(1)} all-gather(f32[5,32,128]{2,1,0:T(8,128)S(1)} %get-tuple-element.25), channel_id=2, replica_groups=mesh['gx'=4,'gy'=8,'gz_0'=8,'gz_1'=2] {'gz_1'}, dimensions={0}, use_global_device_ids=true | all-gather | bytes 245760 | tf_op jit(solution)/shard_map/all_gather | solution.py:476
  40.4 0.0 collective-permute-done.4.far
  40.4 1.8 %shard_map.72 = (f32[5,5,16,128]{3,2,1,0:T(8,128)S(1)}, f32[32,1,128]{2,1,0:T(1,128)S(1)}) custom-call(s32[1]{0:T(128)} %bitcast.core, f32[4,5,32,128]{3,2,1,0:T(8,128)S(1)} %get-tuple-element.23.ends, f32[5,32,128]{2,1,0:T(8,128)S(1)} %collective-permute-done.4.far, f32[2,5,32,128]{3,2,1,0:T(8,128)S(1)} %bitcast.2, ...), custom_call_target="tpu_custom_call" | custom-call | flops 5000000 | bytes 1000000 | tf_op jit(solution)/shard_map/pallas_call | solution.py:488
  42.2 20.1 %all_to_all.10.parts = f32[32,1,128]{2,1,0:T(1,128)S(1)} all-to-all(f32[32,1,128]{2,1,0:T(1,128)S(1)} %get-tuple-element.27), channel_id=1, replica_groups=mesh['gx'=4,'gy'=8,'gz_0'=8,'gz_1'=2] {'gx','gz_0'}, dimensions={0} | all-to-all | bytes 32768 | tf_op jit(solution)/shard_map/all_to_all | solution.py:451
  62.4 15.7 %all_to_all.11.parts = f32[16,1,128]{2,1,0:T(1,128)S(1)} all-to-all(f32[16,1,128]{2,1,0:T(1,128)S(1)} %shard_map.73), channel_id=1, replica_groups=mesh['gx'=4,'gy'=8,'gz_0'=8,'gz_1'=2] {'gy','gz_1'}, dimensions={0} | all-to-all | bytes 16384 | tf_op jit(solution)/shard_map/all_to_all | solution.py:451
  78.1 1.6 %shard_map.74 = (f32[8,16,128]{2,1,0:T(8,128)}, f32[8,16,128]{2,1,0:T(8,128)}) custom-call(f32[16,1,128]{2,1,0:T(1,128)S(1)} %all_to_all.11.parts, f32[5,8,16,128]{3,2,1,0:T(8,128)S(1)} %get-tuple-element.28.basis, f32[5,5,16,128]{3,2,1,0:T(8,128)S(1)} %get-tuple-element.29.end_basis, f32[4,8,16,128]{3,2,1,0:T(8,128)S(1)} %get-tuple-element.16.fields, ...), custom_call_target="tpu_custom_call" | custom-call | flops 100000 | bytes 1000000 | tf_op jit(solution)/shard_map/pallas_call | solution.py:498
  (2 shorter events, 0.1 us)
Async XLA Ops:
  1.7 5.9 %collective-permute-start = (f32[17,16,128]{2,1,0:T(8,128)S(1)}, f32[17,16,128]{2,1,0:T(8,128)S(1)}, u32[]{:S(2)}, u32[]{:S(2)}) collective-permute-start(f32[17,16,128]{2,1,0:T(8,128)S(1)} %get-tuple-element.17), channel_id=1, source_target_pairs={{0,128},{128,256},{256,384},{1,129},{129,257},{257,385},{2,130},{1... | collective-permute-start | bytes 417800 | tf_op jit(solution)/shard_map/ppermute | solution.py:445
  5.7 5.8 %collective-permute-start.1 = (f32[17,16,128]{2,1,0:T(8,128)S(1)}, f32[17,16,128]{2,1,0:T(8,128)S(1)}, u32[]{:S(2)}, u32[]{:S(2)}) collective-permute-start(f32[17,16,128]{2,1,0:T(8,128)S(1)} %get-tuple-element.18), channel_id=1, source_target_pairs={{128,0},{256,128},{384,256},{129,1},{257,129},{385,257},{130,2},{2... | collective-permute-start | bytes 417800 | tf_op jit(solution)/shard_map/ppermute | solution.py:446
  11.5 5.7 %collective-permute-start.2 = (f32[288,128]{1,0:T(8,128)S(1)}, f32[288,128]{1,0:T(8,128)S(1)}, u32[]{:S(2)}, u32[]{:S(2)}) collective-permute-start(f32[288,128]{1,0:T(8,128)S(1)} %get-tuple-element.19), channel_id=1, source_target_pairs={{0,16},{16,32},{32,48},{48,64},{64,80},{80,96},{96,112},{1,17},{17... | collective-permute-start | bytes 442376 | tf_op jit(solution)/shard_map/ppermute | solution.py:445
  15.1 5.9 %collective-permute-start.3 = (f32[288,128]{1,0:T(8,128)S(1)}, f32[288,128]{1,0:T(8,128)S(1)}, u32[]{:S(2)}, u32[]{:S(2)}) collective-permute-start(f32[288,128]{1,0:T(8,128)S(1)} %get-tuple-element.20), channel_id=1, source_target_pairs={{16,0},{32,16},{48,32},{64,48},{80,64},{96,80},{112,96},{17,1},{33... | collective-permute-start | bytes 442376 | tf_op jit(solution)/shard_map/ppermute | solution.py:446
  21.4 19.1 %collective-permute-start.4 = (f32[5,32,128]{2,1,0:T(8,128)S(1)}, f32[5,32,128]{2,1,0:T(8,128)S(1)}, u32[]{:S(2)}, u32[]{:S(2)}) collective-permute-start(f32[5,32,128]{2,1,0:T(8,128)S(1)} %get-tuple-element.24), channel_id=1, source_target_pairs={{1,2},{2,1},{3,4},{4,3},{5,6},{6,5},{7,8},{8,7},{9,10},{10,9},{11,... | collective-permute-start | bytes 245768 | tf_op jit(solution)/shard_map/ppermute | solution.py:471

commit v5 on v4

--- a/solution.py
+++ b/solution.py
@@ -22,6 +22,7 @@
 GROUPS, PER_GROUP, GROUP = 4, 5, 32
 LOW_AT, HIGH_AT = 5, 26
 SCALE = 64.0
+CHUNK = 4
 PAIRS = [(i, j) for i in range(ITERS) for j in range(i, ITERS + 1)]
 VMEM = pl.BlockSpec(memory_space=pltpu.VMEM)
 HBM = pl.BlockSpec(memory_space=pltpu.HBM)
@@ -141,19 +142,22 @@
     ]
 
 
-def smooth_y(mid, first, count):
-    sides = mid[pl.ds(7 + first, count)] + mid[pl.ds(9 + first, count)]
-    return mid[pl.ds(8 + first, count)] + 0.5 * sides
-
-
-def smooth_z(values):
-    pairs = values + pltpu.roll(values, Z - 1, 1)
-    return pairs + pltpu.roll(pairs, 1, 1)
-
-
-def newton_step(store, shift, at, v, tv, tu):
-    slope, diag, inside = store
-    return ((diag[at] - shift) * v - (slope[at] * tv + tu)) * inside[at]
+def smooth(mid, ahead, here, behind, first, count):
+    n = here.shape[0]
+    mid[0:n, 8 : 8 + ROWS] = (ahead + here) + (here + behind)
+    sides = mid[0:n, pl.ds(7 + first, count)] + mid[0:n, pl.ds(9 + first, count)]
+    rows = mid[0:n, pl.ds(8 + first, count)] + 0.5 * sides
+    return rows + 0.5 * (pltpu.roll(rows, 1, 2) + pltpu.roll(rows, Z - 1, 2))
+
+
+def newton_step(slope, diag, inside, shift, v, tv, tu):
+    return ((diag - shift) * v - (slope * tv + tu)) * inside
+
+
+def chunks(low, high, most):
+    count = -(-(high - low) // most)
+    size = -(-(high - low) // count)
+    return [(p, min(p + size, high)) for p in range(low, high, size)]
 
 
 def interior(wide, theta, basis, sums, ends, cx, mid, slope, diag, inside, va, vb, ua, ub):
@@ -161,43 +165,43 @@
     slots = mid.shape[0]
     slot = [0]
 
-    def smooth(ref, p, first=0, count=ROWS):
-        here = mid.at[slot[0] % slots]
+    def along(ref, p, q, first=0, count=ROWS):
         slot[0] += 1
-        middle = ref[p]
-        here[pl.ds(8, ROWS)] = (ref[p - 1] + middle) + (middle + ref[p + 1])
-        return smooth_z(smooth_y(here, first, count))
+        return smooth(
+            mid.at[slot[0] % slots], ref[p - 1 : q - 1], ref[p:q], ref[p + 1 : q + 1], first, count
+        )
 
     cond, start, rest, flag = (wide.at[k] for k in range(4))
-    for p in range(PLANES):
-        cx[p] = cond[p] * start[p]
-    for p in range(1, PLANES - 1):
-        tc, tx, tcx = (smooth(ref, p) for ref in (cond, start, cx))
-        c = cond[p]
-        near = 16.0 * c + 0.5 * tc
-        if p in planes_of(3):
-            diag[p] = (1.0 + 6.0 * flag[p] + near) * (1.0 / SCALE)
-        slope[p] = c * (0.5 / SCALE)
-        inside[p] = jnp.where(c > 0.0, 1.0, 0.0)
-        r = (rest[p] - near * start[p] + 0.5 * (c * tx + tcx)) * inside[p]
-        va[p] = r
-        ua[p] = r * slope[p]
-        if HALO <= p < HALO + X:
-            basis[0, p - HALO] = r[TOP : TOP + Y]
+    cx[...] = cond[...] * start[...]
+    for p, q in chunks(1, PLANES - 1, CHUNK):
+        tc, tx, tcx = (along(ref, p, q) for ref in (cond, start, cx))
+        c = cond[p:q]
+        near = 16.0 * c + tc
+        diag[p:q] = (1.0 + 6.0 * flag[p:q] + near) * (1.0 / SCALE)
+        half_c = c * (1.0 / SCALE)
+        slope[p:q] = half_c
+        there = jnp.where(c > 0.0, 1.0, 0.0)
+        inside[p:q] = there
+        r = (rest[p:q] - near * start[p:q] + (c * tx + tcx)) * there
+        va[p:q] = r
+        ua[p:q] = r * half_c
+    basis[0] = va[HALO : HALO + X, TOP : TOP + Y]
     for k in range(ITERS):
         v_old, u_old, v_new, u_new = (va, ua, vb, ub) if k % 2 == 0 else (vb, ub, va, ua)
         last = k + 1 == ITERS
         first, count = (TOP, Y) if last else (0, ROWS)
-        shift = jnp.tile(theta[k], (count // 8, 1))
-        for p in range(2 + k, PLANES - 2 - k):
-            tv, tu = smooth(v_old, p, first, count), smooth(u_old, p, first, count)
-            at = (p, pl.ds(first, count))
-            v = newton_step((slope, diag, inside), shift, at, v_old[at], tv, tu)
-            if not last:
-                v_new[p] = v
-                u_new[p] = v * slope[p]
-            if HALO <= p < HALO + X:
-                basis[k + 1, p - HALO] = v if last else v[TOP : TOP + Y]
+        rows = pl.ds(first, count)
+        shift = jnp.tile(theta[k], (count // 8, 1))[None]
+        for p, q in chunks(2 + k, PLANES - 2 - k, CHUNK):
+            tv, tu = along(v_old, p, q, first, count), along(u_old, p, q, first, count)
+            v = newton_step(slope[p:q, rows], diag[p:q, rows], inside[p:q, rows], shift, v_old[p:q, rows], tv, tu)
+            if last:
+                basis[k + 1, p - HALO : q - HALO] = v
+            else:
+                v_new[p:q] = v
+                u_new[p:q] = v * slope[p:q]
+        if not last:
+            basis[k + 1] = v_new[HALO : HALO + X, TOP : TOP + Y]
 
     inner = (lane[:8] >= HALO) & (lane[:8] < Z - HALO)
     for n, (i, j) in enumerate(PAIRS):
@@ -243,45 +247,46 @@
             out = jnp.where(place < LOW_AT, low, ends[k, q])
             cells[k, q] = jnp.where((place >= HIGH_AT) & (place < HIGH_AT + HALO), high, out)
 
-    def next_group(values, by):
-        return pltpu.roll(values, (GROUP * by) % Z, 1)
-
-    def smooth(ref, q, first=0, count=ROWS):
-        here = mid.at[slot[0] % slots]
+    def along(ref, first=0, count=ROWS):
         slot[0] += 1
-        before = ref[q - 1] if q else next_group(ref[PER_GROUP - 1], 1)
-        after = ref[q + 1] if q + 1 < PER_GROUP else next_group(ref[0], -1)
-        middle = ref[q]
-        here[pl.ds(8, ROWS)] = (before + middle) + (middle + after)
-        return smooth_z(smooth_y(here, first, count))
+        here = ref[...]
+        before = pltpu.roll(ref[PER_GROUP - 1], GROUP, 1)[None]
+        after = pltpu.roll(ref[0], Z - GROUP, 1)[None]
+        return smooth(
+            mid.at[slot[0] % slots],
+            jnp.concatenate([before, ref[: PER_GROUP - 1]]),
+            here,
+            jnp.concatenate([ref[1:], after]),
+            first,
+            count,
+        )
 
     cond, start, rest, flag = (cells.at[k] for k in range(4))
-    for q in range(PER_GROUP):
-        cx[q] = cond[q] * start[q]
-    for q in range(PER_GROUP):
-        tc, tx, tcx = (smooth(ref, q) for ref in (cond, start, cx))
-        c = cond[q]
-        near = 16.0 * c + 0.5 * tc
-        diag[q] = (1.0 + 6.0 * flag[q] + near) * (1.0 / SCALE)
-        slope[q] = c * (0.5 / SCALE)
-        inside[q] = jnp.where(c > 0.0, 1.0, 0.0)
-        r = (rest[q] - near * start[q] + 0.5 * (c * tx + tcx)) * inside[q]
-        va[q] = r
-        ua[q] = r * slope[q]
-        basis[0, q] = r[TOP : TOP + Y]
+    cx[...] = cond[...] * start[...]
+    tc, tx, tcx = (along(ref) for ref in (cond, start, cx))
+    c = cond[...]
+    near = 16.0 * c + tc
+    diag[...] = (1.0 + 6.0 * flag[...] + near) * (1.0 / SCALE)
+    half_c = c * (1.0 / SCALE)
+    slope[...] = half_c
+    there = jnp.where(c > 0.0, 1.0, 0.0)
+    inside[...] = there
+    r = (rest[...] - near * start[...] + (c * tx + tcx)) * there
+    va[...] = r
+    ua[...] = r * half_c
+    basis[0] = r[:, TOP : TOP + Y]
     for k in range(ITERS):
         v_old, u_old, v_new, u_new = (va, ua, vb, ub) if k % 2 == 0 else (vb, ub, va, ua)
         last = k + 1 == ITERS
         first, count = (TOP, Y) if last else (0, ROWS)
-        shift = jnp.tile(theta[k], (count // 8, 1))
-        for q in range(PER_GROUP):
-            tv, tu = smooth(v_old, q, first, count), smooth(u_old, q, first, count)
-            at = (q, pl.ds(first, count))
-            v = newton_step((slope, diag, inside), shift, at, v_old[at], tv, tu)
-            if not last:
-                v_new[q] = v
-                u_new[q] = v * slope[q]
-            basis[k + 1, q] = v if last else v[TOP : TOP + Y]
+        rows = pl.ds(first, count)
+        shift = jnp.tile(theta[k], (count // 8, 1))[None]
+        tv, tu = along(v_old, first, count), along(u_old, first, count)
+        v = newton_step(slope[:, rows], diag[:, rows], inside[:, rows], shift, v_old[:, rows], tv, tu)
+        if not last:
+            v_new[...] = v
+            u_new[...] = v * slope[...]
+        basis[k + 1] = v if last else v[:, TOP : TOP + Y]
 
     end_cells = ((place >= LOW_AT) & (place < LOW_AT + HALO)) | ((place >= HIGH_AT - HALO) & (place < HIGH_AT))
     mine = []
@@ -301,15 +306,11 @@
         else:
             total = jnp.zeros((8, Z), F32)
         stack[pl.ds(8 * n, 8)] = total
-    row = lax.broadcasted_iota(jnp.int32, (Z, Z), 0)
-    column = lax.broadcasted_iota(jnp.int32, (Z, Z), 1)
-    pick = jnp.where((row // 8 == column % 16) & (column < 32), 1.0, 0.0)
-    by_row = lax.dot_general(
-        jnp.ones((8, Z), F32), stack[...], (((1,), (1,)), ((), ())),
-        precision=lax.Precision.HIGHEST, preferred_element_type=F32,
-    )
+    by_sum = stack[pl.ds(0, 16, stride=8)]
+    for n in range(1, 8):
+        by_sum = by_sum + stack[pl.ds(n, 16, stride=8)]
     total = lax.dot_general(
-        by_row, pick, (((1,), (0,)), ((), ())),
+        jnp.ones((8, Z), F32), jnp.tile(by_sum, (8, 1)), (((1,), (1,)), ((), ())),
         precision=lax.Precision.HIGHEST, preferred_element_type=F32,
     )
     for n in range(dots.shape[0]):
@@ -475,7 +476,7 @@
     )
     chip = lax.all_gather(near, GZ[1], axis=0)
     sided = (PLANES, ROWS, Z)
-    middle = (6, ROWS + 16, Z)
+    middle = (3, PLANES, ROWS + 16, Z)
     basis, sums, ends = call(
         interior,
         [VMEM] * 2,
@@ -489,7 +490,7 @@
         edges,
         [SMEM] + [VMEM] * 5,
         [(ITERS + 1, PER_GROUP, Y, Z), (lax.axis_size(first), 1, Z)],
-        [(4, *packed), packed, middle] + [packed] * 7 + [(Z, Z)],
+        [(4, *packed), packed, (3, PER_GROUP, ROWS + 16, Z)] + [packed] * 7 + [(Z, Z)],
         flops=5000000,
     )(core, ends, far, chip, theta, sums)
     parts = exchange(dots, first)

time: 80 us -> 71.7 us (0.90)
  Pallas kernels: 14.9 us -> 6.52 us
    pallas_call x1, Pallas kernels: 9.99 us -> 2.05 us  [body(): call(interior, [VMEM] * 2, [(ITERS + 1, *brick), (len(PAIRS), 8, Z), (4,...]
  transfers between devices with their start and end apart: 5 -> 5, of which waited for: 4 -> 4; matrix products, arithmetic and copies ran while one was open for 0% -> 0% of each run, Pallas kernels for 13% -> 3%
where the time goes in v5:
time: 71.7 us; the launch traced here: 71.4 us
  blocking collectives  37.8 us (53%)
  starting transfers between devices  17.2 us (24%)
  waiting for transfers between devices  9.08 us (13%)
  Pallas kernels  6.52 us (9%)
  between operations  0.73 us (1%)
    all_to_all x2, blocking collectives, exchange(): return lax.all_to_all(copies, axes, split_axis=0, concat_axis=0, tiled=True)  35.9 us
    ppermute x2, waiting for transfers between devices, both_ways(): from_above = lax.ppermute(low, axis, [(i + 1, i) for i in range(ends)])  7.61 us
    ppermute x2, starting transfers between devices, both_ways(): from_below = lax.ppermute(high, axis, [(i, i + 1) for i in range(ends)])  7.52 us
    ppermute x1, starting transfers between devices, body(): lax.ppermute(far, GZ, [p for i in range(1, lax.axis_size(GZ) - 1, 2) for...  7.13 us
    ppermute x2, starting transfers between devices, both_ways(): from_above = lax.ppermute(low, axis, [(i + 1, i) for i in range(ends)])  2.58 us
    pallas_call x1, Pallas kernels, body(): call(interior, [VMEM] * 2, [(ITERS + 1, *brick), (len(PAIRS), 8, Z), (4,...  2.05 us
    all_gather x1, blocking collectives, body(): chip = lax.all_gather(near, GZ[1], axis=0)  1.92 us
    pallas_call x1, Pallas kernels, body(): call(finish, [VMEM] * 5, [brick, brick])  1.56 us
  transfers between devices with their start and end apart: 5, of which 4 were waited for; matrix products, arithmetic and copies ran while one was open for 0% of the time, Pallas kernels for 3%

profile of v5, /device:TPU:1, one launch (start us, length us, event | category | flops | bytes accessed | tf_op | source)
XLA Modules:
  0.0 71.4 jit_solution(4556314536001003222)
XLA Ops:
  0.6 1.1 %shard_map.68 = (f32[4,8,16,128]{3,2,1,0:T(8,128)S(1)}, f32[17,16,128]{2,1,0:T(8,128)S(1)}, f32[17,16,128]{2,1,0:T(8,128)S(1)}, f32[4,8,128]{2,1,0:T(8,128)S(1)}) custom-call(f32[8,16,128]{2,1,0:T(8,128)} %opening_at.1, f32[8,16,128]{2,1,0:T(8,128)} %source_at.1, s32[8,16,128]{2,1,0:T(8,128)} %category_at.1, s32[8,16,128]{2,1,0:T(8,128)} %flags_at.1, f32[16]{0:T(128)} %table_at.1), custom_call_target="tpu_custom_call" | custom-call | flops 100000 | bytes 1000000 | tf_op jit(solution)/shard_map/pallas_call | solution.py:458
  1.7 3.9 %collective-permute-start = (f32[17,16,128]{2,1,0:T(8,128)S(1)}, f32[17,16,128]{2,1,0:T(8,128)S(1)}, u32[]{:S(2)}, u32[]{:S(2)}) collective-permute-start(f32[17,16,128]{2,1,0:T(8,128)S(1)} %get-tuple-element.17), channel_id=1, source_target_pairs={{0,128},{128,256},{256,384},{1,129},{129,257},{257,385},{2,130},{1... | collective-permute-start | bytes 417800 | tf_op jit(solution)/shard_map/ppermute | solution.py:446
  5.7 1.3 %collective-permute-start.1 = (f32[17,16,128]{2,1,0:T(8,128)S(1)}, f32[17,16,128]{2,1,0:T(8,128)S(1)}, u32[]{:S(2)}, u32[]{:S(2)}) collective-permute-start(f32[17,16,128]{2,1,0:T(8,128)S(1)} %get-tuple-element.18), channel_id=1, source_target_pairs={{128,0},{256,128},{384,256},{129,1},{257,129},{385,257},{130,2},{2... | collective-permute-start | bytes 417800 | tf_op jit(solution)/shard_map/ppermute | solution.py:447
  7.0 0.7 collective-permute-done.left
  7.7 3.8 %collective-permute-done.1.right = f32[17,16,128]{2,1,0:T(8,128)S(1)} collective-permute-done((f32[17,16,128]{2,1,0:T(8,128)S(1)}, f32[17,16,128]{2,1,0:T(8,128)S(1)}, u32[]{:S(2)}, u32[]{:S(2)}) %collective-permute-start.1) | collective-permute-done | bytes 139296 | tf_op jit(solution)/shard_map/ppermute | solution.py:447
  11.5 3.6 %collective-permute-start.2 = (f32[288,128]{1,0:T(8,128)S(1)}, f32[288,128]{1,0:T(8,128)S(1)}, u32[]{:S(2)}, u32[]{:S(2)}) collective-permute-start(f32[288,128]{1,0:T(8,128)S(1)} %get-tuple-element.19), channel_id=1, source_target_pairs={{0,16},{16,32},{32,48},{48,64},{64,80},{80,96},{96,112},{1,17},{17... | collective-permute-start | bytes 442376 | tf_op jit(solution)/shard_map/ppermute | solution.py:446
  15.1 1.3 %collective-permute-start.3 = (f32[288,128]{1,0:T(8,128)S(1)}, f32[288,128]{1,0:T(8,128)S(1)}, u32[]{:S(2)}, u32[]{:S(2)}) collective-permute-start(f32[288,128]{1,0:T(8,128)S(1)} %get-tuple-element.20), channel_id=1, source_target_pairs={{16,0},{32,16},{48,32},{64,48},{80,64},{96,80},{112,96},{17,1},{33... | collective-permute-start | bytes 442376 | tf_op jit(solution)/shard_map/ppermute | solution.py:447
  16.4 0.8 %collective-permute-done.2.below = f32[288,128]{1,0:T(8,128)S(1)} collective-permute-done((f32[288,128]{1,0:T(8,128)S(1)}, f32[288,128]{1,0:T(8,128)S(1)}, u32[]{:S(2)}, u32[]{:S(2)}) %collective-permute-start.2) | collective-permute-done | bytes 147488 | tf_op jit(solution)/shard_map/ppermute | solution.py:446
  17.2 3.8 %collective-permute-done.3.above = f32[288,128]{1,0:T(8,128)S(1)} collective-permute-done((f32[288,128]{1,0:T(8,128)S(1)}, f32[288,128]{1,0:T(8,128)S(1)}, u32[]{:S(2)}, u32[]{:S(2)}) %collective-permute-start.3) | collective-permute-done | bytes 147488 | tf_op jit(solution)/shard_map/ppermute | solution.py:447
  21.0 0.4 shard_map.70
  21.4 7.1 %collective-permute-start.4 = (f32[5,32,128]{2,1,0:T(8,128)S(1)}, f32[5,32,128]{2,1,0:T(8,128)S(1)}, u32[]{:S(2)}, u32[]{:S(2)}) collective-permute-start(f32[5,32,128]{2,1,0:T(8,128)S(1)} %get-tuple-element.24), channel_id=1, source_target_pairs={{1,2},{2,1},{3,4},{4,3},{5,6},{6,5},{7,8},{8,7},{9,10},{10,9},{11,... | collective-permute-start | bytes 245768 | tf_op jit(solution)/shard_map/ppermute | solution.py:472
  28.5 2.0 %shard_map.71 = (f32[5,8,16,128]{3,2,1,0:T(8,128)S(1)}, f32[14,8,128]{2,1,0:T(8,128)S(1)}, f32[4,5,32,128]{3,2,1,0:T(8,128)S(1)}) custom-call(f32[4,18,32,128]{3,2,1,0:T(8,128)S(1)} %get-tuple-element.21.wide, f32[4,8,128]{2,1,0:T(8,128)S(1)} %get-tuple-element.22.theta), custom_call_target="tpu_custom_call" | custom-call | flops 20000000 | bytes 1000000 | tf_op jit(solution)/shard_map/pallas_call | solution.py:480
  30.6 1.9 %all-gather = f32[10,32,128]{2,1,0:T(8,128)S(1)} all-gather(f32[5,32,128]{2,1,0:T(8,128)S(1)} %get-tuple-element.25), channel_id=2, replica_groups=mesh['gx'=4,'gy'=8,'gz_0'=8,'gz_1'=2] {'gz_1'}, dimensions={0}, use_global_device_ids=true | all-gather | bytes 245760 | tf_op jit(solution)/shard_map/all_gather | solution.py:477
  32.5 0.0 collective-permute-done.4.far
  32.5 1.4 %shard_map.72 = (f32[5,5,16,128]{3,2,1,0:T(8,128)S(1)}, f32[32,1,128]{2,1,0:T(1,128)S(1)}) custom-call(s32[1]{0:T(128)} %bitcast.core, f32[4,5,32,128]{3,2,1,0:T(8,128)S(1)} %get-tuple-element.23.ends, f32[5,32,128]{2,1,0:T(8,128)S(1)} %collective-permute-done.4.far, f32[2,5,32,128]{3,2,1,0:T(8,128)S(1)} %bitcast.2, ...), custom_call_target="tpu_custom_call" | custom-call | flops 5000000 | bytes 1000000 | tf_op jit(solution)/shard_map/pallas_call | solution.py:489
  33.9 20.1 %all_to_all.10.parts = f32[32,1,128]{2,1,0:T(1,128)S(1)} all-to-all(f32[32,1,128]{2,1,0:T(1,128)S(1)} %get-tuple-element.27), channel_id=1, replica_groups=mesh['gx'=4,'gy'=8,'gz_0'=8,'gz_1'=2] {'gx','gz_0'}, dimensions={0} | all-to-all | bytes 32768 | tf_op jit(solution)/shard_map/all_to_all | solution.py:452
  54.1 15.7 %all_to_all.11.parts = f32[16,1,128]{2,1,0:T(1,128)S(1)} all-to-all(f32[16,1,128]{2,1,0:T(1,128)S(1)} %shard_map.73), channel_id=1, replica_groups=mesh['gx'=4,'gy'=8,'gz_0'=8,'gz_1'=2] {'gy','gz_1'}, dimensions={0} | all-to-all | bytes 16384 | tf_op jit(solution)/shard_map/all_to_all | solution.py:452
  69.8 1.6 %shard_map.74 = (f32[8,16,128]{2,1,0:T(8,128)}, f32[8,16,128]{2,1,0:T(8,128)}) custom-call(f32[16,1,128]{2,1,0:T(1,128)S(1)} %all_to_all.11.parts, f32[5,8,16,128]{3,2,1,0:T(8,128)S(1)} %get-tuple-element.28.basis, f32[5,5,16,128]{3,2,1,0:T(8,128)S(1)} %get-tuple-element.29.end_basis, f32[4,8,16,128]{3,2,1,0:T(8,128)S(1)} %get-tuple-element.16.fields, ...), custom_call_target="tpu_custom_call" | custom-call | flops 100000 | bytes 1000000 | tf_op jit(solution)/shard_map/pallas_call | solution.py:499
  (2 shorter events, 0.1 us)
Async XLA Ops:
  1.7 5.9 %collective-permute-start = (f32[17,16,128]{2,1,0:T(8,128)S(1)}, f32[17,16,128]{2,1,0:T(8,128)S(1)}, u32[]{:S(2)}, u32[]{:S(2)}) collective-permute-start(f32[17,16,128]{2,1,0:T(8,128)S(1)} %get-tuple-element.17), channel_id=1, source_target_pairs={{0,128},{128,256},{256,384},{1,129},{129,257},{257,385},{2,130},{1... | collective-permute-start | bytes 417800 | tf_op jit(solution)/shard_map/ppermute | solution.py:446
  5.7 5.8 %collective-permute-start.1 = (f32[17,16,128]{2,1,0:T(8,128)S(1)}, f32[17,16,128]{2,1,0:T(8,128)S(1)}, u32[]{:S(2)}, u32[]{:S(2)}) collective-permute-start(f32[17,16,128]{2,1,0:T(8,128)S(1)} %get-tuple-element.18), channel_id=1, source_target_pairs={{128,0},{256,128},{384,256},{129,1},{257,129},{385,257},{130,2},{2... | collective-permute-start | bytes 417800 | tf_op jit(solution)/shard_map/ppermute | solution.py:447
  11.5 5.7 %collective-permute-start.2 = (f32[288,128]{1,0:T(8,128)S(1)}, f32[288,128]{1,0:T(8,128)S(1)}, u32[]{:S(2)}, u32[]{:S(2)}) collective-permute-start(f32[288,128]{1,0:T(8,128)S(1)} %get-tuple-element.19), channel_id=1, source_target_pairs={{0,16},{16,32},{32,48},{48,64},{64,80},{80,96},{96,112},{1,17},{17... | collective-permute-start | bytes 442376 | tf_op jit(solution)/shard_map/ppermute | solution.py:446
  15.1 5.9 %collective-permute-start.3 = (f32[288,128]{1,0:T(8,128)S(1)}, f32[288,128]{1,0:T(8,128)S(1)}, u32[]{:S(2)}, u32[]{:S(2)}) collective-permute-start(f32[288,128]{1,0:T(8,128)S(1)} %get-tuple-element.20), channel_id=1, source_target_pairs={{16,0},{32,16},{48,32},{64,48},{80,64},{96,80},{112,96},{17,1},{33... | collective-permute-start | bytes 442376 | tf_op jit(solution)/shard_map/ppermute | solution.py:447
  21.4 11.1 %collective-permute-start.4 = (f32[5,32,128]{2,1,0:T(8,128)S(1)}, f32[5,32,128]{2,1,0:T(8,128)S(1)}, u32[]{:S(2)}, u32[]{:S(2)}) collective-permute-start(f32[5,32,128]{2,1,0:T(8,128)S(1)} %get-tuple-element.24), channel_id=1, source_target_pairs={{1,2},{2,1},{3,4},{4,3},{5,6},{6,5},{7,8},{8,7},{9,10},{10,9},{11,... | collective-permute-start | bytes 245768 | tf_op jit(solution)/shard_map/ppermute | solution.py:472

commit v6 on v5

--- a/solution.py
+++ b/solution.py
@@ -7,7 +7,7 @@
 from jax.sharding import PartitionSpec as P
 
 ITERS = 4
-GZ = ("gz_0", "gz_1")
+GX, GY, GZ = (("gx_0", "gx_1"), ("gy_0", "gy_1"), ("gz_0", "gz_1"))
 F32 = jnp.float32
 X, Y, Z = 8, 16, 128
 HALO = ITERS + 1
@@ -46,7 +46,7 @@
 
 
 def prepare(
-    opening_at, source_at, category_at, flags_at, table_at, fields, low, high, theta,
+    place_x, opening_at, source_at, category_at, flags_at, table_at, fields, near, far, theta,
     opening, source, category, flags, table, arrived,
 ):
     copies = [
@@ -77,41 +77,51 @@
         values = (cond, start, 2.0 * source[p] - 6.0 * flag * start, flag)
         for k, v in enumerate(values):
             fields[k, p] = v
-            if p < WIDTHS[k]:
-                low[AT_X[k] + p] = v
-            if p >= X - WIDTHS[k]:
-                high[AT_X[k] + p - (X - WIDTHS[k])] = v
-
-
-def plane(fields, left, right, k, p):
+    first = place_x[0] == 0
+    for k, w in enumerate(WIDTHS):
+        for n in range(w):
+            low, high = fields[k, n], fields[k, X - w + n]
+            near[AT_X[k] + n] = jnp.where(first, high, low)
+            far[AT_X[k] + n] = jnp.where(first, low, high)
+
+
+def halo(place, far, pair, at, lower):
+    far_side = (place == 0) if lower else (place == 1)
+    return jnp.where(far_side, far[at], pair[(1 - place, *at)])
+
+
+def plane(place, fields, far, pair, k, p, rows=slice(None)):
     if p < HALO:
-        return left, (AT_X[k] + p - (HALO - WIDTHS[k]),)
+        return halo(place, far, pair, (AT_X[k] + p - (HALO - WIDTHS[k]), rows), True)
     if p < HALO + X:
-        return fields, (k, p - HALO)
-    return right, (AT_X[k] + p - HALO - X,)
-
-
-def slabs_y(fields, left, right, low, high):
+        return fields[k, p - HALO, rows]
+    return halo(place, far, pair, (AT_X[k] + p - HALO - X, rows), False)
+
+
+def slabs_y(place_x, place_y, fields, far_x, pair_x, near, far):
+    first = place_y[0] == 0
     for k, w in enumerate(WIDTHS):
         for n, p in enumerate(planes_of(k)):
-            ref, at = plane(fields, left, right, k, p)
             to = pl.ds(AT_Y[k] + w * n, w)
-            low[to] = ref[(*at, pl.ds(0, w))]
-            high[to] = ref[(*at, pl.ds(Y - w, w))]
-
-
-def assemble(core, fields, left, right, below, above, wide, near, far):
+            low, high = (
+                plane(place_x[0], fields, far_x, pair_x, k, p, pl.ds(at, w)) for at in (0, Y - w)
+            )
+            near[to] = jnp.where(first, high, low)
+            far[to] = jnp.where(first, low, high)
+
+
+def assemble(place_x, place_y, place_z, fields, far_x, pair_x, far_y, pair_y, wide, near, far):
     lane = lax.broadcasted_iota(jnp.int32, (ROWS, Z), 1)
-    first_core = core[0] == 0
+    first_core = place_z[0] == 0
     nothing = jnp.zeros((8, Z), F32)
     for k, w in enumerate(WIDTHS):
         for n, p in enumerate(planes_of(k)):
-            ref, at = plane(fields, left, right, k, p)
+            at = (pl.ds(AT_Y[k] + w * n, w),)
             wide[k, p, 0:TOP] = nothing
             wide[k, p, TOP + Y : ROWS] = nothing
-            wide[k, p, TOP : TOP + Y] = ref[at]
-            wide[k, p, TOP - w : TOP] = below[AT_Y[k] + w * n : AT_Y[k] + w * (n + 1)]
-            wide[k, p, TOP + Y : TOP + Y + w] = above[AT_Y[k] + w * n : AT_Y[k] + w * (n + 1)]
+            wide[k, p, TOP : TOP + Y] = plane(place_x[0], fields, far_x, pair_x, k, p)
+            wide[k, p, TOP - w : TOP] = halo(place_y[0], far_y, pair_y, at, True)
+            wide[k, p, TOP + Y : TOP + Y + w] = halo(place_y[0], far_y, pair_y, at, False)
     for q in range(PER_GROUP):
         low = jnp.zeros((ROWS, Z), F32)
         high = low
@@ -229,18 +239,14 @@
             ends[k, q] = out
 
 
-def edges(core, ends, far, chip, theta, inner_sums, basis, dots, cells, cx, mid, slope, diag, inside, va, vb, ua, ub, stack):
+def edges(place_z, ends, far, chip, theta, inner_sums, basis, dots, cells, cx, mid, slope, diag, inside, va, vb, ua, ub, stack):
     lane = lax.broadcasted_iota(jnp.int32, (ROWS, Z), 1)
     place = lane % GROUP
-    first_core = core[0] == 0
-    partner = 1 - core[0]
     slots = mid.shape[0]
     slot = [0]
 
     for q in range(PER_GROUP):
-        near, other = chip[partner, q], far[q]
-        below = jnp.where(first_core, other, near)
-        above = jnp.where(first_core, near, other)
+        below, above = (halo(place_z[0], far, chip, (q,), lower) for lower in (True, False))
         for k in range(4):
             low = pltpu.roll(below, (LOW_AT - AT_X[k]) % Z, 1)
             high = pltpu.roll(above, (HIGH_AT - AT_X[k]) % Z, 1)
@@ -441,11 +447,10 @@
             mismatch[p, rows] = both[1]
 
 
-def both_ways(low, high, axis):
-    ends = lax.axis_size(axis) - 1
-    from_below = lax.ppermute(high, axis, [(i, i + 1) for i in range(ends)])
-    from_above = lax.ppermute(low, axis, [(i + 1, i) for i in range(ends)])
-    return from_below, from_above
+def trade(near, far, axes):
+    ends = lax.axis_size(axes) - 1
+    others = [p for i in range(1, ends, 2) for p in ((i, i + 1), (i + 1, i))]
+    return lax.ppermute(far, axes, others), lax.all_gather(near, axes[1], axis=0)
 
 
 def exchange(copies, axes):
@@ -454,27 +459,30 @@
 
 def body(opening, source, category, table, flags):
     brick = (X, Y, Z)
+    place_x, place_y, place_z = (lax.axis_index(axes[1]).reshape(1) for axes in (GX, GY, GZ))
     whole = pltpu.VMEM(brick, jnp.int32)
-    fields, low, high, theta = call(
+    fields, near, far, theta = call(
         prepare,
-        [HBM] * 5,
+        [SMEM] + [HBM] * 5,
         [(4, *brick), (SLAB_X, Y, Z), (SLAB_X, Y, Z), (ITERS, 8, Z)],
         [brick, brick, whole, whole, pltpu.SMEM(table.shape, F32), pltpu.SemaphoreType.DMA((5,))],
-    )(*(pltpu.with_memory_space_constraint(a, pltpu.HBM) for a in (opening, source, category, flags, table)))
-    left, right = both_ways(low, high, "gx")
-    low, high = call(slabs_y, [VMEM] * 3, [(SLAB_Y, Z)] * 2)(fields, left, right)
-    below, above = both_ways(low, high, "gy")
-    core = lax.axis_index(GZ[1]).reshape(1)
+    )(
+        place_x,
+        *(
+            pltpu.with_memory_space_constraint(a, pltpu.HBM)
+            for a in (opening, source, category, flags, table)
+        ),
+    )
+    by_x = trade(near, far, GX)
+    near, far = call(slabs_y, [SMEM] * 2 + [VMEM] * 3, [(SLAB_Y, Z)] * 2)(
+        place_x, place_y, fields, *by_x
+    )
+    by_y = trade(near, far, GY)
     packed = (PER_GROUP, ROWS, Z)
-    wide, near, far = call(assemble, [SMEM] + [VMEM] * 5, [(4, PLANES, ROWS, Z), packed, packed])(
-        core, fields, left, right, below, above
-    )
-    far = lax.ppermute(
-        far,
-        GZ,
-        [p for i in range(1, lax.axis_size(GZ) - 1, 2) for p in ((i, i + 1), (i + 1, i))],
-    )
-    chip = lax.all_gather(near, GZ[1], axis=0)
+    wide, near, far = call(assemble, [SMEM] * 3 + [VMEM] * 5, [(4, PLANES, ROWS, Z), packed, packed])(
+        place_x, place_y, place_z, fields, *by_x, *by_y
+    )
+    far, chip = trade(near, far, GZ)
     sided = (PLANES, ROWS, Z)
     middle = (3, PLANES, ROWS + 16, Z)
     basis, sums, ends = call(
@@ -485,14 +493,14 @@
         flops=20000000,
         vmem=12,
     )(wide, theta)
-    first, second = ("gx", "gz_0"), ("gy", "gz_1")
+    first, second = (*GX, "gz_0"), (*GY, "gz_1")
     end_basis, dots = call(
         edges,
         [SMEM] + [VMEM] * 5,
         [(ITERS + 1, PER_GROUP, Y, Z), (lax.axis_size(first), 1, Z)],
         [(4, *packed), packed, (3, PER_GROUP, ROWS + 16, Z)] + [packed] * 7 + [(Z, Z)],
         flops=5000000,
-    )(core, ends, far, chip, theta, sums)
+    )(place_z, ends, far, chip, theta, sums)
     parts = exchange(dots, first)
     (copies,) = call(relay, [VMEM], [(lax.axis_size(second), 1, Z)])(parts)
     parts = exchange(copies, second)
@@ -503,9 +511,9 @@
 
 
 def solution(mesh):
-    shape = mesh.devices.shape
-    split = Mesh(mesh.devices.reshape(shape[0], shape[1], shape[2] // 2, 2), ("gx", "gy", *GZ))
-    spec = P("gx", "gy", GZ)
+    pairs = [n for size in mesh.devices.shape for n in (size // 2, 2)]
+    split = Mesh(mesh.devices.reshape(pairs), (*GX, *GY, *GZ))
+    spec = P(GX, GY, GZ)
     return jax.shard_map(
         body, mesh=split, in_specs=(spec, spec, spec, P(), spec), out_specs=(spec, spec), check_vma=False
     )

time: 71.7 us -> 67.4 us (0.940)
  blocking collectives: 37.8 us -> 51.9 us
  starting transfers between devices: 17.2 us -> 7.91 us
  waiting for transfers between devices: 9.08 us -> 0.01 us
    all_gather x1 -> x3, blocking collectives: 1.92 us -> 17.2 us  [trade(): lax.all_gather(near, axes[1], axis=0)]
    ppermute x5 -> x3, starting transfers between devices: 17.2 us -> 7.91 us  [trade(): lax.ppermute(far, axes, others)]
    ppermute x5 -> x3, waiting for transfers between devices: 9.08 us -> 0.01 us  [trade(): lax.ppermute(far, axes, others)]
    all_to_all x2, blocking collectives: 35.9 us -> 34.7 us  [exchange(): return lax.all_to_all(copies, axes, split_axis=0, concat_axis=0, tiled=True)]
  transfers between devices with their start and end apart: 5 -> 3, of which waited for: 4 -> 0; matrix products, arithmetic and copies ran while one was open for 0% -> 0% of each run, Pallas kernels for 3% -> 3%
where the time goes in v6:
time: 67.4 us; the launch traced here: 67.1 us
  blocking collectives  51.9 us (77%)
  starting transfers between devices  7.91 us (12%)
  Pallas kernels  6.56 us (10%)
  between operations  0.72 us (1%)
    all_to_all x2, blocking collectives, exchange(): return lax.all_to_all(copies, axes, split_axis=0, concat_axis=0, tiled=True)  34.7 us
    all_gather x3, blocking collectives, trade(): lax.all_gather(near, axes[1], axis=0)  17.2 us
    ppermute x3, starting transfers between devices, trade(): lax.ppermute(far, axes, others)  7.91 us
    pallas_call x1, Pallas kernels, body(): call(interior, [VMEM] * 2, [(ITERS + 1, *brick), (len(PAIRS), 8, Z), (4,...  2.05 us
    pallas_call x1, Pallas kernels, body(): call(finish, [VMEM] * 5, [brick, brick])  1.56 us
    pallas_call x1, Pallas kernels, body(): call(edges, [SMEM] + [VMEM] * 5, [(ITERS + 1, PER_GROUP, Y, Z), (lax.axis...  1.38 us
  transfers between devices with their start and end apart: 3, of which 0 were waited for; matrix products, arithmetic and copies ran while one was open for 0% of the time, Pallas kernels for 3%

profile of v6, /device:TPU:1, one launch (start us, length us, event | category | flops | bytes accessed | tf_op | source)
XLA Modules:
  0.0 67.1 jit_solution(12685003377419251624)
XLA Ops:
  0.6 1.1 %shard_map.68 = (f32[4,8,16,128]{3,2,1,0:T(8,128)S(1)}, f32[17,16,128]{2,1,0:T(8,128)S(1)}, f32[17,16,128]{2,1,0:T(8,128)S(1)}, f32[4,8,128]{2,1,0:T(8,128)S(1)}) custom-call(s32[1]{0:T(128)} %bitcast.1.place_x, f32[8,16,128]{2,1,0:T(8,128)} %opening_at.1, f32[8,16,128]{2,1,0:T(8,128)} %source_at.1, s32[8,16,128]{2,1,0:T(8,128)} %category_at.1, ...), custom_call_target="tpu_custom_call" | custom-call | flops 100000 | bytes 1000000 | tf_op jit(solution)/shard_map/pallas_call | solution.py:464
  1.7 0.7 collective-permute-start
  2.4 7.6 %all-gather = f32[34,16,128]{2,1,0:T(8,128)S(1)} all-gather(f32[17,16,128]{2,1,0:T(8,128)S(1)} %get-tuple-element.18), channel_id=2, replica_groups=mesh['gx_0'=2,'gx_1'=2,'gy_0'=4,'gy_1'=2,'gz_0'=8,'gz_1'=2] {'gx_1'}, dimensions={0}, use_global_device_ids=true | all-gather | bytes 417792 | tf_op jit(solution)/shard_map/all_gather | solution.py:453
  10.0 0.0 collective-permute-done.far_x
  10.0 0.1 shard_map.69
  10.1 0.7 collective-permute-start.1
  10.7 7.7 %all-gather.1 = f32[576,128]{1,0:T(8,128)S(1)} all-gather(f32[288,128]{1,0:T(8,128)S(1)} %get-tuple-element.20), channel_id=3, replica_groups=mesh['gx_0'=2,'gx_1'=2,'gy_0'=4,'gy_1'=2,'gz_0'=8,'gz_1'=2] {'gy_1'}, dimensions={0}, use_global_device_ids=true | all-gather | bytes 442368 | tf_op jit(solution)/shard_map/all_gather | solution.py:453
  18.4 0.0 collective-permute-done.1.far_y
  18.4 0.4 shard_map.70
  18.8 6.6 %collective-permute-start.2 = (f32[5,32,128]{2,1,0:T(8,128)S(1)}, f32[5,32,128]{2,1,0:T(8,128)S(1)}, u32[]{:S(2)}, u32[]{:S(2)}) collective-permute-start(f32[5,32,128]{2,1,0:T(8,128)S(1)} %get-tuple-element.24), channel_id=1, source_target_pairs={{1,2},{2,1},{3,4},{4,3},{5,6},{6,5},{7,8},{8,7},{9,10},{10,9},{11,... | collective-permute-start | bytes 245768 | tf_op jit(solution)/shard_map/ppermute | solution.py:453
  25.4 2.1 %shard_map.71 = (f32[5,8,16,128]{3,2,1,0:T(8,128)S(1)}, f32[14,8,128]{2,1,0:T(8,128)S(1)}, f32[4,5,32,128]{3,2,1,0:T(8,128)S(1)}) custom-call(f32[4,18,32,128]{3,2,1,0:T(8,128)S(1)} %get-tuple-element.21.wide, f32[4,8,128]{2,1,0:T(8,128)S(1)} %get-tuple-element.22.theta), custom_call_target="tpu_custom_call" | custom-call | flops 20000000 | bytes 1000000 | tf_op jit(solution)/shard_map/pallas_call | solution.py:488
  27.4 1.9 %all-gather.2 = f32[10,32,128]{2,1,0:T(8,128)S(1)} all-gather(f32[5,32,128]{2,1,0:T(8,128)S(1)} %get-tuple-element.25), channel_id=4, replica_groups=mesh['gx_0'=2,'gx_1'=2,'gy_0'=4,'gy_1'=2,'gz_0'=8,'gz_1'=2] {'gz_1'}, dimensions={0}, use_global_device_ids=true | all-gather | bytes 245760 | tf_op jit(solution)/shard_map/all_gather | solution.py:453
  29.4 0.0 collective-permute-done.2.far
  29.4 1.4 %shard_map.72 = (f32[5,5,16,128]{3,2,1,0:T(8,128)S(1)}, f32[32,1,128]{2,1,0:T(1,128)S(1)}) custom-call(s32[1]{0:T(128)} %bitcast.place_z, f32[4,5,32,128]{3,2,1,0:T(8,128)S(1)} %get-tuple-element.23.ends, f32[5,32,128]{2,1,0:T(8,128)S(1)} %collective-permute-done.2.far, f32[2,5,32,128]{3,2,1,0:T(8,128)S(1)} %bitcast.9, ...), custom_call_target="tpu_custom_call" | custom-call | flops 5000000 | bytes 1000000 | tf_op jit(solution)/shard_map/pallas_call | solution.py:497
  30.8 19.7 %all_to_all.10.parts = f32[32,1,128]{2,1,0:T(1,128)S(1)} all-to-all(f32[32,1,128]{2,1,0:T(1,128)S(1)} %get-tuple-element.27), channel_id=1, replica_groups=mesh['gx_0'=2,'gx_1'=2,'gy_0'=4,'gy_1'=2,'gz_0'=8,'gz_1'=2] {'gx_0','gx_..., dimensions={0} | all-to-all | bytes 32768 | tf_op jit(solution)/shard_map/all_to_all | solution.py:457
  50.6 15.0 %all_to_all.11.parts = f32[16,1,128]{2,1,0:T(1,128)S(1)} all-to-all(f32[16,1,128]{2,1,0:T(1,128)S(1)} %shard_map.73), channel_id=1, replica_groups=mesh['gx_0'=2,'gx_1'=2,'gy_0'=4,'gy_1'=2,'gz_0'=8,'gz_1'=2] {'gy_0','gy_..., dimensions={0} | all-to-all | bytes 16384 | tf_op jit(solution)/shard_map/all_to_all | solution.py:457
  65.5 1.6 %shard_map.74 = (f32[8,16,128]{2,1,0:T(8,128)}, f32[8,16,128]{2,1,0:T(8,128)}) custom-call(f32[16,1,128]{2,1,0:T(1,128)S(1)} %all_to_all.11.parts, f32[5,8,16,128]{3,2,1,0:T(8,128)S(1)} %get-tuple-element.28.basis, f32[5,5,16,128]{3,2,1,0:T(8,128)S(1)} %get-tuple-element.29.end_basis, f32[4,8,16,128]{3,2,1,0:T(8,128)S(1)} %get-tuple-element.16.fields, ...), custom_call_target="tpu_custom_call" | custom-call | flops 100000 | bytes 1000000 | tf_op jit(solution)/shard_map/pallas_call | solution.py:507
  (1 shorter events, 0.0 us)
Async XLA Ops:
  1.7 8.3 %collective-permute-start = (f32[17,16,128]{2,1,0:T(8,128)S(1)}, f32[17,16,128]{2,1,0:T(8,128)S(1)}, u32[]{:S(2)}, u32[]{:S(2)}) collective-permute-start(f32[17,16,128]{2,1,0:T(8,128)S(1)} %get-tuple-element.17), channel_id=1, source_target_pairs={{128,256},{256,128},{129,257},{257,129},{130,258},{258,130},{131,2... | collective-permute-start | bytes 417800 | tf_op jit(solution)/shard_map/ppermute | solution.py:453
  10.1 8.4 %collective-permute-start.1 = (f32[288,128]{1,0:T(8,128)S(1)}, f32[288,128]{1,0:T(8,128)S(1)}, u32[]{:S(2)}, u32[]{:S(2)}) collective-permute-start(f32[288,128]{1,0:T(8,128)S(1)} %get-tuple-element.19), channel_id=1, source_target_pairs={{16,32},{32,16},{48,64},{64,48},{80,96},{96,80},{17,33},{33,17},{4... | collective-permute-start | bytes 442376 | tf_op jit(solution)/shard_map/ppermute | solution.py:453
  18.8 10.6 %collective-permute-start.2 = (f32[5,32,128]{2,1,0:T(8,128)S(1)}, f32[5,32,128]{2,1,0:T(8,128)S(1)}, u32[]{:S(2)}, u32[]{:S(2)}) collective-permute-start(f32[5,32,128]{2,1,0:T(8,128)S(1)} %get-tuple-element.24), channel_id=1, source_target_pairs={{1,2},{2,1},{3,4},{4,3},{5,6},{6,5},{7,8},{8,7},{9,10},{10,9},{11,... | collective-permute-start | bytes 245768 | tf_op jit(solution)/shard_map/ppermute | solution.py:453

commit v7 on v6

--- a/solution.py
+++ b/solution.py
@@ -375,38 +375,42 @@
     return quick(p, e + (a[0] * b[1] + a[1] * b[0]))
 
 
-def over(a, b):
-    q = a[0] / b[0]
-    none = jnp.zeros_like(q)
-    rest = minus(a, times((q, none), b))
-    return quick(q, rest[0] / b[0])
-
-
-def conjugate_gradients(gram, theta):
+def reciprocal(a):
+    q = 1.0 / a[0]
+    qh, ql = halves(q)
+    ah, al = halves(a[0])
+    p = q * a[0]
+    rest = ((1.0 - p) - (((qh * ah - p) + qh * al + ql * ah) + ql * al)) - q * a[1]
+    return quick(q, q * rest)
+
+
+def coefficients(gram, theta):
     none = jnp.zeros_like(theta[0])
-    zero, one = (none, none), (none + 1.0, none)
     shift = [(t, none) for t in theta]
-
-    def along(k, vector):
-        total = times(gram[k, 0], vector[0])
-        for j in range(1, len(vector)):
-            total = plus(total, times(gram[k, j], vector[j]))
-        return total
-
-    r, p = [one], [one]
-    y = [zero] * ITERS
-    rr = gram[0, 0]
-    for k in range(ITERS):
-        image = [times(shift[i], p[i]) for i in range(k + 1)] + [zero]
-        image = [image[0]] + [plus(image[i], p[i - 1]) for i in range(1, k + 2)]
-        step = over(rr, times(p[k], along(k, image)))
-        y = [plus(y[i], times(step, p[i])) if i <= k else y[i] for i in range(ITERS)]
-        r = [minus(r[i] if i <= k else zero, times(step, image[i])) for i in range(k + 2)]
-        if k + 1 < ITERS:
-            new = times(r[k + 1], along(k + 1, r))
-            ratio = over(new, rr)
-            p = [plus(r[i], times(ratio, p[i])) if i <= k else r[i] for i in range(k + 2)]
-            rr = new
+    system = [
+        [plus(gram[i, j + 1], times(shift[j], gram[i, j])) for j in range(i + 1)]
+        for i in range(ITERS)
+    ]
+    right = [gram[i, 0] for i in range(ITERS)]
+    lower, inverse = {}, []
+    for j in range(ITERS):
+        inverse.append(reciprocal(system[j][j]))
+        for i in range(j + 1, ITERS):
+            lower[i, j] = times(system[i][j], inverse[j])
+        for i in range(j + 1, ITERS):
+            for k in range(j + 1, i + 1):
+                system[i][k] = minus(system[i][k], times(lower[i, j], system[k][j]))
+            right[i] = minus(right[i], times(lower[i, j], right[j]))
+    y = [None] * ITERS
+    for i in reversed(range(ITERS)):
+        y[i] = times(right[i], inverse[i])
+        for k in reversed(range(i + 1, ITERS)):
+            y[i] = minus(y[i], times(lower[k, i], y[k]))
+    r = [minus((none + 1.0, none), times(shift[0], y[0]))]
+    for k in range(1, ITERS):
+        total = plus(y[k - 1], times(shift[k], y[k]))
+        r.append((-total[0], -total[1]))
+    r.append((-y[-1][0], -y[-1][1]))
     return [a[0] * (1.0 / SCALE) for a in y], [a[0] for a in r]
 
 
@@ -418,7 +422,7 @@
         gram[i, j] = gram[j, i] = quick(
             *(jnp.broadcast_to(v[0:1, n : n + 1], (8, Z)) for v in (total, rest))
         )
-    y, r = conjugate_gradients(gram, [theta[k] for k in range(ITERS)])
+    y, r = coefficients(gram, [theta[k] for k in range(ITERS)])
 
     def combine(v):
         x, m = y[0] * v[0], r[ITERS] * v[ITERS]

time: 67.4 us -> 67 us (level)
  no operation moved by 1% of the time
where the time goes in v7:
time: 67 us; the launch traced here: 66.7 us
  blocking collectives  51.9 us (77%)
  starting transfers between devices  7.91 us (12%)
  Pallas kernels  6.19 us (9%)
  between operations  0.72 us (1%)
    all_to_all x2, blocking collectives, exchange(): return lax.all_to_all(copies, axes, split_axis=0, concat_axis=0, tiled=True)  34.7 us
    all_gather x3, blocking collectives, trade(): lax.all_gather(near, axes[1], axis=0)  17.2 us
    ppermute x3, starting transfers between devices, trade(): lax.ppermute(far, axes, others)  7.91 us
    pallas_call x1, Pallas kernels, body(): call(interior, [VMEM] * 2, [(ITERS + 1, *brick), (len(PAIRS), 8, Z), (4,...  2.05 us
    pallas_call x1, Pallas kernels, body(): call(edges, [SMEM] + [VMEM] * 5, [(ITERS + 1, PER_GROUP, Y, Z), (lax.axis...  1.38 us
  transfers between devices with their start and end apart: 3, of which 0 were waited for; matrix products, arithmetic and copies ran while one was open for 0% of the time, Pallas kernels for 3%

profile of v7, /device:TPU:1, one launch (start us, length us, event | category | flops | bytes accessed | tf_op | source)
XLA Modules:
  0.0 66.7 jit_solution(18438164307041587890)
XLA Ops:
  0.6 1.1 %shard_map.68 = (f32[4,8,16,128]{3,2,1,0:T(8,128)S(1)}, f32[17,16,128]{2,1,0:T(8,128)S(1)}, f32[17,16,128]{2,1,0:T(8,128)S(1)}, f32[4,8,128]{2,1,0:T(8,128)S(1)}) custom-call(s32[1]{0:T(128)} %bitcast.1.place_x, f32[8,16,128]{2,1,0:T(8,128)} %opening_at.1, f32[8,16,128]{2,1,0:T(8,128)} %source_at.1, s32[8,16,128]{2,1,0:T(8,128)} %category_at.1, ...), custom_call_target="tpu_custom_call" | custom-call | flops 100000 | bytes 1000000 | tf_op jit(solution)/shard_map/pallas_call | solution.py:468
  1.7 0.7 %collective-permute-start = (f32[17,16,128]{2,1,0:T(8,128)S(1)}, f32[17,16,128]{2,1,0:T(8,128)S(1)}, u32[]{:S(2)}, u32[]{:S(2)}) collective-permute-start(f32[17,16,128]{2,1,0:T(8,128)S(1)} %get-tuple-element.17), channel_id=1, source_target_pairs={{128,256},{256,128},{129,257},{257,129},{130,258},{258,130},{131,2... | collective-permute-start | bytes 417800 | tf_op jit(solution)/shard_map/ppermute | solution.py:457
  2.4 7.6 %all-gather = f32[34,16,128]{2,1,0:T(8,128)S(1)} all-gather(f32[17,16,128]{2,1,0:T(8,128)S(1)} %get-tuple-element.18), channel_id=2, replica_groups=mesh['gx_0'=2,'gx_1'=2,'gy_0'=4,'gy_1'=2,'gz_0'=8,'gz_1'=2] {'gx_1'}, dimensions={0}, use_global_device_ids=true | all-gather | bytes 417792 | tf_op jit(solution)/shard_map/all_gather | solution.py:457
  10.0 0.0 collective-permute-done.far_x
  10.0 0.1 shard_map.69
  10.1 0.7 %collective-permute-start.1 = (f32[288,128]{1,0:T(8,128)S(1)}, f32[288,128]{1,0:T(8,128)S(1)}, u32[]{:S(2)}, u32[]{:S(2)}) collective-permute-start(f32[288,128]{1,0:T(8,128)S(1)} %get-tuple-element.19), channel_id=1, source_target_pairs={{16,32},{32,16},{48,64},{64,48},{80,96},{96,80},{17,33},{33,17},{4... | collective-permute-start | bytes 442376 | tf_op jit(solution)/shard_map/ppermute | solution.py:457
  10.7 7.7 %all-gather.1 = f32[576,128]{1,0:T(8,128)S(1)} all-gather(f32[288,128]{1,0:T(8,128)S(1)} %get-tuple-element.20), channel_id=3, replica_groups=mesh['gx_0'=2,'gx_1'=2,'gy_0'=4,'gy_1'=2,'gz_0'=8,'gz_1'=2] {'gy_1'}, dimensions={0}, use_global_device_ids=true | all-gather | bytes 442368 | tf_op jit(solution)/shard_map/all_gather | solution.py:457
  18.4 0.0 collective-permute-done.1.far_y
  18.4 0.4 shard_map.70
  18.8 6.6 %collective-permute-start.2 = (f32[5,32,128]{2,1,0:T(8,128)S(1)}, f32[5,32,128]{2,1,0:T(8,128)S(1)}, u32[]{:S(2)}, u32[]{:S(2)}) collective-permute-start(f32[5,32,128]{2,1,0:T(8,128)S(1)} %get-tuple-element.24), channel_id=1, source_target_pairs={{1,2},{2,1},{3,4},{4,3},{5,6},{6,5},{7,8},{8,7},{9,10},{10,9},{11,... | collective-permute-start | bytes 245768 | tf_op jit(solution)/shard_map/ppermute | solution.py:457
  25.4 2.1 %shard_map.71 = (f32[5,8,16,128]{3,2,1,0:T(8,128)S(1)}, f32[14,8,128]{2,1,0:T(8,128)S(1)}, f32[4,5,32,128]{3,2,1,0:T(8,128)S(1)}) custom-call(f32[4,18,32,128]{3,2,1,0:T(8,128)S(1)} %get-tuple-element.21.wide, f32[4,8,128]{2,1,0:T(8,128)S(1)} %get-tuple-element.22.theta), custom_call_target="tpu_custom_call" | custom-call | flops 20000000 | bytes 1000000 | tf_op jit(solution)/shard_map/pallas_call | solution.py:492
  27.4 1.9 %all-gather.2 = f32[10,32,128]{2,1,0:T(8,128)S(1)} all-gather(f32[5,32,128]{2,1,0:T(8,128)S(1)} %get-tuple-element.25), channel_id=4, replica_groups=mesh['gx_0'=2,'gx_1'=2,'gy_0'=4,'gy_1'=2,'gz_0'=8,'gz_1'=2] {'gz_1'}, dimensions={0}, use_global_device_ids=true | all-gather | bytes 245760 | tf_op jit(solution)/shard_map/all_gather | solution.py:457
  29.4 0.0 collective-permute-done.2.far
  29.4 1.4 %shard_map.72 = (f32[5,5,16,128]{3,2,1,0:T(8,128)S(1)}, f32[32,1,128]{2,1,0:T(1,128)S(1)}) custom-call(s32[1]{0:T(128)} %bitcast.place_z, f32[4,5,32,128]{3,2,1,0:T(8,128)S(1)} %get-tuple-element.23.ends, f32[5,32,128]{2,1,0:T(8,128)S(1)} %collective-permute-done.2.far, f32[2,5,32,128]{3,2,1,0:T(8,128)S(1)} %bitcast.9, ...), custom_call_target="tpu_custom_call" | custom-call | flops 5000000 | bytes 1000000 | tf_op jit(solution)/shard_map/pallas_call | solution.py:501
  30.8 19.7 %all_to_all.10.parts = f32[32,1,128]{2,1,0:T(1,128)S(1)} all-to-all(f32[32,1,128]{2,1,0:T(1,128)S(1)} %get-tuple-element.27), channel_id=1, replica_groups=mesh['gx_0'=2,'gx_1'=2,'gy_0'=4,'gy_1'=2,'gz_0'=8,'gz_1'=2] {'gx_0','gx_..., dimensions={0} | all-to-all | bytes 32768 | tf_op jit(solution)/shard_map/all_to_all | solution.py:461
  50.6 15.0 %all_to_all.11.parts = f32[16,1,128]{2,1,0:T(1,128)S(1)} all-to-all(f32[16,1,128]{2,1,0:T(1,128)S(1)} %shard_map.73), channel_id=1, replica_groups=mesh['gx_0'=2,'gx_1'=2,'gy_0'=4,'gy_1'=2,'gz_0'=8,'gz_1'=2] {'gy_0','gy_..., dimensions={0} | all-to-all | bytes 16384 | tf_op jit(solution)/shard_map/all_to_all | solution.py:461
  65.5 1.2 %shard_map.74 = (f32[8,16,128]{2,1,0:T(8,128)}, f32[8,16,128]{2,1,0:T(8,128)}) custom-call(f32[16,1,128]{2,1,0:T(1,128)S(1)} %all_to_all.11.parts, f32[5,8,16,128]{3,2,1,0:T(8,128)S(1)} %get-tuple-element.28.basis, f32[5,5,16,128]{3,2,1,0:T(8,128)S(1)} %get-tuple-element.29.end_basis, f32[4,8,16,128]{3,2,1,0:T(8,128)S(1)} %get-tuple-element.16.fields, ...), custom_call_target="tpu_custom_call" | custom-call | flops 100000 | bytes 1000000 | tf_op jit(solution)/shard_map/pallas_call | solution.py:511
  (1 shorter events, 0.0 us)
Async XLA Ops:
  1.7 8.3 %collective-permute-start = (f32[17,16,128]{2,1,0:T(8,128)S(1)}, f32[17,16,128]{2,1,0:T(8,128)S(1)}, u32[]{:S(2)}, u32[]{:S(2)}) collective-permute-start(f32[17,16,128]{2,1,0:T(8,128)S(1)} %get-tuple-element.17), channel_id=1, source_target_pairs={{128,256},{256,128},{129,257},{257,129},{130,258},{258,130},{131,2... | collective-permute-start | bytes 417800 | tf_op jit(solution)/shard_map/ppermute | solution.py:457
  10.1 8.4 %collective-permute-start.1 = (f32[288,128]{1,0:T(8,128)S(1)}, f32[288,128]{1,0:T(8,128)S(1)}, u32[]{:S(2)}, u32[]{:S(2)}) collective-permute-start(f32[288,128]{1,0:T(8,128)S(1)} %get-tuple-element.19), channel_id=1, source_target_pairs={{16,32},{32,16},{48,64},{64,48},{80,96},{96,80},{17,33},{33,17},{4... | collective-permute-start | bytes 442376 | tf_op jit(solution)/shard_map/ppermute | solution.py:457
  18.8 10.6 %collective-permute-start.2 = (f32[5,32,128]{2,1,0:T(8,128)S(1)}, f32[5,32,128]{2,1,0:T(8,128)S(1)}, u32[]{:S(2)}, u32[]{:S(2)}) collective-permute-start(f32[5,32,128]{2,1,0:T(8,128)S(1)} %get-tuple-element.24), channel_id=1, source_target_pairs={{1,2},{2,1},{3,4},{4,3},{5,6},{6,5},{7,8},{8,7},{9,10},{10,9},{11,... | collective-permute-start | bytes 245768 | tf_op jit(solution)/shard_map/ppermute | solution.py:457

commit v8 on v7

--- a/solution.py
+++ b/solution.py
@@ -497,7 +497,7 @@
         flops=20000000,
         vmem=12,
     )(wide, theta)
-    first, second = (*GX, "gz_0"), (*GY, "gz_1")
+    first, second = (*GY, "gz_1"), (*GX, "gz_0")
     end_basis, dots = call(
         edges,
         [SMEM] + [VMEM] * 5,

time: 67 us -> 65.6 us (0.979)
  blocking collectives: 51.9 us -> 50.5 us
    all_to_all x2, blocking collectives: 34.7 us -> 33.3 us  [exchange(): return lax.all_to_all(copies, axes, split_axis=0, concat_axis=0, tiled=True)]
where the time goes in v8:
time: 65.6 us; the launch traced here: 65.3 us
  blocking collectives  50.5 us (77%)
  starting transfers between devices  7.91 us (12%)
  Pallas kernels  6.18 us (9%)
  between operations  0.7 us (1%)
    all_to_all x2, blocking collectives, exchange(): return lax.all_to_all(copies, axes, split_axis=0, concat_axis=0, tiled=True)  33.3 us
    all_gather x3, blocking collectives, trade(): lax.all_gather(near, axes[1], axis=0)  17.2 us
    ppermute x3, starting transfers between devices, trade(): lax.ppermute(far, axes, others)  7.91 us
    pallas_call x1, Pallas kernels, body(): call(interior, [VMEM] * 2, [(ITERS + 1, *brick), (len(PAIRS), 8, Z), (4,...  2.05 us
    pallas_call x1, Pallas kernels, body(): call(edges, [SMEM] + [VMEM] * 5, [(ITERS + 1, PER_GROUP, Y, Z), (lax.axis...  1.38 us
  transfers between devices with their start and end apart: 3, of which 0 were waited for; matrix products, arithmetic and copies ran while one was open for 0% of the time, Pallas kernels for 3%

profile of v8, /device:TPU:1, one launch (start us, length us, event | category | flops | bytes accessed | tf_op | source)
XLA Modules:
  0.0 65.3 jit_solution(11431808995699879519)
XLA Ops:
  0.6 1.1 %shard_map.68 = (f32[4,8,16,128]{3,2,1,0:T(8,128)S(1)}, f32[17,16,128]{2,1,0:T(8,128)S(1)}, f32[17,16,128]{2,1,0:T(8,128)S(1)}, f32[4,8,128]{2,1,0:T(8,128)S(1)}) custom-call(s32[1]{0:T(128)} %bitcast.1.place_x, f32[8,16,128]{2,1,0:T(8,128)} %opening_at.1, f32[8,16,128]{2,1,0:T(8,128)} %source_at.1, s32[8,16,128]{2,1,0:T(8,128)} %category_at.1, ...), custom_call_target="tpu_custom_call" | custom-call | flops 100000 | bytes 1000000 | tf_op jit(solution)/shard_map/pallas_call | solution.py:468
  1.7 0.7 %collective-permute-start = (f32[17,16,128]{2,1,0:T(8,128)S(1)}, f32[17,16,128]{2,1,0:T(8,128)S(1)}, u32[]{:S(2)}, u32[]{:S(2)}) collective-permute-start(f32[17,16,128]{2,1,0:T(8,128)S(1)} %get-tuple-element.17), channel_id=1, source_target_pairs={{128,256},{256,128},{129,257},{257,129},{130,258},{258,130},{131,2... | collective-permute-start | bytes 417800 | tf_op jit(solution)/shard_map/ppermute | solution.py:457
  2.4 7.6 %all-gather = f32[34,16,128]{2,1,0:T(8,128)S(1)} all-gather(f32[17,16,128]{2,1,0:T(8,128)S(1)} %get-tuple-element.18), channel_id=2, replica_groups=mesh['gx_0'=2,'gx_1'=2,'gy_0'=4,'gy_1'=2,'gz_0'=8,'gz_1'=2] {'gx_1'}, dimensions={0}, use_global_device_ids=true | all-gather | bytes 417792 | tf_op jit(solution)/shard_map/all_gather | solution.py:457
  10.0 0.0 collective-permute-done.far_x
  10.0 0.1 shard_map.69
  10.1 0.7 %collective-permute-start.1 = (f32[288,128]{1,0:T(8,128)S(1)}, f32[288,128]{1,0:T(8,128)S(1)}, u32[]{:S(2)}, u32[]{:S(2)}) collective-permute-start(f32[288,128]{1,0:T(8,128)S(1)} %get-tuple-element.19), channel_id=1, source_target_pairs={{16,32},{32,16},{48,64},{64,48},{80,96},{96,80},{17,33},{33,17},{4... | collective-permute-start | bytes 442376 | tf_op jit(solution)/shard_map/ppermute | solution.py:457
  10.7 7.7 %all-gather.1 = f32[576,128]{1,0:T(8,128)S(1)} all-gather(f32[288,128]{1,0:T(8,128)S(1)} %get-tuple-element.20), channel_id=3, replica_groups=mesh['gx_0'=2,'gx_1'=2,'gy_0'=4,'gy_1'=2,'gz_0'=8,'gz_1'=2] {'gy_1'}, dimensions={0}, use_global_device_ids=true | all-gather | bytes 442368 | tf_op jit(solution)/shard_map/all_gather | solution.py:457
  18.4 0.0 collective-permute-done.1.far_y
  18.4 0.4 shard_map.70
  18.8 6.6 %collective-permute-start.2 = (f32[5,32,128]{2,1,0:T(8,128)S(1)}, f32[5,32,128]{2,1,0:T(8,128)S(1)}, u32[]{:S(2)}, u32[]{:S(2)}) collective-permute-start(f32[5,32,128]{2,1,0:T(8,128)S(1)} %get-tuple-element.24), channel_id=1, source_target_pairs={{1,2},{2,1},{3,4},{4,3},{5,6},{6,5},{7,8},{8,7},{9,10},{10,9},{11,... | collective-permute-start | bytes 245768 | tf_op jit(solution)/shard_map/ppermute | solution.py:457
  25.4 2.1 %shard_map.71 = (f32[5,8,16,128]{3,2,1,0:T(8,128)S(1)}, f32[14,8,128]{2,1,0:T(8,128)S(1)}, f32[4,5,32,128]{3,2,1,0:T(8,128)S(1)}) custom-call(f32[4,18,32,128]{3,2,1,0:T(8,128)S(1)} %get-tuple-element.21.wide, f32[4,8,128]{2,1,0:T(8,128)S(1)} %get-tuple-element.22.theta), custom_call_target="tpu_custom_call" | custom-call | flops 20000000 | bytes 1000000 | tf_op jit(solution)/shard_map/pallas_call | solution.py:492
  27.4 1.9 %all-gather.2 = f32[10,32,128]{2,1,0:T(8,128)S(1)} all-gather(f32[5,32,128]{2,1,0:T(8,128)S(1)} %get-tuple-element.25), channel_id=4, replica_groups=mesh['gx_0'=2,'gx_1'=2,'gy_0'=4,'gy_1'=2,'gz_0'=8,'gz_1'=2] {'gz_1'}, dimensions={0}, use_global_device_ids=true | all-gather | bytes 245760 | tf_op jit(solution)/shard_map/all_gather | solution.py:457
  29.4 0.0 collective-permute-done.2.far
  29.4 1.4 %shard_map.72 = (f32[5,5,16,128]{3,2,1,0:T(8,128)S(1)}, f32[16,1,128]{2,1,0:T(1,128)S(1)}) custom-call(s32[1]{0:T(128)} %bitcast.place_z, f32[4,5,32,128]{3,2,1,0:T(8,128)S(1)} %get-tuple-element.23.ends, f32[5,32,128]{2,1,0:T(8,128)S(1)} %collective-permute-done.2.far, f32[2,5,32,128]{3,2,1,0:T(8,128)S(1)} %bitcast.9, ...), custom_call_target="tpu_custom_call" | custom-call | flops 5000000 | bytes 1000000 | tf_op jit(solution)/shard_map/pallas_call | solution.py:501
  30.7 13.6 %all_to_all.10.parts = f32[16,1,128]{2,1,0:T(1,128)S(1)} all-to-all(f32[16,1,128]{2,1,0:T(1,128)S(1)} %get-tuple-element.27), channel_id=1, replica_groups=mesh['gx_0'=2,'gx_1'=2,'gy_0'=4,'gy_1'=2,'gz_0'=8,'gz_1'=2] {'gy_0','gy_..., dimensions={0} | all-to-all | bytes 16384 | tf_op jit(solution)/shard_map/all_to_all | solution.py:461
  44.3 19.7 %all_to_all.11.parts = f32[32,1,128]{2,1,0:T(1,128)S(1)} all-to-all(f32[32,1,128]{2,1,0:T(1,128)S(1)} %shard_map.73), channel_id=1, replica_groups=mesh['gx_0'=2,'gx_1'=2,'gy_0'=4,'gy_1'=2,'gz_0'=8,'gz_1'=2] {'gx_0','gx_..., dimensions={0} | all-to-all | bytes 32768 | tf_op jit(solution)/shard_map/all_to_all | solution.py:461
  64.1 1.2 %shard_map.74 = (f32[8,16,128]{2,1,0:T(8,128)}, f32[8,16,128]{2,1,0:T(8,128)}) custom-call(f32[32,1,128]{2,1,0:T(1,128)S(1)} %all_to_all.11.parts, f32[5,8,16,128]{3,2,1,0:T(8,128)S(1)} %get-tuple-element.28.basis, f32[5,5,16,128]{3,2,1,0:T(8,128)S(1)} %get-tuple-element.29.end_basis, f32[4,8,16,128]{3,2,1,0:T(8,128)S(1)} %get-tuple-element.16.fields, ...), custom_call_target="tpu_custom_call" | custom-call | flops 100000 | bytes 1000000 | tf_op jit(solution)/shard_map/pallas_call | solution.py:511
  (1 shorter events, 0.0 us)
Async XLA Ops:
  1.7 8.3 %collective-permute-start = (f32[17,16,128]{2,1,0:T(8,128)S(1)}, f32[17,16,128]{2,1,0:T(8,128)S(1)}, u32[]{:S(2)}, u32[]{:S(2)}) collective-permute-start(f32[17,16,128]{2,1,0:T(8,128)S(1)} %get-tuple-element.17), channel_id=1, source_target_pairs={{128,256},{256,128},{129,257},{257,129},{130,258},{258,130},{131,2... | collective-permute-start | bytes 417800 | tf_op jit(solution)/shard_map/ppermute | solution.py:457
  10.1 8.4 %collective-permute-start.1 = (f32[288,128]{1,0:T(8,128)S(1)}, f32[288,128]{1,0:T(8,128)S(1)}, u32[]{:S(2)}, u32[]{:S(2)}) collective-permute-start(f32[288,128]{1,0:T(8,128)S(1)} %get-tuple-element.19), channel_id=1, source_target_pairs={{16,32},{32,16},{48,64},{64,48},{80,96},{96,80},{17,33},{33,17},{4... | collective-permute-start | bytes 442376 | tf_op jit(solution)/shard_map/ppermute | solution.py:457
  18.8 10.6 %collective-permute-start.2 = (f32[5,32,128]{2,1,0:T(8,128)S(1)}, f32[5,32,128]{2,1,0:T(8,128)S(1)}, u32[]{:S(2)}, u32[]{:S(2)}) collective-permute-start(f32[5,32,128]{2,1,0:T(8,128)S(1)} %get-tuple-element.24), channel_id=1, source_target_pairs={{1,2},{2,1},{3,4},{4,3},{5,6},{6,5},{7,8},{8,7},{9,10},{10,9},{11,... | collective-permute-start | bytes 245768 | tf_op jit(solution)/shard_map/ppermute | solution.py:457

commit v9 on v8

--- a/solution.py
+++ b/solution.py
@@ -152,12 +152,20 @@
     ]
 
 
-def smooth(mid, ahead, here, behind, first, count):
-    n = here.shape[0]
-    mid[0:n, 8 : 8 + ROWS] = (ahead + here) + (here + behind)
+def smooth_xy(mid, planes, first, count):
+    n = planes.shape[0] - 2
+    here = planes[1:-1]
+    mid[0:n, 8 : 8 + ROWS] = (planes[:-2] + here) + (here + planes[2:])
     sides = mid[0:n, pl.ds(7 + first, count)] + mid[0:n, pl.ds(9 + first, count)]
-    rows = mid[0:n, pl.ds(8 + first, count)] + 0.5 * sides
-    return rows + 0.5 * (pltpu.roll(rows, 1, 2) + pltpu.roll(rows, Z - 1, 2))
+    return mid[0:n, pl.ds(8 + first, count)] + 0.5 * sides
+
+
+def smooth_z(here, low, high):
+    return here + 0.5 * (low + high)
+
+
+def turned(values):
+    return pltpu.roll(values, 1, 2), pltpu.roll(values, Z - 1, 2)
 
 
 def newton_step(slope, diag, inside, shift, v, tv, tu):
@@ -170,46 +178,51 @@
     return [(p, min(p + size, high)) for p in range(low, high, size)]
 
 
-def interior(wide, theta, basis, sums, ends, cx, mid, slope, diag, inside, va, vb, ua, ub):
+def interior(wide, theta, basis, sums, ends, mid, tops, slopes, diag, inside, va, vb, za, zb, zc):
     lane = lax.broadcasted_iota(jnp.int32, (ROWS, Z), 1)
     slots = mid.shape[0]
     slot = [0]
 
-    def along(ref, p, q, first=0, count=ROWS):
+    def smoothed(ref, p, q, first=0, count=ROWS):
         slot[0] += 1
-        return smooth(
-            mid.at[slot[0] % slots], ref[p - 1 : q - 1], ref[p:q], ref[p + 1 : q + 1], first, count
-        )
+        return smooth_xy(mid.at[slot[0] % slots], ref[p - 1 : q + 1], first, count)
 
     cond, start, rest, flag = (wide.at[k] for k in range(4))
-    cx[...] = cond[...] * start[...]
+    for p, q in chunks(0, PLANES, CHUNK):
+        c, x = cond[p:q], start[p:q]
+        (c_low, c_high), (x_low, x_high) = turned(c), turned(x)
+        za[p:q] = smooth_z(c, c_low, c_high)
+        zb[p:q] = smooth_z(x, x_low, x_high)
+        zc[p:q] = smooth_z(c * x, c_low * x_low, c_high * x_high)
+        for n, values in enumerate((c, c_low, c_high)):
+            slopes[n, p:q] = values * (1.0 / SCALE)
     for p, q in chunks(1, PLANES - 1, CHUNK):
-        tc, tx, tcx = (along(ref, p, q) for ref in (cond, start, cx))
+        tc, tx, tcx = (smoothed(ref, p, q) for ref in (za, zb, zc))
         c = cond[p:q]
         near = 16.0 * c + tc
         diag[p:q] = (1.0 + 6.0 * flag[p:q] + near) * (1.0 / SCALE)
-        half_c = c * (1.0 / SCALE)
-        slope[p:q] = half_c
         there = jnp.where(c > 0.0, 1.0, 0.0)
         inside[p:q] = there
-        r = (rest[p:q] - near * start[p:q] + (c * tx + tcx)) * there
-        va[p:q] = r
-        ua[p:q] = r * half_c
+        va[p:q] = (rest[p:q] - near * start[p:q] + (c * tx + tcx)) * there
     basis[0] = va[HALO : HALO + X, TOP : TOP + Y]
     for k in range(ITERS):
-        v_old, u_old, v_new, u_new = (va, ua, vb, ub) if k % 2 == 0 else (vb, ub, va, ua)
+        v_old, v_new = (va, vb) if k % 2 == 0 else (vb, va)
         last = k + 1 == ITERS
         first, count = (TOP, Y) if last else (0, ROWS)
         rows = pl.ds(first, count)
         shift = jnp.tile(theta[k], (count // 8, 1))[None]
+        for p, q in chunks(1 + k, PLANES - 1 - k, CHUNK):
+            v = v_old[p:q]
+            low, high = turned(v)
+            za[p:q] = smooth_z(v, low, high)
+            zb[p:q] = smooth_z(slopes[0, p:q] * v, slopes[1, p:q] * low, slopes[2, p:q] * high)
         for p, q in chunks(2 + k, PLANES - 2 - k, CHUNK):
-            tv, tu = along(v_old, p, q, first, count), along(u_old, p, q, first, count)
-            v = newton_step(slope[p:q, rows], diag[p:q, rows], inside[p:q, rows], shift, v_old[p:q, rows], tv, tu)
+            tv, tu = smoothed(za, p, q, first, count), smoothed(zb, p, q, first, count)
+            v = newton_step(slopes[0, p:q, rows], diag[p:q, rows], inside[p:q, rows], shift, v_old[p:q, rows], tv, tu)
             if last:
                 basis[k + 1, p - HALO : q - HALO] = v
             else:
                 v_new[p:q] = v
-                u_new[p:q] = v * slope[p:q]
         if not last:
             basis[k + 1] = v_new[HALO : HALO + X, TOP : TOP + Y]
 
@@ -223,23 +236,26 @@
                 total = term if total is None else total + term
         sums[n] = jnp.where(inner, total, 0.0)
 
-    place = lane % GROUP
+    place, from_high = lane % GROUP, (lane + HALO) % Z
+    low_cells = (place >= LOW_AT) & (place < LOW_AT + 2 * HALO)
+    high_cells = (place >= HIGH_AT - 2 * HALO) & (place < HIGH_AT)
     for k in range(4):
         for q in range(PER_GROUP):
-            out = jnp.zeros((ROWS, Z), F32)
+            low = high = jnp.zeros((ROWS, Z), F32)
             for g in range(GROUPS):
                 p = PER_GROUP * g + q
                 if p in planes_of(k):
-                    mine = (lane // GROUP) == g
-                    low = pltpu.roll(wide[k, p], GROUP * g + LOW_AT, 1)
-                    high = pltpu.roll(wide[k, p], (GROUP * g + HIGH_AT) % Z, 1)
-                    low_here = mine & (place >= LOW_AT) & (place < LOW_AT + 2 * HALO)
-                    high_here = mine & (place >= HIGH_AT - 2 * HALO) & (place < HIGH_AT)
-                    out = jnp.where(low_here, low, jnp.where(high_here, high, out))
-            ends[k, q] = out
-
-
-def edges(place_z, ends, far, chip, theta, inner_sums, basis, dots, cells, cx, mid, slope, diag, inside, va, vb, ua, ub, stack):
+                    both = pltpu.roll(wide[k, p], GROUP * g + LOW_AT, 1)
+                    low = jnp.where((lane // GROUP == g) & low_cells, both, low)
+                    here = (from_high // GROUP == g) & (from_high % GROUP < 2 * HALO)
+                    high = jnp.where(here, both, high)
+            ends[k, q] = jnp.where(low_cells, low, 0.0)
+            tops[k, q] = high
+    for k in range(4):
+        ends[k] = jnp.where(high_cells, pltpu.roll(tops[k], HIGH_AT - LOW_AT, 2), ends[k])
+
+
+def edges(place_z, ends, far, chip, theta, inner_sums, basis, dots, cells, mid, slopes, stack):
     lane = lax.broadcasted_iota(jnp.int32, (ROWS, Z), 1)
     place = lane % GROUP
     slots = mid.shape[0]
@@ -253,45 +269,43 @@
             out = jnp.where(place < LOW_AT, low, ends[k, q])
             cells[k, q] = jnp.where((place >= HIGH_AT) & (place < HIGH_AT + HALO), high, out)
 
-    def along(ref, first=0, count=ROWS):
+    def smoothed(planes, first=0, count=ROWS):
         slot[0] += 1
-        here = ref[...]
-        before = pltpu.roll(ref[PER_GROUP - 1], GROUP, 1)[None]
-        after = pltpu.roll(ref[0], Z - GROUP, 1)[None]
-        return smooth(
-            mid.at[slot[0] % slots],
-            jnp.concatenate([before, ref[: PER_GROUP - 1]]),
-            here,
-            jnp.concatenate([ref[1:], after]),
-            first,
-            count,
-        )
-
-    cond, start, rest, flag = (cells.at[k] for k in range(4))
-    cx[...] = cond[...] * start[...]
-    tc, tx, tcx = (along(ref) for ref in (cond, start, cx))
-    c = cond[...]
-    near = 16.0 * c + tc
-    diag[...] = (1.0 + 6.0 * flag[...] + near) * (1.0 / SCALE)
-    half_c = c * (1.0 / SCALE)
-    slope[...] = half_c
-    there = jnp.where(c > 0.0, 1.0, 0.0)
-    inside[...] = there
-    r = (rest[...] - near * start[...] + (c * tx + tcx)) * there
-    va[...] = r
-    ua[...] = r * half_c
-    basis[0] = r[:, TOP : TOP + Y]
+        return smooth_xy(mid.at[slot[0] % slots], planes, first, count)
+
+    def spread(values):
+        return [
+            jnp.concatenate(
+                [
+                    pltpu.roll(values[PER_GROUP - 1], GROUP + by, 1)[None],
+                    pltpu.roll(values, by % Z, 2) if by else values,
+                    pltpu.roll(values[0], Z - GROUP + by, 1)[None],
+                ]
+            )
+            for by in (0, 1, -1)
+        ]
+
+    cond, start, rest, flag = (cells[k] for k in range(4))
+    cs, xs = spread(cond), spread(start)
+    tc, tx, tcx = (
+        smoothed(smooth_z(*values)) for values in (cs, xs, [c * x for c, x in zip(cs, xs)])
+    )
+    for n, values in enumerate(cs):
+        slopes[n] = values * (1.0 / SCALE)
+    near = 16.0 * cond + tc
+    diag = (1.0 + 6.0 * flag + near) * (1.0 / SCALE)
+    there = jnp.where(cond > 0.0, 1.0, 0.0)
+    v = (rest - near * start + (cond * tx + tcx)) * there
+    basis[0] = v[:, TOP : TOP + Y]
     for k in range(ITERS):
-        v_old, u_old, v_new, u_new = (va, ua, vb, ub) if k % 2 == 0 else (vb, ub, va, ua)
         last = k + 1 == ITERS
         first, count = (TOP, Y) if last else (0, ROWS)
-        rows = pl.ds(first, count)
+        rows = slice(first, first + count)
         shift = jnp.tile(theta[k], (count // 8, 1))[None]
-        tv, tu = along(v_old, first, count), along(u_old, first, count)
-        v = newton_step(slope[:, rows], diag[:, rows], inside[:, rows], shift, v_old[:, rows], tv, tu)
-        if not last:
-            v_new[...] = v
-            u_new[...] = v * slope[...]
+        vs = spread(v)
+        tv = smoothed(smooth_z(*vs), first, count)
+        tu = smoothed(smooth_z(*(slopes[n] * values for n, values in enumerate(vs))), first, count)
+        v = newton_step(slopes[0, 1:-1][:, rows], diag[:, rows], there[:, rows], shift, v[:, rows], tv, tu)
         basis[k + 1] = v if last else v[:, TOP : TOP + Y]
 
     end_cells = ((place >= LOW_AT) & (place < LOW_AT + HALO)) | ((place >= HIGH_AT - HALO) & (place < HIGH_AT))
@@ -493,7 +507,7 @@
         interior,
         [VMEM] * 2,
         [(ITERS + 1, *brick), (len(PAIRS), 8, Z), (4, *packed)],
-        [sided, middle] + [sided] * 7,
+        [middle, (4, *packed), (3, *sided)] + [sided] * 7,
         flops=20000000,
         vmem=12,
     )(wide, theta)
@@ -502,7 +516,7 @@
         edges,
         [SMEM] + [VMEM] * 5,
         [(ITERS + 1, PER_GROUP, Y, Z), (lax.axis_size(first), 1, Z)],
-        [(4, *packed), packed, (3, PER_GROUP, ROWS + 16, Z)] + [packed] * 7 + [(Z, Z)],
+        [(4, *packed), (3, PER_GROUP, ROWS + 16, Z), (3, PER_GROUP + 2, ROWS, Z), (Z, Z)],
         flops=5000000,
     )(place_z, ends, far, chip, theta, sums)
     parts = exchange(dots, first)

time: 65.6 us -> 65.4 us (level)
  no operation moved by 1% of the time
where the time goes in v9:
time: 65.4 us; the launch traced here: 65.1 us
  blocking collectives  50.6 us (77%)
  starting transfers between devices  7.91 us (12%)
  Pallas kernels  5.84 us (9%)
  between operations  0.7 us (1%)
    all_to_all x2, blocking collectives, exchange(): return lax.all_to_all(copies, axes, split_axis=0, concat_axis=0, tiled=True)  33.5 us
    all_gather x3, blocking collectives, trade(): lax.all_gather(near, axes[1], axis=0)  17.2 us
    ppermute x3, starting transfers between devices, trade(): lax.ppermute(far, axes, others)  7.91 us
    pallas_call x1, Pallas kernels, body(): call(interior, [VMEM] * 2, [(ITERS + 1, *brick), (len(PAIRS), 8, Z), (4,...  1.73 us
    pallas_call x1, Pallas kernels, body(): call(edges, [SMEM] + [VMEM] * 5, [(ITERS + 1, PER_GROUP, Y, Z), (lax.axis...  1.37 us
  transfers between devices with their start and end apart: 3, of which 0 were waited for; matrix products, arithmetic and copies ran while one was open for 0% of the time, Pallas kernels for 3%

profile of v9, /device:TPU:1, one launch (start us, length us, event | category | flops | bytes accessed | tf_op | source)
XLA Modules:
  0.0 65.1 jit_solution(6221308596386638032)
XLA Ops:
  0.6 1.1 %shard_map.68 = (f32[4,8,16,128]{3,2,1,0:T(8,128)S(1)}, f32[17,16,128]{2,1,0:T(8,128)S(1)}, f32[17,16,128]{2,1,0:T(8,128)S(1)}, f32[4,8,128]{2,1,0:T(8,128)S(1)}) custom-call(s32[1]{0:T(128)} %bitcast.1.place_x, f32[8,16,128]{2,1,0:T(8,128)} %opening_at.1, f32[8,16,128]{2,1,0:T(8,128)} %source_at.1, s32[8,16,128]{2,1,0:T(8,128)} %category_at.1, ...), custom_call_target="tpu_custom_call" | custom-call | flops 100000 | bytes 1000000 | tf_op jit(solution)/shard_map/pallas_call | solution.py:482
  1.7 0.7 %collective-permute-start = (f32[17,16,128]{2,1,0:T(8,128)S(1)}, f32[17,16,128]{2,1,0:T(8,128)S(1)}, u32[]{:S(2)}, u32[]{:S(2)}) collective-permute-start(f32[17,16,128]{2,1,0:T(8,128)S(1)} %get-tuple-element.17), channel_id=1, source_target_pairs={{128,256},{256,128},{129,257},{257,129},{130,258},{258,130},{131,2... | collective-permute-start | bytes 417800 | tf_op jit(solution)/shard_map/ppermute | solution.py:471
  2.4 7.6 %all-gather = f32[34,16,128]{2,1,0:T(8,128)S(1)} all-gather(f32[17,16,128]{2,1,0:T(8,128)S(1)} %get-tuple-element.18), channel_id=2, replica_groups=mesh['gx_0'=2,'gx_1'=2,'gy_0'=4,'gy_1'=2,'gz_0'=8,'gz_1'=2] {'gx_1'}, dimensions={0}, use_global_device_ids=true | all-gather | bytes 417792 | tf_op jit(solution)/shard_map/all_gather | solution.py:471
  10.0 0.0 collective-permute-done.far_x
  10.0 0.1 shard_map.69
  10.1 0.7 %collective-permute-start.1 = (f32[288,128]{1,0:T(8,128)S(1)}, f32[288,128]{1,0:T(8,128)S(1)}, u32[]{:S(2)}, u32[]{:S(2)}) collective-permute-start(f32[288,128]{1,0:T(8,128)S(1)} %get-tuple-element.19), channel_id=1, source_target_pairs={{16,32},{32,16},{48,64},{64,48},{80,96},{96,80},{17,33},{33,17},{4... | collective-permute-start | bytes 442376 | tf_op jit(solution)/shard_map/ppermute | solution.py:471
  10.7 7.7 %all-gather.1 = f32[576,128]{1,0:T(8,128)S(1)} all-gather(f32[288,128]{1,0:T(8,128)S(1)} %get-tuple-element.20), channel_id=3, replica_groups=mesh['gx_0'=2,'gx_1'=2,'gy_0'=4,'gy_1'=2,'gz_0'=8,'gz_1'=2] {'gy_1'}, dimensions={0}, use_global_device_ids=true | all-gather | bytes 442368 | tf_op jit(solution)/shard_map/all_gather | solution.py:471
  18.4 0.0 collective-permute-done.1.far_y
  18.4 0.4 shard_map.70
  18.8 6.6 %collective-permute-start.2 = (f32[5,32,128]{2,1,0:T(8,128)S(1)}, f32[5,32,128]{2,1,0:T(8,128)S(1)}, u32[]{:S(2)}, u32[]{:S(2)}) collective-permute-start(f32[5,32,128]{2,1,0:T(8,128)S(1)} %get-tuple-element.24), channel_id=1, source_target_pairs={{1,2},{2,1},{3,4},{4,3},{5,6},{6,5},{7,8},{8,7},{9,10},{10,9},{11,... | collective-permute-start | bytes 245768 | tf_op jit(solution)/shard_map/ppermute | solution.py:471
  25.4 1.7 %shard_map.71 = (f32[5,8,16,128]{3,2,1,0:T(8,128)S(1)}, f32[14,8,128]{2,1,0:T(8,128)S(1)}, f32[4,5,32,128]{3,2,1,0:T(8,128)S(1)}) custom-call(f32[4,18,32,128]{3,2,1,0:T(8,128)S(1)} %get-tuple-element.21.wide, f32[4,8,128]{2,1,0:T(8,128)S(1)} %get-tuple-element.22.theta), custom_call_target="tpu_custom_call" | custom-call | flops 20000000 | bytes 1000000 | tf_op jit(solution)/shard_map/pallas_call | solution.py:506
  27.1 1.9 %all-gather.2 = f32[10,32,128]{2,1,0:T(8,128)S(1)} all-gather(f32[5,32,128]{2,1,0:T(8,128)S(1)} %get-tuple-element.25), channel_id=4, replica_groups=mesh['gx_0'=2,'gx_1'=2,'gy_0'=4,'gy_1'=2,'gz_0'=8,'gz_1'=2] {'gz_1'}, dimensions={0}, use_global_device_ids=true | all-gather | bytes 245760 | tf_op jit(solution)/shard_map/all_gather | solution.py:471
  29.0 0.0 collective-permute-done.2.far
  29.0 1.4 %shard_map.72 = (f32[5,5,16,128]{3,2,1,0:T(8,128)S(1)}, f32[16,1,128]{2,1,0:T(1,128)S(1)}) custom-call(s32[1]{0:T(128)} %bitcast.place_z, f32[4,5,32,128]{3,2,1,0:T(8,128)S(1)} %get-tuple-element.23.ends, f32[5,32,128]{2,1,0:T(8,128)S(1)} %collective-permute-done.2.far, f32[2,5,32,128]{3,2,1,0:T(8,128)S(1)} %bitcast.9, ...), custom_call_target="tpu_custom_call" | custom-call | flops 5000000 | bytes 1000000 | tf_op jit(solution)/shard_map/pallas_call | solution.py:515
  30.4 13.6 %all_to_all.10.parts = f32[16,1,128]{2,1,0:T(1,128)S(1)} all-to-all(f32[16,1,128]{2,1,0:T(1,128)S(1)} %get-tuple-element.27), channel_id=1, replica_groups=mesh['gx_0'=2,'gx_1'=2,'gy_0'=4,'gy_1'=2,'gz_0'=8,'gz_1'=2] {'gy_0','gy_..., dimensions={0} | all-to-all | bytes 16384 | tf_op jit(solution)/shard_map/all_to_all | solution.py:475
  44.0 19.9 %all_to_all.11.parts = f32[32,1,128]{2,1,0:T(1,128)S(1)} all-to-all(f32[32,1,128]{2,1,0:T(1,128)S(1)} %shard_map.73), channel_id=1, replica_groups=mesh['gx_0'=2,'gx_1'=2,'gy_0'=4,'gy_1'=2,'gz_0'=8,'gz_1'=2] {'gx_0','gx_..., dimensions={0} | all-to-all | bytes 32768 | tf_op jit(solution)/shard_map/all_to_all | solution.py:475
  63.9 1.2 %shard_map.74 = (f32[8,16,128]{2,1,0:T(8,128)}, f32[8,16,128]{2,1,0:T(8,128)}) custom-call(f32[32,1,128]{2,1,0:T(1,128)S(1)} %all_to_all.11.parts, f32[5,8,16,128]{3,2,1,0:T(8,128)S(1)} %get-tuple-element.28.basis, f32[5,5,16,128]{3,2,1,0:T(8,128)S(1)} %get-tuple-element.29.end_basis, f32[4,8,16,128]{3,2,1,0:T(8,128)S(1)} %get-tuple-element.16.fields, ...), custom_call_target="tpu_custom_call" | custom-call | flops 100000 | bytes 1000000 | tf_op jit(solution)/shard_map/pallas_call | solution.py:525
  (1 shorter events, 0.0 us)
Async XLA Ops:
  1.7 8.3 %collective-permute-start = (f32[17,16,128]{2,1,0:T(8,128)S(1)}, f32[17,16,128]{2,1,0:T(8,128)S(1)}, u32[]{:S(2)}, u32[]{:S(2)}) collective-permute-start(f32[17,16,128]{2,1,0:T(8,128)S(1)} %get-tuple-element.17), channel_id=1, source_target_pairs={{128,256},{256,128},{129,257},{257,129},{130,258},{258,130},{131,2... | collective-permute-start | bytes 417800 | tf_op jit(solution)/shard_map/ppermute | solution.py:471
  10.1 8.4 %collective-permute-start.1 = (f32[288,128]{1,0:T(8,128)S(1)}, f32[288,128]{1,0:T(8,128)S(1)}, u32[]{:S(2)}, u32[]{:S(2)}) collective-permute-start(f32[288,128]{1,0:T(8,128)S(1)} %get-tuple-element.19), channel_id=1, source_target_pairs={{16,32},{32,16},{48,64},{64,48},{80,96},{96,80},{17,33},{33,17},{4... | collective-permute-start | bytes 442376 | tf_op jit(solution)/shard_map/ppermute | solution.py:471
  18.8 10.2 %collective-permute-start.2 = (f32[5,32,128]{2,1,0:T(8,128)S(1)}, f32[5,32,128]{2,1,0:T(8,128)S(1)}, u32[]{:S(2)}, u32[]{:S(2)}) collective-permute-start(f32[5,32,128]{2,1,0:T(8,128)S(1)} %get-tuple-element.24), channel_id=1, source_target_pairs={{1,2},{2,1},{3,4},{4,3},{5,6},{6,5},{7,8},{8,7},{9,10},{10,9},{11,... | collective-permute-start | bytes 245768 | tf_op jit(solution)/shard_map/ppermute | solution.py:471

commit v10 on v9

--- a/solution.py
+++ b/solution.py
@@ -22,7 +22,7 @@
 GROUPS, PER_GROUP, GROUP = 4, 5, 32
 LOW_AT, HIGH_AT = 5, 26
 SCALE = 64.0
-CHUNK = 4
+CHUNK = 3
 PAIRS = [(i, j) for i in range(ITERS) for j in range(i, ITERS + 1)]
 VMEM = pl.BlockSpec(memory_space=pltpu.VMEM)
 HBM = pl.BlockSpec(memory_space=pltpu.HBM)
@@ -154,8 +154,8 @@
 
 def smooth_xy(mid, planes, first, count):
     n = planes.shape[0] - 2
-    here = planes[1:-1]
-    mid[0:n, 8 : 8 + ROWS] = (planes[:-2] + here) + (here + planes[2:])
+    pairs = planes[:-1] + planes[1:]
+    mid[0:n, 8 : 8 + ROWS] = pairs[:-1] + pairs[1:]
     sides = mid[0:n, pl.ds(7 + first, count)] + mid[0:n, pl.ds(9 + first, count)]
     return mid[0:n, pl.ds(8 + first, count)] + 0.5 * sides
 
@@ -187,8 +187,39 @@
         slot[0] += 1
         return smooth_xy(mid.at[slot[0] % slots], ref[p - 1 : q + 1], first, count)
 
+    place, from_high = lane % GROUP, (lane + HALO) % Z
+    low_cells = (place >= LOW_AT) & (place < LOW_AT + 2 * HALO)
+    high_cells = (place >= HIGH_AT - 2 * HALO) & (place < HIGH_AT)
+
+    def pack(k, q):
+        low = high = jnp.zeros((ROWS, Z), F32)
+        for g in range(GROUPS):
+            p = PER_GROUP * g + q
+            if p in planes_of(k):
+                both = pltpu.roll(wide[k, p], GROUP * g + LOW_AT, 1)
+                low = jnp.where((lane // GROUP == g) & low_cells, both, low)
+                here = (from_high // GROUP == g) & (from_high % GROUP < 2 * HALO)
+                high = jnp.where(here, both, high)
+        ends[k, q] = jnp.where(low_cells, low, 0.0)
+        tops[k, q] = high
+
+    to_pack = [(k, q) for k in range(4) for q in range(PER_GROUP)]
+
+    def in_turn(low, high, turn, then):
+        waiting, done = [], low + 1
+        for p, q in chunks(low, high, CHUNK):
+            turn(p, q)
+            if to_pack:
+                pack(*to_pack.pop(0))
+            waiting.append((done, q - 1))
+            done = q - 1
+            if len(waiting) > 1:
+                then(*waiting.pop(0))
+        then(*waiting.pop(0))
+
     cond, start, rest, flag = (wide.at[k] for k in range(4))
-    for p, q in chunks(0, PLANES, CHUNK):
+
+    def turn_first(p, q):
         c, x = cond[p:q], start[p:q]
         (c_low, c_high), (x_low, x_high) = turned(c), turned(x)
         za[p:q] = smooth_z(c, c_low, c_high)
@@ -196,7 +227,8 @@
         zc[p:q] = smooth_z(c * x, c_low * x_low, c_high * x_high)
         for n, values in enumerate((c, c_low, c_high)):
             slopes[n, p:q] = values * (1.0 / SCALE)
-    for p, q in chunks(1, PLANES - 1, CHUNK):
+
+    def first_vector(p, q):
         tc, tx, tcx = (smoothed(ref, p, q) for ref in (za, zb, zc))
         c = cond[p:q]
         near = 16.0 * c + tc
@@ -204,6 +236,8 @@
         there = jnp.where(c > 0.0, 1.0, 0.0)
         inside[p:q] = there
         va[p:q] = (rest[p:q] - near * start[p:q] + (c * tx + tcx)) * there
+
+    in_turn(0, PLANES, turn_first, first_vector)
     basis[0] = va[HALO : HALO + X, TOP : TOP + Y]
     for k in range(ITERS):
         v_old, v_new = (va, vb) if k % 2 == 0 else (vb, va)
@@ -211,20 +245,26 @@
         first, count = (TOP, Y) if last else (0, ROWS)
         rows = pl.ds(first, count)
         shift = jnp.tile(theta[k], (count // 8, 1))[None]
-        for p, q in chunks(1 + k, PLANES - 1 - k, CHUNK):
+
+        def turn(p, q):
             v = v_old[p:q]
             low, high = turned(v)
             za[p:q] = smooth_z(v, low, high)
             zb[p:q] = smooth_z(slopes[0, p:q] * v, slopes[1, p:q] * low, slopes[2, p:q] * high)
-        for p, q in chunks(2 + k, PLANES - 2 - k, CHUNK):
+
+        def next_vector(p, q):
             tv, tu = smoothed(za, p, q, first, count), smoothed(zb, p, q, first, count)
             v = newton_step(slopes[0, p:q, rows], diag[p:q, rows], inside[p:q, rows], shift, v_old[p:q, rows], tv, tu)
             if last:
                 basis[k + 1, p - HALO : q - HALO] = v
             else:
                 v_new[p:q] = v
+
+        in_turn(1 + k, PLANES - 1 - k, turn, next_vector)
         if not last:
             basis[k + 1] = v_new[HALO : HALO + X, TOP : TOP + Y]
+    while to_pack:
+        pack(*to_pack.pop(0))
 
     inner = (lane[:8] >= HALO) & (lane[:8] < Z - HALO)
     for n, (i, j) in enumerate(PAIRS):
@@ -236,38 +276,23 @@
                 total = term if total is None else total + term
         sums[n] = jnp.where(inner, total, 0.0)
 
-    place, from_high = lane % GROUP, (lane + HALO) % Z
-    low_cells = (place >= LOW_AT) & (place < LOW_AT + 2 * HALO)
-    high_cells = (place >= HIGH_AT - 2 * HALO) & (place < HIGH_AT)
-    for k in range(4):
-        for q in range(PER_GROUP):
-            low = high = jnp.zeros((ROWS, Z), F32)
-            for g in range(GROUPS):
-                p = PER_GROUP * g + q
-                if p in planes_of(k):
-                    both = pltpu.roll(wide[k, p], GROUP * g + LOW_AT, 1)
-                    low = jnp.where((lane // GROUP == g) & low_cells, both, low)
-                    here = (from_high // GROUP == g) & (from_high % GROUP < 2 * HALO)
-                    high = jnp.where(here, both, high)
-            ends[k, q] = jnp.where(low_cells, low, 0.0)
-            tops[k, q] = high
     for k in range(4):
         ends[k] = jnp.where(high_cells, pltpu.roll(tops[k], HIGH_AT - LOW_AT, 2), ends[k])
 
 
-def edges(place_z, ends, far, chip, theta, inner_sums, basis, dots, cells, mid, slopes, stack):
+def edges(place_z, ends, far, chip, theta, inner_sums, basis, dots, mid, slopes, stack):
     lane = lax.broadcasted_iota(jnp.int32, (ROWS, Z), 1)
     place = lane % GROUP
     slots = mid.shape[0]
     slot = [0]
 
-    for q in range(PER_GROUP):
-        below, above = (halo(place_z[0], far, chip, (q,), lower) for lower in (True, False))
-        for k in range(4):
-            low = pltpu.roll(below, (LOW_AT - AT_X[k]) % Z, 1)
-            high = pltpu.roll(above, (HIGH_AT - AT_X[k]) % Z, 1)
-            out = jnp.where(place < LOW_AT, low, ends[k, q])
-            cells[k, q] = jnp.where((place >= HIGH_AT) & (place < HIGH_AT + HALO), high, out)
+    below, above = (halo(place_z[0], far, chip, (slice(None),), lower) for lower in (True, False))
+
+    def cells(k):
+        low = pltpu.roll(below, (LOW_AT - AT_X[k]) % Z, 2)
+        high = pltpu.roll(above, (HIGH_AT - AT_X[k]) % Z, 2)
+        out = jnp.where(place < LOW_AT, low, ends[k])
+        return jnp.where((place >= HIGH_AT) & (place < HIGH_AT + HALO), high, out)
 
     def smoothed(planes, first=0, count=ROWS):
         slot[0] += 1
@@ -285,13 +310,14 @@
             for by in (0, 1, -1)
         ]
 
-    cond, start, rest, flag = (cells[k] for k in range(4))
+    cond, start = cells(0), cells(1)
     cs, xs = spread(cond), spread(start)
     tc, tx, tcx = (
         smoothed(smooth_z(*values)) for values in (cs, xs, [c * x for c, x in zip(cs, xs)])
     )
     for n, values in enumerate(cs):
         slopes[n] = values * (1.0 / SCALE)
+    rest, flag = cells(2), cells(3)
     near = 16.0 * cond + tc
     diag = (1.0 + 6.0 * flag + near) * (1.0 / SCALE)
     there = jnp.where(cond > 0.0, 1.0, 0.0)
@@ -516,7 +542,7 @@
         edges,
         [SMEM] + [VMEM] * 5,
         [(ITERS + 1, PER_GROUP, Y, Z), (lax.axis_size(first), 1, Z)],
-        [(4, *packed), (3, PER_GROUP, ROWS + 16, Z), (3, PER_GROUP + 2, ROWS, Z), (Z, Z)],
+        [(3, PER_GROUP, ROWS + 16, Z), (3, PER_GROUP + 2, ROWS, Z), (Z, Z)],
         flops=5000000,
     )(place_z, ends, far, chip, theta, sums)
     parts = exchange(dots, first)

time: 65.4 us -> 65.4 us (level)
  transfers between devices with their start and end apart: 3 -> 3, of which waited for: 0 -> 0; matrix products, arithmetic and copies ran while one was open for 0% -> 0% of each run, Pallas kernels for 3% -> 2%
where the time goes in v10:
time: 65.4 us; the launch traced here: 65.1 us
  blocking collectives  50.8 us (78%)
  starting transfers between devices  7.91 us (12%)
  Pallas kernels  5.7 us (9%)
  between operations  0.7 us (1%)
    all_to_all x2, blocking collectives, exchange(): return lax.all_to_all(copies, axes, split_axis=0, concat_axis=0, tiled=True)  33.6 us
    all_gather x3, blocking collectives, trade(): lax.all_gather(near, axes[1], axis=0)  17.2 us
    ppermute x3, starting transfers between devices, trade(): lax.ppermute(far, axes, others)  7.91 us
    pallas_call x1, Pallas kernels, body(): call(interior, [VMEM] * 2, [(ITERS + 1, *brick), (len(PAIRS), 8, Z), (4,...  1.6 us
    pallas_call x1, Pallas kernels, body(): call(edges, [SMEM] + [VMEM] * 5, [(ITERS + 1, PER_GROUP, Y, Z), (lax.axis...  1.36 us
  transfers between devices with their start and end apart: 3, of which 0 were waited for; matrix products, arithmetic and copies ran while one was open for 0% of the time, Pallas kernels for 2%

profile of v10, /device:TPU:1, one launch (start us, length us, event | category | flops | bytes accessed | tf_op | source)
XLA Modules:
  0.0 65.1 jit_solution(11682002954316554612)
XLA Ops:
  0.6 1.1 %shard_map.68 = (f32[4,8,16,128]{3,2,1,0:T(8,128)S(1)}, f32[17,16,128]{2,1,0:T(8,128)S(1)}, f32[17,16,128]{2,1,0:T(8,128)S(1)}, f32[4,8,128]{2,1,0:T(8,128)S(1)}) custom-call(s32[1]{0:T(128)} %bitcast.1.place_x, f32[8,16,128]{2,1,0:T(8,128)} %opening_at.1, f32[8,16,128]{2,1,0:T(8,128)} %source_at.1, s32[8,16,128]{2,1,0:T(8,128)} %category_at.1, ...), custom_call_target="tpu_custom_call" | custom-call | flops 100000 | bytes 1000000 | tf_op jit(solution)/shard_map/pallas_call | solution.py:508
  1.7 0.7 %collective-permute-start = (f32[17,16,128]{2,1,0:T(8,128)S(1)}, f32[17,16,128]{2,1,0:T(8,128)S(1)}, u32[]{:S(2)}, u32[]{:S(2)}) collective-permute-start(f32[17,16,128]{2,1,0:T(8,128)S(1)} %get-tuple-element.17), channel_id=1, source_target_pairs={{128,256},{256,128},{129,257},{257,129},{130,258},{258,130},{131,2... | collective-permute-start | bytes 417800 | tf_op jit(solution)/shard_map/ppermute | solution.py:497
  2.4 7.6 %all-gather = f32[34,16,128]{2,1,0:T(8,128)S(1)} all-gather(f32[17,16,128]{2,1,0:T(8,128)S(1)} %get-tuple-element.18), channel_id=2, replica_groups=mesh['gx_0'=2,'gx_1'=2,'gy_0'=4,'gy_1'=2,'gz_0'=8,'gz_1'=2] {'gx_1'}, dimensions={0}, use_global_device_ids=true | all-gather | bytes 417792 | tf_op jit(solution)/shard_map/all_gather | solution.py:497
  10.0 0.0 collective-permute-done.far_x
  10.0 0.1 shard_map.69
  10.1 0.7 %collective-permute-start.1 = (f32[288,128]{1,0:T(8,128)S(1)}, f32[288,128]{1,0:T(8,128)S(1)}, u32[]{:S(2)}, u32[]{:S(2)}) collective-permute-start(f32[288,128]{1,0:T(8,128)S(1)} %get-tuple-element.19), channel_id=1, source_target_pairs={{16,32},{32,16},{48,64},{64,48},{80,96},{96,80},{17,33},{33,17},{4... | collective-permute-start | bytes 442376 | tf_op jit(solution)/shard_map/ppermute | solution.py:497
  10.7 7.7 %all-gather.1 = f32[576,128]{1,0:T(8,128)S(1)} all-gather(f32[288,128]{1,0:T(8,128)S(1)} %get-tuple-element.20), channel_id=3, replica_groups=mesh['gx_0'=2,'gx_1'=2,'gy_0'=4,'gy_1'=2,'gz_0'=8,'gz_1'=2] {'gy_1'}, dimensions={0}, use_global_device_ids=true | all-gather | bytes 442368 | tf_op jit(solution)/shard_map/all_gather | solution.py:497
  18.4 0.0 collective-permute-done.1.far_y
  18.4 0.4 shard_map.70
  18.8 6.6 %collective-permute-start.2 = (f32[5,32,128]{2,1,0:T(8,128)S(1)}, f32[5,32,128]{2,1,0:T(8,128)S(1)}, u32[]{:S(2)}, u32[]{:S(2)}) collective-permute-start(f32[5,32,128]{2,1,0:T(8,128)S(1)} %get-tuple-element.24), channel_id=1, source_target_pairs={{1,2},{2,1},{3,4},{4,3},{5,6},{6,5},{7,8},{8,7},{9,10},{10,9},{11,... | collective-permute-start | bytes 245768 | tf_op jit(solution)/shard_map/ppermute | solution.py:497
  25.4 1.6 %shard_map.71 = (f32[5,8,16,128]{3,2,1,0:T(8,128)S(1)}, f32[14,8,128]{2,1,0:T(8,128)S(1)}, f32[4,5,32,128]{3,2,1,0:T(8,128)S(1)}) custom-call(f32[4,18,32,128]{3,2,1,0:T(8,128)S(1)} %get-tuple-element.21.wide, f32[4,8,128]{2,1,0:T(8,128)S(1)} %get-tuple-element.22.theta), custom_call_target="tpu_custom_call" | custom-call | flops 20000000 | bytes 1000000 | tf_op jit(solution)/shard_map/pallas_call | solution.py:532
  27.0 1.9 %all-gather.2 = f32[10,32,128]{2,1,0:T(8,128)S(1)} all-gather(f32[5,32,128]{2,1,0:T(8,128)S(1)} %get-tuple-element.25), channel_id=4, replica_groups=mesh['gx_0'=2,'gx_1'=2,'gy_0'=4,'gy_1'=2,'gz_0'=8,'gz_1'=2] {'gz_1'}, dimensions={0}, use_global_device_ids=true | all-gather | bytes 245760 | tf_op jit(solution)/shard_map/all_gather | solution.py:497
  28.9 0.0 collective-permute-done.2.far
  28.9 1.4 %shard_map.72 = (f32[5,5,16,128]{3,2,1,0:T(8,128)S(1)}, f32[16,1,128]{2,1,0:T(1,128)S(1)}) custom-call(s32[1]{0:T(128)} %bitcast.place_z, f32[4,5,32,128]{3,2,1,0:T(8,128)S(1)} %get-tuple-element.23.ends, f32[5,32,128]{2,1,0:T(8,128)S(1)} %collective-permute-done.2.far, f32[2,5,32,128]{3,2,1,0:T(8,128)S(1)} %bitcast.9, ...), custom_call_target="tpu_custom_call" | custom-call | flops 5000000 | bytes 1000000 | tf_op jit(solution)/shard_map/pallas_call | solution.py:541
  30.3 13.6 %all_to_all.10.parts = f32[16,1,128]{2,1,0:T(1,128)S(1)} all-to-all(f32[16,1,128]{2,1,0:T(1,128)S(1)} %get-tuple-element.27), channel_id=1, replica_groups=mesh['gx_0'=2,'gx_1'=2,'gy_0'=4,'gy_1'=2,'gz_0'=8,'gz_1'=2] {'gy_0','gy_..., dimensions={0} | all-to-all | bytes 16384 | tf_op jit(solution)/shard_map/all_to_all | solution.py:501
  43.9 20.0 %all_to_all.11.parts = f32[32,1,128]{2,1,0:T(1,128)S(1)} all-to-all(f32[32,1,128]{2,1,0:T(1,128)S(1)} %shard_map.73), channel_id=1, replica_groups=mesh['gx_0'=2,'gx_1'=2,'gy_0'=4,'gy_1'=2,'gz_0'=8,'gz_1'=2] {'gx_0','gx_..., dimensions={0} | all-to-all | bytes 32768 | tf_op jit(solution)/shard_map/all_to_all | solution.py:501
  63.9 1.2 %shard_map.74 = (f32[8,16,128]{2,1,0:T(8,128)}, f32[8,16,128]{2,1,0:T(8,128)}) custom-call(f32[32,1,128]{2,1,0:T(1,128)S(1)} %all_to_all.11.parts, f32[5,8,16,128]{3,2,1,0:T(8,128)S(1)} %get-tuple-element.28.basis, f32[5,5,16,128]{3,2,1,0:T(8,128)S(1)} %get-tuple-element.29.end_basis, f32[4,8,16,128]{3,2,1,0:T(8,128)S(1)} %get-tuple-element.16.fields, ...), custom_call_target="tpu_custom_call" | custom-call | flops 100000 | bytes 1000000 | tf_op jit(solution)/shard_map/pallas_call | solution.py:551
  (1 shorter events, 0.0 us)
Async XLA Ops:
  1.7 8.3 %collective-permute-start = (f32[17,16,128]{2,1,0:T(8,128)S(1)}, f32[17,16,128]{2,1,0:T(8,128)S(1)}, u32[]{:S(2)}, u32[]{:S(2)}) collective-permute-start(f32[17,16,128]{2,1,0:T(8,128)S(1)} %get-tuple-element.17), channel_id=1, source_target_pairs={{128,256},{256,128},{129,257},{257,129},{130,258},{258,130},{131,2... | collective-permute-start | bytes 417800 | tf_op jit(solution)/shard_map/ppermute | solution.py:497
  10.1 8.4 %collective-permute-start.1 = (f32[288,128]{1,0:T(8,128)S(1)}, f32[288,128]{1,0:T(8,128)S(1)}, u32[]{:S(2)}, u32[]{:S(2)}) collective-permute-start(f32[288,128]{1,0:T(8,128)S(1)} %get-tuple-element.19), channel_id=1, source_target_pairs={{16,32},{32,16},{48,64},{64,48},{80,96},{96,80},{17,33},{33,17},{4... | collective-permute-start | bytes 442376 | tf_op jit(solution)/shard_map/ppermute | solution.py:497
  18.8 10.1 %collective-permute-start.2 = (f32[5,32,128]{2,1,0:T(8,128)S(1)}, f32[5,32,128]{2,1,0:T(8,128)S(1)}, u32[]{:S(2)}, u32[]{:S(2)}) collective-permute-start(f32[5,32,128]{2,1,0:T(8,128)S(1)} %get-tuple-element.24), channel_id=1, source_target_pairs={{1,2},{2,1},{3,4},{4,3},{5,6},{6,5},{7,8},{8,7},{9,10},{10,9},{11,... | collective-permute-start | bytes 245768 | tf_op jit(solution)/shard_map/ppermute | solution.py:497

commit v11 on v10

--- a/solution.py
+++ b/solution.py
@@ -148,7 +148,7 @@
     low = 2.0 + 8.0 * least + 8.0 * mean
     middle, half = 0.5 * (top + low), 0.5 * (top - low)
     return [
-        (middle + half * c) * (1.0 / SCALE) for c in (0.9238795, -0.9238795, 0.3826834, -0.3826834)
+        (middle + half * c) * (1.0 / SCALE) for c in (-0.9238795, 0.9238795, -0.3826834, 0.3826834)
     ]
 
 

time: 65.4 us -> 65.4 us (level)
  no operation moved by 1% of the time
where the time goes in v11:
time: 65.4 us; the launch traced here: 65.1 us
  blocking collectives  50.8 us (78%)
  starting transfers between devices  7.91 us (12%)
  Pallas kernels  5.7 us (9%)
  between operations  0.7 us (1%)
    all_to_all x2, blocking collectives, exchange(): return lax.all_to_all(copies, axes, split_axis=0, concat_axis=0, tiled=True)  33.6 us
    all_gather x3, blocking collectives, trade(): lax.all_gather(near, axes[1], axis=0)  17.2 us
    ppermute x3, starting transfers between devices, trade(): lax.ppermute(far, axes, others)  7.91 us
    pallas_call x1, Pallas kernels, body(): call(interior, [VMEM] * 2, [(ITERS + 1, *brick), (len(PAIRS), 8, Z), (4,...  1.6 us
    pallas_call x1, Pallas kernels, body(): call(edges, [SMEM] + [VMEM] * 5, [(ITERS + 1, PER_GROUP, Y, Z), (lax.axis...  1.36 us
  transfers between devices with their start and end apart: 3, of which 0 were waited for; matrix products, arithmetic and copies ran while one was open for 0% of the time, Pallas kernels for 2%

profile of v11, /device:TPU:1, one launch (start us, length us, event | category | flops | bytes accessed | tf_op | source)
XLA Modules:
  0.0 65.1 jit_solution(18176249940697758482)
XLA Ops:
  0.6 1.1 %shard_map.68 = (f32[4,8,16,128]{3,2,1,0:T(8,128)S(1)}, f32[17,16,128]{2,1,0:T(8,128)S(1)}, f32[17,16,128]{2,1,0:T(8,128)S(1)}, f32[4,8,128]{2,1,0:T(8,128)S(1)}) custom-call(s32[1]{0:T(128)} %bitcast.1.place_x, f32[8,16,128]{2,1,0:T(8,128)} %opening_at.1, f32[8,16,128]{2,1,0:T(8,128)} %source_at.1, s32[8,16,128]{2,1,0:T(8,128)} %category_at.1, ...), custom_call_target="tpu_custom_call" | custom-call | flops 100000 | bytes 1000000 | tf_op jit(solution)/shard_map/pallas_call | solution.py:508
  1.7 0.7 %collective-permute-start = (f32[17,16,128]{2,1,0:T(8,128)S(1)}, f32[17,16,128]{2,1,0:T(8,128)S(1)}, u32[]{:S(2)}, u32[]{:S(2)}) collective-permute-start(f32[17,16,128]{2,1,0:T(8,128)S(1)} %get-tuple-element.17), channel_id=1, source_target_pairs={{128,256},{256,128},{129,257},{257,129},{130,258},{258,130},{131,2... | collective-permute-start | bytes 417800 | tf_op jit(solution)/shard_map/ppermute | solution.py:497
  2.4 7.6 %all-gather = f32[34,16,128]{2,1,0:T(8,128)S(1)} all-gather(f32[17,16,128]{2,1,0:T(8,128)S(1)} %get-tuple-element.18), channel_id=2, replica_groups=mesh['gx_0'=2,'gx_1'=2,'gy_0'=4,'gy_1'=2,'gz_0'=8,'gz_1'=2] {'gx_1'}, dimensions={0}, use_global_device_ids=true | all-gather | bytes 417792 | tf_op jit(solution)/shard_map/all_gather | solution.py:497
  10.0 0.0 collective-permute-done.far_x
  10.0 0.1 shard_map.69
  10.1 0.7 %collective-permute-start.1 = (f32[288,128]{1,0:T(8,128)S(1)}, f32[288,128]{1,0:T(8,128)S(1)}, u32[]{:S(2)}, u32[]{:S(2)}) collective-permute-start(f32[288,128]{1,0:T(8,128)S(1)} %get-tuple-element.19), channel_id=1, source_target_pairs={{16,32},{32,16},{48,64},{64,48},{80,96},{96,80},{17,33},{33,17},{4... | collective-permute-start | bytes 442376 | tf_op jit(solution)/shard_map/ppermute | solution.py:497
  10.7 7.7 %all-gather.1 = f32[576,128]{1,0:T(8,128)S(1)} all-gather(f32[288,128]{1,0:T(8,128)S(1)} %get-tuple-element.20), channel_id=3, replica_groups=mesh['gx_0'=2,'gx_1'=2,'gy_0'=4,'gy_1'=2,'gz_0'=8,'gz_1'=2] {'gy_1'}, dimensions={0}, use_global_device_ids=true | all-gather | bytes 442368 | tf_op jit(solution)/shard_map/all_gather | solution.py:497
  18.4 0.0 collective-permute-done.1.far_y
  18.4 0.4 shard_map.70
  18.8 6.6 %collective-permute-start.2 = (f32[5,32,128]{2,1,0:T(8,128)S(1)}, f32[5,32,128]{2,1,0:T(8,128)S(1)}, u32[]{:S(2)}, u32[]{:S(2)}) collective-permute-start(f32[5,32,128]{2,1,0:T(8,128)S(1)} %get-tuple-element.24), channel_id=1, source_target_pairs={{1,2},{2,1},{3,4},{4,3},{5,6},{6,5},{7,8},{8,7},{9,10},{10,9},{11,... | collective-permute-start | bytes 245768 | tf_op jit(solution)/shard_map/ppermute | solution.py:497
  25.4 1.6 %shard_map.71 = (f32[5,8,16,128]{3,2,1,0:T(8,128)S(1)}, f32[14,8,128]{2,1,0:T(8,128)S(1)}, f32[4,5,32,128]{3,2,1,0:T(8,128)S(1)}) custom-call(f32[4,18,32,128]{3,2,1,0:T(8,128)S(1)} %get-tuple-element.21.wide, f32[4,8,128]{2,1,0:T(8,128)S(1)} %get-tuple-element.22.theta), custom_call_target="tpu_custom_call" | custom-call | flops 20000000 | bytes 1000000 | tf_op jit(solution)/shard_map/pallas_call | solution.py:532
  27.0 1.9 %all-gather.2 = f32[10,32,128]{2,1,0:T(8,128)S(1)} all-gather(f32[5,32,128]{2,1,0:T(8,128)S(1)} %get-tuple-element.25), channel_id=4, replica_groups=mesh['gx_0'=2,'gx_1'=2,'gy_0'=4,'gy_1'=2,'gz_0'=8,'gz_1'=2] {'gz_1'}, dimensions={0}, use_global_device_ids=true | all-gather | bytes 245760 | tf_op jit(solution)/shard_map/all_gather | solution.py:497
  28.9 0.0 collective-permute-done.2.far
  28.9 1.4 %shard_map.72 = (f32[5,5,16,128]{3,2,1,0:T(8,128)S(1)}, f32[16,1,128]{2,1,0:T(1,128)S(1)}) custom-call(s32[1]{0:T(128)} %bitcast.place_z, f32[4,5,32,128]{3,2,1,0:T(8,128)S(1)} %get-tuple-element.23.ends, f32[5,32,128]{2,1,0:T(8,128)S(1)} %collective-permute-done.2.far, f32[2,5,32,128]{3,2,1,0:T(8,128)S(1)} %bitcast.9, ...), custom_call_target="tpu_custom_call" | custom-call | flops 5000000 | bytes 1000000 | tf_op jit(solution)/shard_map/pallas_call | solution.py:541
  30.3 13.6 %all_to_all.10.parts = f32[16,1,128]{2,1,0:T(1,128)S(1)} all-to-all(f32[16,1,128]{2,1,0:T(1,128)S(1)} %get-tuple-element.27), channel_id=1, replica_groups=mesh['gx_0'=2,'gx_1'=2,'gy_0'=4,'gy_1'=2,'gz_0'=8,'gz_1'=2] {'gy_0','gy_..., dimensions={0} | all-to-all | bytes 16384 | tf_op jit(solution)/shard_map/all_to_all | solution.py:501
  43.9 20.0 %all_to_all.11.parts = f32[32,1,128]{2,1,0:T(1,128)S(1)} all-to-all(f32[32,1,128]{2,1,0:T(1,128)S(1)} %shard_map.73), channel_id=1, replica_groups=mesh['gx_0'=2,'gx_1'=2,'gy_0'=4,'gy_1'=2,'gz_0'=8,'gz_1'=2] {'gx_0','gx_..., dimensions={0} | all-to-all | bytes 32768 | tf_op jit(solution)/shard_map/all_to_all | solution.py:501
  63.9 1.2 %shard_map.74 = (f32[8,16,128]{2,1,0:T(8,128)}, f32[8,16,128]{2,1,0:T(8,128)}) custom-call(f32[32,1,128]{2,1,0:T(1,128)S(1)} %all_to_all.11.parts, f32[5,8,16,128]{3,2,1,0:T(8,128)S(1)} %get-tuple-element.28.basis, f32[5,5,16,128]{3,2,1,0:T(8,128)S(1)} %get-tuple-element.29.end_basis, f32[4,8,16,128]{3,2,1,0:T(8,128)S(1)} %get-tuple-element.16.fields, ...), custom_call_target="tpu_custom_call" | custom-call | flops 100000 | bytes 1000000 | tf_op jit(solution)/shard_map/pallas_call | solution.py:551
  (1 shorter events, 0.0 us)
Async XLA Ops:
  1.7 8.3 %collective-permute-start = (f32[17,16,128]{2,1,0:T(8,128)S(1)}, f32[17,16,128]{2,1,0:T(8,128)S(1)}, u32[]{:S(2)}, u32[]{:S(2)}) collective-permute-start(f32[17,16,128]{2,1,0:T(8,128)S(1)} %get-tuple-element.17), channel_id=1, source_target_pairs={{128,256},{256,128},{129,257},{257,129},{130,258},{258,130},{131,2... | collective-permute-start | bytes 417800 | tf_op jit(solution)/shard_map/ppermute | solution.py:497
  10.1 8.4 %collective-permute-start.1 = (f32[288,128]{1,0:T(8,128)S(1)}, f32[288,128]{1,0:T(8,128)S(1)}, u32[]{:S(2)}, u32[]{:S(2)}) collective-permute-start(f32[288,128]{1,0:T(8,128)S(1)} %get-tuple-element.19), channel_id=1, source_target_pairs={{16,32},{32,16},{48,64},{64,48},{80,96},{96,80},{17,33},{33,17},{4... | collective-permute-start | bytes 442376 | tf_op jit(solution)/shard_map/ppermute | solution.py:497
  18.8 10.1 %collective-permute-start.2 = (f32[5,32,128]{2,1,0:T(8,128)S(1)}, f32[5,32,128]{2,1,0:T(8,128)S(1)}, u32[]{:S(2)}, u32[]{:S(2)}) collective-permute-start(f32[5,32,128]{2,1,0:T(8,128)S(1)} %get-tuple-element.24), channel_id=1, source_target_pairs={{1,2},{2,1},{3,4},{4,3},{5,6},{6,5},{7,8},{8,7},{9,10},{10,9},{11,... | collective-permute-start | bytes 245768 | tf_op jit(solution)/shard_map/ppermute | solution.py:497

commit v12 on v11

--- a/solution.py
+++ b/solution.py
@@ -370,7 +370,7 @@
 
 
 def row_sum(parts):
-    rows = [(parts[n], None) for n in range(parts.shape[0])]
+    rows = [(parts[n, 0:1], None) for n in range(parts.shape[0])]
     while len(rows) > 1:
         pairs, rows = zip(rows[::2], rows[1::2]), []
         for (a, ea), (b, eb) in pairs:
@@ -381,10 +381,9 @@
 
 def relay(parts, copies):
     total, rest = row_sum(parts)
-    lane = lax.broadcasted_iota(jnp.int32, total.shape, 1)
-    total = jnp.where(lane < 16, total, rest)
     for n in range(copies.shape[0]):
-        copies[n] = total
+        copies[n, 0:1] = total
+        copies[n, 1:2] = rest
 
 
 def quick(a, b):
@@ -456,7 +455,8 @@
 
 def finish(parts, basis, end_basis, fields, theta, closing, mismatch):
     total, rest = row_sum(parts)
-    rest = rest + pltpu.roll(total, Z - 16, 1)
+    for n in range(parts.shape[0]):
+        rest = rest + parts[n, 1:2]
     gram = {}
     for n, (i, j) in enumerate(PAIRS):
         gram[i, j] = gram[j, i] = quick(
@@ -546,7 +546,7 @@
         flops=5000000,
     )(place_z, ends, far, chip, theta, sums)
     parts = exchange(dots, first)
-    (copies,) = call(relay, [VMEM], [(lax.axis_size(second), 1, Z)])(parts)
+    (copies,) = call(relay, [VMEM], [(lax.axis_size(second), 2, Z)])(parts)
     parts = exchange(copies, second)
     closing, mismatch = call(finish, [VMEM] * 5, [brick, brick])(
         parts, basis, end_basis, fields, theta

time: 65.4 us -> 65.5 us (level)
  no operation moved by 1% of the time
where the time goes in v12:
time: 65.5 us; the launch traced here: 65.2 us
  blocking collectives  50.9 us (78%)
  starting transfers between devices  7.91 us (12%)
  Pallas kernels  5.72 us (9%)
  between operations  0.69 us (1%)
    all_to_all x2, blocking collectives, exchange(): return lax.all_to_all(copies, axes, split_axis=0, concat_axis=0, tiled=True)  33.7 us
    all_gather x3, blocking collectives, trade(): lax.all_gather(near, axes[1], axis=0)  17.2 us
    ppermute x3, starting transfers between devices, trade(): lax.ppermute(far, axes, others)  7.91 us
    pallas_call x1, Pallas kernels, body(): call(interior, [VMEM] * 2, [(ITERS + 1, *brick), (len(PAIRS), 8, Z), (4,...  1.6 us
    pallas_call x1, Pallas kernels, body(): call(edges, [SMEM] + [VMEM] * 5, [(ITERS + 1, PER_GROUP, Y, Z), (lax.axis...  1.36 us
  transfers between devices with their start and end apart: 3, of which 0 were waited for; matrix products, arithmetic and copies ran while one was open for 0% of the time, Pallas kernels for 2%

profile of v12, /device:TPU:1, one launch (start us, length us, event | category | flops | bytes accessed | tf_op | source)
XLA Modules:
  0.0 65.2 jit_solution(11082121507665458597)
XLA Ops:
  0.6 1.1 %shard_map.68 = (f32[4,8,16,128]{3,2,1,0:T(8,128)S(1)}, f32[17,16,128]{2,1,0:T(8,128)S(1)}, f32[17,16,128]{2,1,0:T(8,128)S(1)}, f32[4,8,128]{2,1,0:T(8,128)S(1)}) custom-call(s32[1]{0:T(128)} %bitcast.1.place_x, f32[8,16,128]{2,1,0:T(8,128)} %opening_at.1, f32[8,16,128]{2,1,0:T(8,128)} %source_at.1, s32[8,16,128]{2,1,0:T(8,128)} %category_at.1, ...), custom_call_target="tpu_custom_call" | custom-call | flops 100000 | bytes 1000000 | tf_op jit(solution)/shard_map/pallas_call | solution.py:508
  1.7 0.7 %collective-permute-start = (f32[17,16,128]{2,1,0:T(8,128)S(1)}, f32[17,16,128]{2,1,0:T(8,128)S(1)}, u32[]{:S(2)}, u32[]{:S(2)}) collective-permute-start(f32[17,16,128]{2,1,0:T(8,128)S(1)} %get-tuple-element.17), channel_id=1, source_target_pairs={{128,256},{256,128},{129,257},{257,129},{130,258},{258,130},{131,2... | collective-permute-start | bytes 417800 | tf_op jit(solution)/shard_map/ppermute | solution.py:497
  2.4 7.6 %all-gather = f32[34,16,128]{2,1,0:T(8,128)S(1)} all-gather(f32[17,16,128]{2,1,0:T(8,128)S(1)} %get-tuple-element.18), channel_id=2, replica_groups=mesh['gx_0'=2,'gx_1'=2,'gy_0'=4,'gy_1'=2,'gz_0'=8,'gz_1'=2] {'gx_1'}, dimensions={0}, use_global_device_ids=true | all-gather | bytes 417792 | tf_op jit(solution)/shard_map/all_gather | solution.py:497
  10.0 0.0 collective-permute-done.far_x
  10.0 0.1 shard_map.69
  10.1 0.7 %collective-permute-start.1 = (f32[288,128]{1,0:T(8,128)S(1)}, f32[288,128]{1,0:T(8,128)S(1)}, u32[]{:S(2)}, u32[]{:S(2)}) collective-permute-start(f32[288,128]{1,0:T(8,128)S(1)} %get-tuple-element.19), channel_id=1, source_target_pairs={{16,32},{32,16},{48,64},{64,48},{80,96},{96,80},{17,33},{33,17},{4... | collective-permute-start | bytes 442376 | tf_op jit(solution)/shard_map/ppermute | solution.py:497
  10.7 7.7 %all-gather.1 = f32[576,128]{1,0:T(8,128)S(1)} all-gather(f32[288,128]{1,0:T(8,128)S(1)} %get-tuple-element.20), channel_id=3, replica_groups=mesh['gx_0'=2,'gx_1'=2,'gy_0'=4,'gy_1'=2,'gz_0'=8,'gz_1'=2] {'gy_1'}, dimensions={0}, use_global_device_ids=true | all-gather | bytes 442368 | tf_op jit(solution)/shard_map/all_gather | solution.py:497
  18.4 0.0 collective-permute-done.1.far_y
  18.4 0.4 shard_map.70
  18.8 6.6 %collective-permute-start.2 = (f32[5,32,128]{2,1,0:T(8,128)S(1)}, f32[5,32,128]{2,1,0:T(8,128)S(1)}, u32[]{:S(2)}, u32[]{:S(2)}) collective-permute-start(f32[5,32,128]{2,1,0:T(8,128)S(1)} %get-tuple-element.24), channel_id=1, source_target_pairs={{1,2},{2,1},{3,4},{4,3},{5,6},{6,5},{7,8},{8,7},{9,10},{10,9},{11,... | collective-permute-start | bytes 245768 | tf_op jit(solution)/shard_map/ppermute | solution.py:497
  25.4 1.6 %shard_map.71 = (f32[5,8,16,128]{3,2,1,0:T(8,128)S(1)}, f32[14,8,128]{2,1,0:T(8,128)S(1)}, f32[4,5,32,128]{3,2,1,0:T(8,128)S(1)}) custom-call(f32[4,18,32,128]{3,2,1,0:T(8,128)S(1)} %get-tuple-element.21.wide, f32[4,8,128]{2,1,0:T(8,128)S(1)} %get-tuple-element.22.theta), custom_call_target="tpu_custom_call" | custom-call | flops 20000000 | bytes 1000000 | tf_op jit(solution)/shard_map/pallas_call | solution.py:532
  27.0 1.9 %all-gather.2 = f32[10,32,128]{2,1,0:T(8,128)S(1)} all-gather(f32[5,32,128]{2,1,0:T(8,128)S(1)} %get-tuple-element.25), channel_id=4, replica_groups=mesh['gx_0'=2,'gx_1'=2,'gy_0'=4,'gy_1'=2,'gz_0'=8,'gz_1'=2] {'gz_1'}, dimensions={0}, use_global_device_ids=true | all-gather | bytes 245760 | tf_op jit(solution)/shard_map/all_gather | solution.py:497
  28.9 0.0 collective-permute-done.2.far
  28.9 1.4 %shard_map.72 = (f32[5,5,16,128]{3,2,1,0:T(8,128)S(1)}, f32[16,1,128]{2,1,0:T(1,128)S(1)}) custom-call(s32[1]{0:T(128)} %bitcast.place_z, f32[4,5,32,128]{3,2,1,0:T(8,128)S(1)} %get-tuple-element.23.ends, f32[5,32,128]{2,1,0:T(8,128)S(1)} %collective-permute-done.2.far, f32[2,5,32,128]{3,2,1,0:T(8,128)S(1)} %bitcast.9, ...), custom_call_target="tpu_custom_call" | custom-call | flops 5000000 | bytes 1000000 | tf_op jit(solution)/shard_map/pallas_call | solution.py:541
  30.3 13.6 %all_to_all.10.parts = f32[16,1,128]{2,1,0:T(1,128)S(1)} all-to-all(f32[16,1,128]{2,1,0:T(1,128)S(1)} %get-tuple-element.27), channel_id=1, replica_groups=mesh['gx_0'=2,'gx_1'=2,'gy_0'=4,'gy_1'=2,'gz_0'=8,'gz_1'=2] {'gy_0','gy_..., dimensions={0} | all-to-all | bytes 16384 | tf_op jit(solution)/shard_map/all_to_all | solution.py:501
  43.9 20.1 %all_to_all.11.parts = f32[32,2,128]{2,1,0:T(2,128)S(1)} all-to-all(f32[32,2,128]{2,1,0:T(2,128)S(1)} %shard_map.73), channel_id=1, replica_groups=mesh['gx_0'=2,'gx_1'=2,'gy_0'=4,'gy_1'=2,'gz_0'=8,'gz_1'=2] {'gx_0','gx_..., dimensions={0} | all-to-all | bytes 65536 | tf_op jit(solution)/shard_map/all_to_all | solution.py:501
  64.0 1.2 %shard_map.74 = (f32[8,16,128]{2,1,0:T(8,128)}, f32[8,16,128]{2,1,0:T(8,128)}) custom-call(f32[32,2,128]{2,1,0:T(2,128)S(1)} %all_to_all.11.parts, f32[5,8,16,128]{3,2,1,0:T(8,128)S(1)} %get-tuple-element.28.basis, f32[5,5,16,128]{3,2,1,0:T(8,128)S(1)} %get-tuple-element.29.end_basis, f32[4,8,16,128]{3,2,1,0:T(8,128)S(1)} %get-tuple-element.16.fields, ...), custom_call_target="tpu_custom_call" | custom-call | flops 100000 | bytes 1000000 | tf_op jit(solution)/shard_map/pallas_call | solution.py:551
  (1 shorter events, 0.0 us)
Async XLA Ops:
  1.7 8.3 %collective-permute-start = (f32[17,16,128]{2,1,0:T(8,128)S(1)}, f32[17,16,128]{2,1,0:T(8,128)S(1)}, u32[]{:S(2)}, u32[]{:S(2)}) collective-permute-start(f32[17,16,128]{2,1,0:T(8,128)S(1)} %get-tuple-element.17), channel_id=1, source_target_pairs={{128,256},{256,128},{129,257},{257,129},{130,258},{258,130},{131,2... | collective-permute-start | bytes 417800 | tf_op jit(solution)/shard_map/ppermute | solution.py:497
  10.1 8.4 %collective-permute-start.1 = (f32[288,128]{1,0:T(8,128)S(1)}, f32[288,128]{1,0:T(8,128)S(1)}, u32[]{:S(2)}, u32[]{:S(2)}) collective-permute-start(f32[288,128]{1,0:T(8,128)S(1)} %get-tuple-element.19), channel_id=1, source_target_pairs={{16,32},{32,16},{48,64},{64,48},{80,96},{96,80},{17,33},{33,17},{4... | collective-permute-start | bytes 442376 | tf_op jit(solution)/shard_map/ppermute | solution.py:497
  18.8 10.1 %collective-permute-start.2 = (f32[5,32,128]{2,1,0:T(8,128)S(1)}, f32[5,32,128]{2,1,0:T(8,128)S(1)}, u32[]{:S(2)}, u32[]{:S(2)}) collective-permute-start(f32[5,32,128]{2,1,0:T(8,128)S(1)} %get-tuple-element.24), channel_id=1, source_target_pairs={{1,2},{2,1},{3,4},{4,3},{5,6},{6,5},{7,8},{8,7},{9,10},{10,9},{11,... | collective-permute-start | bytes 245768 | tf_op jit(solution)/shard_map/ppermute | solution.py:497
